TPU v7x, 32 devices: a whole 2x2x4 slice. The times are simulated.
32 devices in a mesh: dp: 8 (over z, x), mp: 4 (over y, core).
Axes of the slice: x: 2, y: 2, z: 4, core: 2. Of those that a mesh axis runs over, the one named last changes fastest.
Arguments:
- values: bfloat16 [8192, 96, 128], P('dp', 'mp'), may hold values from -0.29882812 to 0.29882812
- block_ids: int32 [8192, 96], P('dp', 'mp'), may hold values from 0 to 2047
- labels: int32 [8192], P('dp'), may hold values from 0 to 1
- weights: float32 [1048576], P(('dp', 'mp')), may hold values from -2.4 to 2.4
- history: float32 [2, 8, 1048576], P(None, None, ('dp', 'mp')), as said below
- steps: float32 [1], replicated, may hold values from 0.3 to 1
Outputs:
- final_weights: float32 [1048576], P(('dp', 'mp'))
- last_gradient: float32 [1048576], P(('dp', 'mp'))
Inputs may be any that keep to these rules, and one draw needn't show every extreme that they name: `block_ids`: block ids are block numbers within the group of 2048 blocks of their mp shard. `history`: for every stored pair the inner product of its step and its gradient change is positive.
All inputs are finite; a program needn't handle non-finite values.
Results may differ from a plain program's by a relative error of at most 0.00039.
Values may be sent and summed in bfloat16 or wider, within the bound.
No kernel may reach another device: no remote copies, remote signals or barrier semaphores. Data moves between devices by JAX's collectives and lax.ppermute only.
A program may use at most 128 MiB of HBM per device.

v0:
```python
import jax
import jax.numpy as jnp
from jax import lax
from jax.sharding import PartitionSpec as P

ridge = 0.2


def coefficient_direction(s_hist, y_hist, grad):
    count = s_hist.shape[0]
    basis = jnp.concatenate([s_hist, y_hist, grad[None]], axis=0)
    local_gram = jnp.dot(
        basis, basis.T, precision=lax.Precision.HIGHEST, preferred_element_type=jnp.float32
    )
    gram = lax.psum(local_gram, ("dp", "mp"))
    total = 2 * count + 1
    positions = jnp.arange(total, dtype=jnp.int32)
    coeffs = (positions == 2 * count).astype(jnp.float32)
    alphas = [None] * count
    for i in reversed(range(count)):
        alphas[i] = jnp.dot(gram[i], coeffs, precision=lax.Precision.HIGHEST) / gram[i, count + i]
        coeffs = coeffs - alphas[i] * (positions == count + i).astype(jnp.float32)
    last = count - 1
    coeffs = gram[last, count + last] / gram[count + last, count + last] * coeffs
    for i in range(count):
        beta = (
            jnp.dot(gram[count + i], coeffs, precision=lax.Precision.HIGHEST) / gram[i, count + i]
        )
        coeffs = coeffs + (alphas[i] - beta) * (positions == i).astype(jnp.float32)
    return -jnp.dot(
        coeffs, basis, precision=lax.Precision.HIGHEST, preferred_element_type=jnp.float32
    )


def local(values, block_ids, labels, weights, history, steps):
    width = values.shape[2]
    owned = weights.shape[0] // width
    targets = labels.astype(jnp.float32)
    flat_ids = block_ids.reshape(-1)
    s_hist = history[0]
    y_hist = history[1]
    current = weights
    table = lax.all_gather(
        current.reshape(owned, width).astype(jnp.bfloat16), "dp", axis=0, tiled=True
    )
    picked = table[block_ids]
    partial_value = jnp.einsum("rkb,rkb->r", values, picked, preferred_element_type=jnp.float32)
    margin = lax.psum(partial_value, "mp")
    resid = jax.nn.sigmoid(margin) - targets
    contrib = (values.astype(jnp.float32) * resid[:, None, None]).reshape(-1, width)
    terms = jax.ops.segment_sum(contrib, flat_ids, num_segments=table.shape[0])
    share = lax.psum_scatter(terms, "dp", scatter_dimension=0, tiled=True)
    grad = share.reshape(-1) + ridge * current
    heading = coefficient_direction(s_hist, y_hist, grad)
    move = steps[0] * heading
    current = current + move
    return (current, grad)


def solution(mesh):
    placed = (
        P("dp", "mp", None),
        P("dp", "mp"),
        P("dp"),
        P(("dp", "mp")),
        P(None, None, ("dp", "mp")),
        P(),
    )
    return jax.shard_map(
        local,
        mesh=mesh,
        in_specs=placed,
        out_specs=(P(("dp", "mp")), P(("dp", "mp"))),
        check_vma=False,
    )
```

profile of v0, /device:TPU:0, one launch (start us, length us, event | category | flops | bytes accessed | tf_op | source)
XLA Modules:
  0.0 438.8 jit_solution(4914641414444100478)
XLA Ops:
  7.2 0.0 reduce-scatter.2.cloned.1.call-start
  7.2 0.9 compare_select_fusion
  8.1 1.1 copy.8
  9.2 0.2 copy.9
  9.4 0.3 reshape.17
  9.8 0.9 convert_bitcast_fusion
  10.7 33.0 %all_gather.3 = bf16[2048,128]{1,0:T(8,128)(2,1)S(1)} all-gather(bf16[256,128]{1,0:T(8,128)(2,1)S(1)} %convert_bitcast_fusion), channel_id=1, replica_groups=mesh['dp'=8,'mp'=4] {'dp'}, dimensions={0}, use_global_device_ids=true | all-gather | bytes 589824 | tf_op jit(solution)/shard_map/all_gather | solution.py:43
  43.7 85.8 %gather_fusion = bf16[24576,128]{1,0:T(8,128)(2,1)} fusion(bf16[2048,128]{1,0:T(8,128)(2,1)S(1)} %all_gather.3, s32[24576]{0:T(1024)S(1)} %broadcast_clamp_fusion), kind=kCustom, calls=%fused_computation | custom fusion | bytes 12681216 | tf_op jit(solution)/shard_map/gather | solution.py:46
  129.5 0.0 copy-start.3
  129.5 7.7 %fusion = f32[1024]{0:T(1024)S(1)} fusion(bf16[1024,128,24]{1,2,0:T(8,128)(2,1)} %bitcast.124, bf16[1024,24,128]{2,1,0:T(8,128)(2,1)} %param.6), kind=kLoop, calls=%fused_computation.3 | loop fusion | flops 12581888 | bytes 12587008 | tf_op jit(solution)/shard_map/rkb,rkb->r/dot_general | solution.py:47
  137.2 5.7 %psum.14 = f32[1024]{0:T(1024)S(1)} all-reduce(f32[1024]{0:T(1024)S(1)} %fusion), channel_id=1, replica_groups=mesh['dp'=8,'mp'=4] {'mp'}, use_global_device_ids=true, to_apply=%region_0.0 | all-reduce | flops 1024 | bytes 8192 | tf_op jit(solution)/shard_map/psum | solution.py:48
  142.8 0.0 copy-done.3
  142.9 0.0 copy-start
  142.9 8.8 %convert_multiply_fusion.1 = f32[1024,24,128]{2,1,0:T(8,128)} fusion(bf16[1024,24,128]{2,1,0:T(8,128)(2,1)} %param.6, f32[1024]{0:T(1024)S(1)} %convert_subtract_fusion), kind=kLoop, calls=%fused_computation.4 | loop fusion | flops 6291456 | bytes 18878464 | tf_op jit(solution)/shard_map/mul | solution.py:50
  151.7 0.0 copy-start.1
  151.7 0.3 reshape.25
  152.0 132.0 %scatter_custom_fusion = f32[2048,128]{1,0:T(8,128)} fusion(s32[24576]{0:T(1024)S(1)} %reshape.25, f32[24576,128]{1,0:T(8,128)} %bitcast.125, f32[]{:T(128)} %constant.21.clone.1), kind=kCustom, calls=%fused_computation.10 | custom fusion | flops 3145728 | bytes 1049088 | tf_op jit(solution)/shard_map/scatter-add | solution.py:51
  284.0 0.0 reduce-scatter.2.cloned.1.call-update
  284.0 0.0 copy-done
  284.0 1.1 slice_bitcast_fusion.1
  285.8 63.8 %reduce-scatter.2.cloned.1.call-done = f32[256,128]{1,0:T(8,128)} async-done(((f32[2048,128]{1,0:T(8,128)}), f32[256,128]{1,0:T(8,128)}) %reduce-scatter.2.cloned.1.call-update) | async-done | bytes 131088 | tf_op jit(solution)/shard_map/reduce_scatter | solution.py:52
  349.6 0.0 copy-done.1
  349.6 0.9 bitcast_add_fusion
  350.5 0.0 copy-start.2
  350.6 4.9 %fusion.2 = f32[17,17]{1,0:T(8,128)S(1)} fusion(f32[1,32768]{1,0:T(1,128)S(1)} %bitcast.126, f32[8,32768]{1,0:T(8,128)} %get-tuple-element.15, f32[8,32768]{1,0:T(8,128)S(1)} %get-tuple-element.14), kind=kOutput, calls=%fused_computation.7 | convolution fusion | flops 114753536 | bytes 2229380 | tf_op jit(solution)/shard_map/dot_general | solution.py:12
  355.5 40.2 %psum.15 = f32[17,17]{1,0:T(8,128)S(1)} all-reduce(f32[17,17]{1,0:T(8,128)S(1)} %fusion.2), channel_id=1, replica_groups=mesh['dp'=8,'mp'=4] {'dp','mp'}, use_global_device_ids=true, to_apply=%region_3.0 | all-reduce | flops 289 | bytes 2312 | tf_op jit(solution)/shard_map/psum | solution.py:15
  395.7 0.7 fusion.69
  396.4 0.6 fusion.6
  398.3 0.6 fusion.51
  400.2 0.6 fusion.49
  402.1 0.6 fusion.47
  404.1 0.6 fusion.45
  406.0 0.6 fusion.43
  407.9 0.6 fusion.41
  411.2 0.6 fusion.39
  413.0 0.6 fusion.37
  414.9 0.6 fusion.35
  416.8 0.6 fusion.33
  418.8 0.6 fusion.31
  420.6 0.6 fusion.29
  422.6 0.6 fusion.27
  424.5 0.6 fusion.25
  426.5 0.6 fusion.23
  428.4 2.9 fusion.1
  431.3 0.7 multiply_add_fusion
  432.0 0.0 copy-done.2
  (2 shorter events, 0.0 us)
Async XLA Ops:
  7.2 342.5 %reduce-scatter.2.cloned.1.call-start = ((), (), s32[]{:S(2)}) async-start(), calls=%async_computation.1 | async-start | bytes 1179648 | tf_op jit(solution)/shard_map/reduce_scatter | solution.py:52
  129.5 13.3 %copy-start.3 = (s32[1024]{0:T(1024)S(1)}, s32[1024]{0:T(1024)}, u32[]{:S(2)}) copy-start(s32[1024]{0:T(1024)} %param.8) | copy-start | bytes 12292
  142.9 141.2 %copy-start = (f32[2,8,32768]{2,1,0:T(8,128)S(1)}, f32[2,8,32768]{2,1,0:T(8,128)}, u32[]{:S(2)}) copy-start(f32[2,8,32768]{2,1,0:T(8,128)} %param.10) | copy-start | bytes 6291460
  151.7 198.0 %copy-start.1 = (f32[32768]{0:T(1024)S(1)}, f32[32768]{0:T(1024)}, u32[]{:S(2)}) copy-start(f32[32768]{0:T(1024)} %param.9) | copy-start | bytes 393220
  350.5 81.4 %copy-start.2 = (f32[32768]{0:T(1024)}, f32[32768]{0:T(1024)S(1)}, u32[]{:S(2)}) copy-start(f32[32768]{0:T(1024)S(1)} %bitcast_add_fusion) | copy-start | bytes 393220
Sparse Core Ops, SparseCore 0:
  284.1 65.4 reduce-scatter.1
where the time goes:
time: 440 us; the launch traced here: 439 us
  other arithmetic  162 us (37%)
  local copies, waits for them, and re-layouts  89.5 us (20%)
  blocking collectives  78.9 us (18%)
  waiting for transfers between devices  63.8 us (14%)
  between operations  37.1 us (8%)
  matrix products  7.87 us (2%)
    scatter-add x1, other arithmetic, local(): terms = jax.ops.segment_sum(contrib, flat_ids, num_segments=table.shape[0])  132 us
    gather x1, local copies, waits for them, and re-layouts, local(): picked = table[block_ids]  85.8 us
    reduce_scatter x1, waiting for transfers between devices, local(): share = lax.psum_scatter(terms, 'dp', scatter_dimension=0, tiled=True)  63.8 us
    psum x1, blocking collectives, coefficient_direction(): gram = lax.psum(local_gram, ('dp', 'mp'))  40.2 us
    all_gather x1, blocking collectives, local(): lax.all_gather(current.reshape(owned, width).astype(jnp.bfloat16), 'dp',...  33 us
  transfers between devices with their start and end apart: 1, of which 1 were waited for; matrix products, arithmetic and copies ran while one was open for 0% of the time, Pallas kernels for 0%

commit v1 on v0

v1 whole, which is shorter than its diff:
```python
import functools

import jax
import jax.numpy as jnp
from jax import lax
from jax.experimental import pallas as pl
from jax.experimental.pallas import tpu as pltpu
from jax.sharding import PartitionSpec as P

ridge = 0.2
SUB = 8
F32 = jnp.float32


def sublane_masks():
    sub = lax.broadcasted_iota(jnp.int32, (SUB, 128), 0)
    return [sub == s for s in range(SUB)]


def vmem_spec():
    return pl.BlockSpec(memory_space=pltpu.VMEM)


def smem_spec():
    return pl.BlockSpec(memory_space=pltpu.SMEM)


def params(megabytes):
    return pltpu.CompilerParams(vmem_limit_bytes=int(megabytes * 2**20))


def mib(*arrays):
    return sum(a.size * a.dtype.itemsize for a in arrays) / 2**20


def gram_body(hist, out):
    count, feats = hist.shape[1], hist.shape[2]
    width = 128

    def step(j, accs):
        at = pl.ds(pl.multiple_of(j * width, width), width)
        s_tile, y_tile = hist[0, :, at], hist[1, :, at]
        new = []
        for i in range(count):
            row = jnp.broadcast_to(y_tile[i : i + 1, :], (count, width))
            new.append((accs[i][0] + row * s_tile, accs[i][1] + row * y_tile))
        return tuple(new)

    zero = jnp.zeros((count, width), F32)
    accs = lax.fori_loop(0, feats // width, step, tuple((zero, zero) for _ in range(count)))
    lane = lax.broadcasted_iota(jnp.int32, (count, width), 1)
    for part in range(2):
        tile = zero
        for i in range(count):
            tile = jnp.where(lane == i, jnp.sum(accs[i][part], axis=1, keepdims=True), tile)
        out[part * count : (part + 1) * count, :] = tile


def gather_body(ids, vals, gram, *refs):
    *pieces, out, table, rows = refs
    count, active, width = vals.shape
    at = 0
    for piece in pieces:
        size = piece.shape[0]

        def widen(j, carry, piece=piece, at=at):
            src = pl.ds(pl.multiple_of(j * 64, 64), 64)
            dst = pl.ds(pl.multiple_of(j * 64 + at, 64), 64)
            table[dst, :] = piece[src, :].astype(F32)
            return carry

        lax.fori_loop(0, size // 64, widen, 0)
        at += size
    masks = sublane_masks()

    def group(g, carry):
        tile = jnp.zeros((SUB, width), F32)
        for u in range(SUB):
            e = g * SUB + u
            v = vals[e].astype(F32)
            total = None
            for t in range(0, active, SUB):
                pick = None
                for s in range(SUB):
                    row = table[pl.ds(ids[(t + s) * count + e], SUB, stride=0), :]
                    pick = row if pick is None else jnp.where(masks[s], row, pick)
                prod = pick * v[t : t + SUB]
                total = prod if total is None else total + prod
            total = jnp.sum(total, axis=0, keepdims=True)
            tile = jnp.where(masks[u], jnp.broadcast_to(total, (SUB, width)), tile)
        rows[pl.ds(pl.multiple_of(g * SUB, SUB), SUB), :] = tile
        return carry

    lax.fori_loop(0, count // SUB, group, 0)
    lines = count // width
    for b in range(lines):
        flipped = rows[b * width : (b + 1) * width, :].T
        out[b : b + 1, :] = jnp.sum(flipped, axis=0, keepdims=True)
    out[lines : lines + gram.shape[0], :] = gram[...]


def scatter_body(ids, resid, vals, gram, *refs, order, owned):
    n_out = 2
    outs, accs = refs[:n_out], refs[n_out:]
    count, active, width = vals.shape
    blocks = accs[0].shape[0] // SUB
    masks = sublane_masks()
    zero = jnp.zeros((SUB * SUB, width), F32)

    def clear(j, carry):
        at = pl.ds(pl.multiple_of(j * SUB * SUB, SUB * SUB), SUB * SUB)
        for acc in accs:
            acc[at, :] = zero
        return carry

    lax.fori_loop(0, blocks // SUB, clear, 0)
    n_acc = len(accs)
    unroll = 4

    def example(e):
        r = resid[e]
        v = vals[e].astype(F32) * r
        tiles = list(range(0, active, SUB))
        for first in range(0, len(tiles), n_acc):
            batch = []
            for a, t in enumerate(tiles[first : first + n_acc]):
                part = v[t : t + SUB]
                for s in range(SUB):
                    at = pl.ds(pl.multiple_of(ids[(t + s) * count + e] * SUB, SUB), SUB)
                    batch.append((a, s, at, accs[a][at, :] + part))
            for a, s, at, value in batch:
                pltpu.store(accs[a].at[at, :], value, mask=masks[s])

    def group(g, carry):
        for u in range(unroll):
            example(g * unroll + u)
        return carry

    lax.fori_loop(0, count // unroll, group, 0)

    half = len(order) // 2
    for i, p in enumerate(order):
        out = outs[0] if i < half else outs[1]

        def fold(j, carry, p=p, out=out, base=(i % half) * owned):
            total = None
            at = pl.ds(pl.multiple_of((p * owned + j * SUB) * SUB, SUB * SUB), SUB * SUB)
            for acc in accs:
                x = acc[at, :].reshape(SUB, SUB, width)
                total = x if total is None else total + x
            out[pl.ds(pl.multiple_of(base + j * SUB, SUB), SUB), :] = jnp.sum(total, axis=1)
            return carry

        lax.fori_loop(0, owned // SUB, fold, 0)
    for out in outs:
        out[half * owned :, :] = gram[...]


def dots_body(keep, recv, w, hist, grad, dots, gram):
    count, feats = hist.shape[1], hist.shape[2]
    rows, width = w.shape
    grad[...] = keep[:rows, :] + recv[:rows, :] + ridge * w[...]
    gram[...] = keep[rows:, :] + recv[rows:, :]

    def step(j, accs):
        at = pl.ds(pl.multiple_of(j * width, width), width)
        g = grad[pl.ds(j, count, stride=0), :]
        return (accs[0] + g * hist[0, :, at], accs[1] + g * hist[1, :, at])

    zero = jnp.zeros((count, width), F32)
    accs = lax.fori_loop(0, feats // width, step, (zero, zero), unroll=8)
    dots[:count, :] = accs[0]
    dots[count:, :] = accs[1]


def coefficient_body(gram, out):
    count = gram.shape[0] // 2
    width = 128
    lane = lax.broadcasted_iota(jnp.int32, (1, width), 1)
    sy = lambda k, i: gram[k, i]
    yy = lambda k, i: gram[count + k, i]
    unit = lambda k: (lane == k).astype(F32)
    rho = [1.0 / jnp.full((1, width), sy(i, i), F32) for i in range(count)]
    last = count - 1
    gamma = jnp.full((1, width), sy(last, last), F32) / jnp.full((1, width), yy(last, last), F32)
    alpha = [None] * count
    for i in reversed(range(count)):
        value = unit(i)
        for j in range(i + 1, count):
            value = value - alpha[j] * sy(i, j)
        alpha[i] = rho[i] * value
    weight = []
    for i in range(count):
        value = unit(count + i)
        for j in range(count):
            value = value - alpha[j] * yy(i, j)
        value = gamma * value
        for k in range(i):
            value = value + weight[k] * sy(k, i)
        weight.append(alpha[i] - rho[i] * value)
    for k in range(count):
        out[k : k + 1, :] = weight[k]
        out[count + k : count + k + 1, :] = -gamma * alpha[k]
    out[2 * count :, :] = jnp.broadcast_to(gamma, (count, width))


def move_body(steps, coef, dots, recv, grad, w, hist, out):
    count = hist.shape[1]
    rows, width = w.shape
    sums = jnp.sum(dots[...] + recv[...], axis=1, keepdims=True)
    sub = lax.broadcasted_iota(jnp.int32, (2 * count, width), 0)
    lane = lax.broadcasted_iota(jnp.int32, (2 * count, width), 1)
    line = jnp.sum(jnp.where(sub == lane, sums, 0.0), axis=0, keepdims=True)
    mixed = jnp.sum(coef[: 2 * count, :] * line, axis=1, keepdims=True)
    c_s = jnp.broadcast_to(mixed[:count], (count, width))
    c_y = jnp.broadcast_to(mixed[count:], (count, width))
    gamma = coef[2 * count :, :]
    rate = steps[0]
    masks = sublane_masks()

    def step(j, carry):
        tile = jnp.zeros((SUB, width), F32)
        for u in range(SUB):
            at = pl.ds(pl.multiple_of((j * SUB + u) * width, width), width)
            mix = jnp.sum(c_s * hist[0, :, at] + c_y * hist[1, :, at], axis=0, keepdims=True)
            tile = jnp.where(masks[u], jnp.broadcast_to(mix, (SUB, width)), tile)
        at = pl.ds(pl.multiple_of(j * SUB, SUB), SUB)
        out[at, :] = w[at, :] - rate * (gamma * grad[at, :] + tile)
        return carry

    lax.fori_loop(0, rows // SUB, step, 0)


def gather_stages(n):
    stages = []
    top = n // 2
    while top >= 4:
        stages.append([top])
        top //= 2
    stages.append([k for k in (1, 2, 3) if k < n])
    return [s for s in stages if s]


def reduce_bits(n):
    bits = []
    b = 1
    while b < n:
        bits.append(b)
        b *= 2
    return bits


def xor_permute(x, axis, n, k):
    return lax.ppermute(x, axis, [(i, i ^ k) for i in range(n)])


def local(values, block_ids, labels, weights, history, steps, *, n_dp, n_mp):
    count, active, width = values.shape
    features = weights.shape[0]
    owned = features // width
    blocks = owned * n_dp
    pairs = history.shape[1]
    lines = count // width
    me = lax.axis_index("dp")
    w2 = weights.reshape(owned, width)

    pieces = [w2.astype(jnp.bfloat16)]
    order = [0]
    for offsets in gather_stages(n_dp):
        whole = pieces[0] if len(pieces) == 1 else jnp.concatenate(pieces, axis=0)
        came = [xor_permute(whole, "dp", n_dp, k) for k in offsets]
        pieces = pieces + came
        order = order + [p ^ k for k in offsets for p in order]
    place = [0] * n_dp
    for at, p in enumerate(order):
        place[p] = at
    ids_t = block_ids.T
    owner = ids_t // owned
    spot = owner ^ me
    where = jnp.zeros_like(spot)
    for p in range(n_dp):
        where = jnp.where(spot == p, place[p], where)
    flat_ids = (where * owned + (ids_t - owner * owned)).reshape(-1)

    gram = pl.pallas_call(
        gram_body,
        out_shape=jax.ShapeDtypeStruct((2 * pairs, width), F32),
        in_specs=[vmem_spec()],
        out_specs=vmem_spec(),
        compiler_params=params(2 * mib(history) + 2),
    )(history)

    table_mib = blocks * width * 4 / 2**20
    packed = pl.pallas_call(
        gather_body,
        out_shape=jax.ShapeDtypeStruct((lines + 2 * pairs, width), F32),
        in_specs=[smem_spec(), vmem_spec(), vmem_spec()] + [vmem_spec()] * len(pieces),
        out_specs=vmem_spec(),
        scratch_shapes=[pltpu.VMEM((blocks, width), F32), pltpu.VMEM((count, width), F32)],
        compiler_params=params(mib(values) + 2 * table_mib + 6),
    )(flat_ids, values, gram, *pieces)

    packed = jnp.sum(lax.all_gather(packed, "mp", axis=0), axis=0)
    resid = jax.nn.sigmoid(packed[:lines].reshape(-1)) - labels.astype(F32)
    gram_rows = packed[lines:]

    bits = reduce_bits(n_dp)
    wanted = [0]
    for b in reversed(bits):
        wanted = [p ^ b for p in wanted] + wanted
    slots = [place[p] for p in wanted]

    acc_mib = SUB * table_mib
    room = (60 * 1024) / 1024 - mib(values) - table_mib - 6
    n_acc = max(1, min(active // SUB, int(room // acc_mib)))
    half = n_dp // 2 * owned + 2 * pairs
    send, keep = pl.pallas_call(
        functools.partial(scatter_body, order=slots, owned=owned),
        out_shape=[jax.ShapeDtypeStruct((half, width), F32)] * 2,
        in_specs=[smem_spec(), smem_spec(), vmem_spec(), vmem_spec()],
        out_specs=[vmem_spec(), vmem_spec()],
        scratch_shapes=[pltpu.VMEM((blocks * SUB, width), F32)] * n_acc,
        compiler_params=params(mib(values) + table_mib + n_acc * acc_mib + 3),
    )(flat_ids, resid, values, gram_rows)

    size = n_dp // 2
    tail = 2 * pairs
    for b in bits:
        came = xor_permute(send, "dp", n_dp, b)
        if size == 1:
            break
        total = keep + came
        size //= 2
        cut = size * owned
        total_gram = total[2 * cut :]
        send = jnp.concatenate([total[:cut], total_gram], axis=0)
        keep = jnp.concatenate([total[cut : 2 * cut], total_gram], axis=0)

    grad, dots, gram_all = pl.pallas_call(
        dots_body,
        out_shape=[
            jax.ShapeDtypeStruct((owned, width), F32),
            jax.ShapeDtypeStruct((2 * pairs, width), F32),
            jax.ShapeDtypeStruct((2 * pairs, width), F32),
        ],
        in_specs=[vmem_spec()] * 4,
        out_specs=[vmem_spec()] * 3,
        compiler_params=params(2 * mib(history) + 4),
    )(keep, came, w2, history)

    coef = pl.pallas_call(
        coefficient_body,
        out_shape=jax.ShapeDtypeStruct((3 * pairs, width), F32),
        in_specs=[smem_spec()],
        out_specs=vmem_spec(),
        compiler_params=params(4),
    )(gram_all)

    hops = [("mp", n_mp, b) for b in reduce_bits(n_mp)] + [("dp", n_dp, b) for b in bits]
    for axis, n, b in hops[:-1]:
        dots = dots + xor_permute(dots, axis, n, b)
    axis, n, b = hops[-1]
    other = xor_permute(dots, axis, n, b)

    moved = pl.pallas_call(
        move_body,
        out_shape=jax.ShapeDtypeStruct((owned, width), F32),
        in_specs=[smem_spec()] + [vmem_spec()] * 6,
        out_specs=vmem_spec(),
        compiler_params=params(2 * mib(history) + 4),
    )(steps, coef, dots, other, grad, w2, history)
    return moved.reshape(-1), grad.reshape(-1)


def solution(mesh):
    placed = (
        P("dp", "mp", None),
        P("dp", "mp"),
        P("dp"),
        P(("dp", "mp")),
        P(None, None, ("dp", "mp")),
        P(),
    )
    return jax.shard_map(
        functools.partial(local, n_dp=mesh.shape["dp"], n_mp=mesh.shape["mp"]),
        mesh=mesh,
        in_specs=placed,
        out_specs=(P(("dp", "mp")), P(("dp", "mp"))),
        check_vma=False,
    )
```

time: 440 us -> 152 us (0.35)
  other arithmetic: 162 us -> 2.08 us
  local copies, waits for them, and re-layouts: 89.5 us -> 8.14 us
  Pallas kernels: 0 us -> 78.1 us
  blocking collectives: 78.9 us -> 5.35 us
  between operations: 37.1 us -> 1.47 us
  waiting for transfers between devices: 63.8 us -> 38.3 us
  starting transfers between devices: 0.04 us -> 18.8 us
  matrix products: 7.87 us -> 0 us
    scatter-add x1 -> x0, other arithmetic: 132 us -> none  [local(): terms = jax.ops.segment_sum(contrib, flat_ids, num_segments=table.shape[0])]
    gather x1 -> x0, local copies, waits for them, and re-layouts: 85.8 us -> none  [local(): picked = table[block_ids]]
    pallas_call x0 -> x6, Pallas kernels: none -> 78.1 us  [the longest x1 36.3 us: local(): pl.pallas_call(functools.partial(scatter_body, order=slots, owned=owned),...]
    reduce_scatter x1 -> x0, waiting for transfers between devices: 63.8 us -> none  [local(): share = lax.psum_scatter(terms, 'dp', scatter_dimension=0, tiled=True)]
    psum x2 -> x0, blocking collectives: 45.9 us -> none  [the longest x1 40.2 us: coefficient_direction(): gram = lax.psum(local_gram, ('dp', 'mp'))]
    ppermute x0 -> x12, waiting for transfers between devices: none -> 38.3 us  [xor_permute(): return lax.ppermute(x, axis, [(i, i ^ k) for i in range(n)])]
    all_gather x1, blocking collectives: 33 us -> 5.35 us  [local(): packed = jnp.sum(lax.all_gather(packed, 'mp', axis=0), axis=0)]
    ppermute x0 -> x12, starting transfers between devices: none -> 18.8 us  [xor_permute(): return lax.ppermute(x, axis, [(i, i ^ k) for i in range(n)])]
  transfers between devices with their start and end apart: 1 -> 12, of which waited for: 1 -> 9; matrix products, arithmetic and copies ran while one was open for 0% -> 1% of each run, Pallas kernels for 0% -> 2%
where the time goes in v1:
time: 152 us
  Pallas kernels  78.1 us (51%)
  waiting for transfers between devices  38.3 us (25%)
  starting transfers between devices  18.8 us (12%)
  local copies, waits for them, and re-layouts  8.14 us (5%)
  blocking collectives  5.35 us (4%)
  other arithmetic  2.08 us (1%)
    ppermute x12, waiting for transfers between devices, xor_permute(): return lax.ppermute(x, axis, [(i, i ^ k) for i in range(n)])  38.3 us
    pallas_call x1, Pallas kernels, local(): pl.pallas_call(functools.partial(scatter_body, order=slots, owned=owned),...  36.3 us
    pallas_call x1, Pallas kernels, local(): pl.pallas_call(gather_body, out_shape=jax.ShapeDtypeStruct((lines + 2 * p...  35.6 us
    ppermute x12, starting transfers between devices, xor_permute(): return lax.ppermute(x, axis, [(i, i ^ k) for i in range(n)])  18.8 us
    unnamed x15, local copies, waits for them, and re-layouts  8.09 us
    all_gather x1, blocking collectives, local(): packed = jnp.sum(lax.all_gather(packed, 'mp', axis=0), axis=0)  5.35 us
  transfers between devices with their start and end apart: 12, of which 9 were waited for; matrix products, arithmetic and copies ran while one was open for 1% of the time, Pallas kernels for 2%

profile of v1, /device:TPU:0, one launch (start us, length us, event | category | flops | bytes accessed | tf_op | source)
XLA Modules:
  0.0 152.1 jit_solution(2552400973046541025)
XLA Ops:
  0.6 0.0 copy-start.6
  0.6 0.9 bitcast_convert_fusion.refs_0_
  1.6 4.1 %collective-permute-start = (bf16[256,128]{1,0:T(8,128)(2,1)S(1)}, bf16[256,128]{1,0:T(8,128)(2,1)S(1)}, u32[]{:S(2)}, u32[]{:S(2)}) collective-permute-start(bf16[256,128]{1,0:T(8,128)(2,1)S(1)} %bitcast_convert_fusion.refs_0_), channel_id=1, source_target_pairs={{0,16},{4,20},{8,24},{12,28},{16,0},{20,4},{24,8},{28,12},{1,17},{... | collective-permute-start | bytes 196616 | tf_op jit(solution)/shard_map/ppermute | solution.py:254
  5.6 3.6 %collective-permute-done.refs_1_ = bf16[256,128]{1,0:T(8,128)(2,1)S(1)} collective-permute-done((bf16[256,128]{1,0:T(8,128)(2,1)S(1)}, bf16[256,128]{1,0:T(8,128)(2,1)S(1)}, u32[]{:S(2)}, u32[]{:S(2)}) %collective-permute-start) | collective-permute-done | bytes 65568 | tf_op jit(solution)/shard_map/ppermute | solution.py:254
  9.3 1.8 %collective-permute-start.1 = (bf16[512,128]{1,0:T(8,128)(2,1)S(1)}, bf16[512,128]{1,0:T(8,128)(2,1)S(1)}, u32[]{:S(2)}, u32[]{:S(2)}) collective-permute-start(bf16[512,128]{1,0:T(8,128)(2,1)S(1)} %pad_maximum_fusion.2), channel_id=1, source_target_pairs={{0,4},{4,0},{8,12},{12,8},{16,20},{20,16},{24,28},{28,24},{1,5},{5... | collective-permute-start | bytes 393224 | tf_op jit(solution)/shard_map/ppermute | solution.py:254
  11.1 0.4 collective-permute-start.2
  11.4 1.4 collective-permute-start.3
  12.8 1.0 fusion.3
  13.9 0.0 copy-start.2
  13.9 1.6 %copy-done.2 = f32[2,8,32768]{2,1,0:T(8,128)S(1)} copy-done((f32[2,8,32768]{2,1,0:T(8,128)S(1)}, f32[2,8,32768]{2,1,0:T(8,128)}, u32[]{:S(2)}) %copy-start.2) | copy-done | bytes 2097176
  15.5 2.6 %shard_map.77.gram = f32[16,128]{1,0:T(8,128)S(1)} custom-call(f32[2,8,32768]{2,1,0:T(8,128)S(1)} %copy-done.2), custom_call_target="tpu_custom_call" | custom-call | tf_op jit(solution)/shard_map/pallas_call | solution.py:285
  18.1 0.0 collective-permute-done.1.refs_2_
  18.1 0.0 collective-permute-done.2.refs_3_
  18.1 0.0 collective-permute-done.3.refs_4_
  18.1 0.0 copy-start
  18.2 2.8 %copy-done = bf16[1024,24,128]{2,1,0:T(8,128)(2,1)S(1)} copy-done((bf16[1024,24,128]{2,1,0:T(8,128)(2,1)S(1)}, bf16[1024,24,128]{2,1,0:T(8,128)(2,1)}, u32[]{:S(2)}) %copy-start) | copy-done | bytes 6291480
  20.9 0.0 copy-start.3
  20.9 35.6 %shard_map.78 = f32[24,128]{1,0:T(8,128)S(1)} custom-call(s32[24576]{0:T(1024)S(1)} %bitcast.37, bf16[1024,24,128]{2,1,0:T(8,128)(2,1)S(1)} %copy-done, f32[16,128]{1,0:T(8,128)S(1)} %shard_map.77.gram, bf16[256,128]{1,0:T(8,128)(2,1)S(1)} %bitcast_convert_fusion.refs_0_, bf16[256,128]{1,0:T(8,128)(2,1)S(1)} %collective-permute-done.refs_1_, ...), custom_call_target="tpu_custom_call" | custom-call | tf_op jit(solution)/shard_map/pallas_call | solution.py:294
  56.6 0.0 copy-start.4
  56.6 5.4 %all-gather = f32[96,128]{1,0:T(8,128)S(1)} all-gather(f32[24,128]{1,0:T(8,128)S(1)} %shard_map.78), channel_id=2, replica_groups=mesh['dp'=8,'mp'=4] {'mp'}, dimensions={0}, use_global_device_ids=true | all-gather | bytes 61440 | tf_op jit(solution)/shard_map/all_gather | solution.py:303
  62.0 0.0 copy-done.6
  62.0 0.0 copy-start.1
  62.0 2.8 %copy-done.1 = bf16[1024,24,128]{2,1,0:T(8,128)(2,1)S(1)} copy-done((bf16[1024,24,128]{2,1,0:T(8,128)(2,1)S(1)}, bf16[1024,24,128]{2,1,0:T(8,128)(2,1)}, u32[]{:S(2)}) %copy-start.1) | copy-done | bytes 6291480
  64.8 36.3 %shard_map.79 = (f32[1040,128]{1,0:T(8,128)S(1)}, f32[1040,128]{1,0:T(8,128)S(1)}) custom-call(s32[24576]{0:T(1024)S(1)} %bitcast.38, f32[1024]{0:T(1024)S(1)} %fusion.9.resid, bf16[1024,24,128]{2,1,0:T(8,128)(2,1)S(1)} %copy-done.1, f32[16,128]{1,0:T(8,128)S(1)} %slice.29.gram), custom_call_target="tpu_custom_call" | custom-call | tf_op jit(solution)/shard_map/pallas_call | solution.py:317
  101.1 1.8 %collective-permute-start.4 = (f32[1040,128]{1,0:T(8,128)S(1)}, f32[1040,128]{1,0:T(8,128)S(1)}, u32[]{:S(2)}, u32[]{:S(2)}) collective-permute-start(f32[1040,128]{1,0:T(8,128)S(1)} %get-tuple-element.8), channel_id=1, source_target_pairs={{0,4},{4,0},{8,12},{12,8},{16,20},{20,16},{24,28},{28,24},{1,5},{5... | collective-permute-start | bytes 1597448 | tf_op jit(solution)/shard_map/ppermute | solution.py:254
  102.8 12.7 %collective-permute-done.4 = f32[1040,128]{1,0:T(8,128)S(1)} collective-permute-done((f32[1040,128]{1,0:T(8,128)S(1)}, f32[1040,128]{1,0:T(8,128)S(1)}, u32[]{:S(2)}, u32[]{:S(2)}) %collective-permute-start.4) | collective-permute-done | bytes 532512 | tf_op jit(solution)/shard_map/ppermute | solution.py:254
  115.5 0.1 add.28
  115.6 0.9 collective-permute-start.5
  116.5 7.1 %collective-permute-done.5 = f32[528,128]{1,0:T(8,128)S(1)} collective-permute-done((f32[528,128]{1,0:T(8,128)S(1)}, f32[528,128]{1,0:T(8,128)S(1)}, u32[]{:S(2)}, u32[]{:S(2)}) %collective-permute-start.5) | collective-permute-done | bytes 270368 | tf_op jit(solution)/shard_map/ppermute | solution.py:254
  123.6 2.6 %collective-permute-start.6 = (f32[272,128]{1,0:T(8,128)S(1)}, f32[272,128]{1,0:T(8,128)S(1)}, u32[]{:S(2)}, u32[]{:S(2)}) collective-permute-start(f32[272,128]{1,0:T(8,128)S(1)} %pad_maximum_fusion.1), channel_id=1, source_target_pairs={{0,16},{4,20},{8,24},{12,28},{16,0},{20,4},{24,8},{28,12},{1,17},{... | collective-permute-start | bytes 417800 | tf_op jit(solution)/shard_map/ppermute | solution.py:254
  126.2 5.6 %collective-permute-done.6.recv = f32[272,128]{1,0:T(8,128)S(1)} collective-permute-done((f32[272,128]{1,0:T(8,128)S(1)}, f32[272,128]{1,0:T(8,128)S(1)}, u32[]{:S(2)}, u32[]{:S(2)}) %collective-permute-start.6) | collective-permute-done | bytes 139296 | tf_op jit(solution)/shard_map/ppermute | solution.py:254
  131.8 0.0 copy-done.3
  131.8 0.0 copy-done.4
  131.8 1.2 shard_map.80
  133.0 0.0 collective-permute-start.7
  133.0 1.2 collective-permute-done.7
  134.2 1.7 %collective-permute-start.8 = (f32[16,128]{1,0:T(8,128)S(1)}, f32[16,128]{1,0:T(8,128)S(1)}, u32[]{:S(2)}, u32[]{:S(2)}) collective-permute-start(f32[16,128]{1,0:T(8,128)S(1)} %add.30), channel_id=1, source_target_pairs={{0,2},{1,3},{2,0},{3,1},{4,6},{5,7},{6,4},{7,5},{8,10},{9,11},{10,... | collective-permute-start | bytes 24584 | tf_op jit(solution)/shard_map/ppermute | solution.py:254
  135.9 1.9 %collective-permute-done.8 = f32[16,128]{1,0:T(8,128)S(1)} collective-permute-done((f32[16,128]{1,0:T(8,128)S(1)}, f32[16,128]{1,0:T(8,128)S(1)}, u32[]{:S(2)}, u32[]{:S(2)}) %collective-permute-start.8) | collective-permute-done | bytes 8224 | tf_op jit(solution)/shard_map/ppermute | solution.py:254
  137.8 1.7 %collective-permute-start.9 = (f32[16,128]{1,0:T(8,128)S(1)}, f32[16,128]{1,0:T(8,128)S(1)}, u32[]{:S(2)}, u32[]{:S(2)}) collective-permute-start(f32[16,128]{1,0:T(8,128)S(1)} %add.31), channel_id=1, source_target_pairs={{0,4},{4,0},{8,12},{12,8},{16,20},{20,16},{24,28},{28,24},{1,5},{5... | collective-permute-start | bytes 24584 | tf_op jit(solution)/shard_map/ppermute | solution.py:254
  139.5 1.9 %collective-permute-done.9 = f32[16,128]{1,0:T(8,128)S(1)} collective-permute-done((f32[16,128]{1,0:T(8,128)S(1)}, f32[16,128]{1,0:T(8,128)S(1)}, u32[]{:S(2)}, u32[]{:S(2)}) %collective-permute-start.9) | collective-permute-done | bytes 8224 | tf_op jit(solution)/shard_map/ppermute | solution.py:254
  141.5 0.6 collective-permute-start.10
  142.1 3.1 %collective-permute-done.10 = f32[16,128]{1,0:T(8,128)S(1)} collective-permute-done((f32[16,128]{1,0:T(8,128)S(1)}, f32[16,128]{1,0:T(8,128)S(1)}, u32[]{:S(2)}, u32[]{:S(2)}) %collective-permute-start.10) | collective-permute-done | bytes 8224 | tf_op jit(solution)/shard_map/ppermute | solution.py:254
  145.1 1.9 %collective-permute-start.11 = (f32[16,128]{1,0:T(8,128)S(1)}, f32[16,128]{1,0:T(8,128)S(1)}, u32[]{:S(2)}, u32[]{:S(2)}) collective-permute-start(f32[16,128]{1,0:T(8,128)S(1)} %add.33.dots), channel_id=1, source_target_pairs={{0,16},{4,20},{8,24},{12,28},{16,0},{20,4},{24,8},{28,12},{1,17},{... | collective-permute-start | bytes 24584 | tf_op jit(solution)/shard_map/ppermute | solution.py:254
  147.7 0.8 shard_map.81.coef
  148.5 1.2 collective-permute-done.11.recv
  149.7 0.0 copy-start.5
  149.7 0.9 copy-done.5
  150.6 1.6 %shard_map.82 = f32[256,128]{1,0:T(8,128)} custom-call(f32[1]{0:T(128)S(6)} %copy.9.steps, f32[24,128]{1,0:T(8,128)S(1)} %shard_map.81.coef, f32[16,128]{1,0:T(8,128)S(1)} %add.33.dots, f32[16,128]{1,0:T(8,128)S(1)} %collective-permute-done.11.recv, f32[256,128]{1,0:T(8,128)S(1)} %copy-done.5, f32[256,128]{1,0:T(8,128)S(1)} %bitcast.36, ...), custom_call_target="tpu_custom_call" | custom-call | tf_op jit(solution)/shard_map/pallas_call | solution.py:365
  (17 shorter events, 0.2 us)
Async XLA Ops:
  0.6 61.3 %copy-start.6 = (s32[1024]{0:T(1024)S(1)}, s32[1024]{0:T(1024)}, u32[]{:S(2)}) copy-start(s32[1024]{0:T(1024)} %param.8) | copy-start | bytes 12292
  1.6 7.7 %collective-permute-start = (bf16[256,128]{1,0:T(8,128)(2,1)S(1)}, bf16[256,128]{1,0:T(8,128)(2,1)S(1)}, u32[]{:S(2)}, u32[]{:S(2)}) collective-permute-start(bf16[256,128]{1,0:T(8,128)(2,1)S(1)} %bitcast_convert_fusion.refs_0_), channel_id=1, source_target_pairs={{0,16},{4,20},{8,24},{12,28},{16,0},{20,4},{24,8},{28,12},{1,17},{... | collective-permute-start | bytes 196616 | tf_op jit(solution)/shard_map/ppermute | solution.py:254
  9.3 8.8 %collective-permute-start.1 = (bf16[512,128]{1,0:T(8,128)(2,1)S(1)}, bf16[512,128]{1,0:T(8,128)(2,1)S(1)}, u32[]{:S(2)}, u32[]{:S(2)}) collective-permute-start(bf16[512,128]{1,0:T(8,128)(2,1)S(1)} %pad_maximum_fusion.2), channel_id=1, source_target_pairs={{0,4},{4,0},{8,12},{12,8},{16,20},{20,16},{24,28},{28,24},{1,5},{5... | collective-permute-start | bytes 393224 | tf_op jit(solution)/shard_map/ppermute | solution.py:254
  11.1 7.1 %collective-permute-start.2 = (bf16[512,128]{1,0:T(8,128)(2,1)S(1)}, bf16[512,128]{1,0:T(8,128)(2,1)S(1)}, u32[]{:S(2)}, u32[]{:S(2)}) collective-permute-start(bf16[512,128]{1,0:T(8,128)(2,1)S(1)} %pad_maximum_fusion.2), channel_id=1, source_target_pairs={{0,8},{4,12},{8,0},{12,4},{16,24},{20,28},{24,16},{28,20},{1,9},{5... | collective-permute-start | bytes 393224 | tf_op jit(solution)/shard_map/ppermute | solution.py:254
  11.4 6.7 %collective-permute-start.3 = (bf16[512,128]{1,0:T(8,128)(2,1)S(1)}, bf16[512,128]{1,0:T(8,128)(2,1)S(1)}, u32[]{:S(2)}, u32[]{:S(2)}) collective-permute-start(bf16[512,128]{1,0:T(8,128)(2,1)S(1)} %pad_maximum_fusion.2), channel_id=1, source_target_pairs={{0,12},{4,8},{8,4},{12,0},{16,28},{20,24},{24,20},{28,16},{1,13},{... | collective-permute-start | bytes 393224 | tf_op jit(solution)/shard_map/ppermute | solution.py:254
  13.9 1.6 %copy-start.2 = (f32[2,8,32768]{2,1,0:T(8,128)S(1)}, f32[2,8,32768]{2,1,0:T(8,128)}, u32[]{:S(2)}) copy-start(f32[2,8,32768]{2,1,0:T(8,128)} %hist.5) | copy-start | bytes 6291460
  18.1 2.8 %copy-start = (bf16[1024,24,128]{2,1,0:T(8,128)(2,1)S(1)}, bf16[1024,24,128]{2,1,0:T(8,128)(2,1)}, u32[]{:S(2)}) copy-start(bf16[1024,24,128]{2,1,0:T(8,128)(2,1)} %vals.3) | copy-start | bytes 18874372
  20.9 110.9 %copy-start.3 = (f32[2,8,32768]{2,1,0:T(8,128)S(1)}, f32[2,8,32768]{2,1,0:T(8,128)}, u32[]{:S(2)}) copy-start(f32[2,8,32768]{2,1,0:T(8,128)} %hist.5) | copy-start | bytes 6291460
  56.6 75.2 %copy-start.4 = (f32[32768]{0:T(1024)S(1)}, f32[32768]{0:T(1024)}, u32[]{:S(2)}) copy-start(f32[32768]{0:T(1024)} %param.9) | copy-start | bytes 393220
  62.0 2.8 %copy-start.1 = (bf16[1024,24,128]{2,1,0:T(8,128)(2,1)S(1)}, bf16[1024,24,128]{2,1,0:T(8,128)(2,1)}, u32[]{:S(2)}) copy-start(bf16[1024,24,128]{2,1,0:T(8,128)(2,1)} %vals.3) | copy-start | bytes 18874372
  101.1 14.4 %collective-permute-start.4 = (f32[1040,128]{1,0:T(8,128)S(1)}, f32[1040,128]{1,0:T(8,128)S(1)}, u32[]{:S(2)}, u32[]{:S(2)}) collective-permute-start(f32[1040,128]{1,0:T(8,128)S(1)} %get-tuple-element.8), channel_id=1, source_target_pairs={{0,4},{4,0},{8,12},{12,8},{16,20},{20,16},{24,28},{28,24},{1,5},{5... | collective-permute-start | bytes 1597448 | tf_op jit(solution)/shard_map/ppermute | solution.py:254
  115.6 7.9 %collective-permute-start.5 = (f32[528,128]{1,0:T(8,128)S(1)}, f32[528,128]{1,0:T(8,128)S(1)}, u32[]{:S(2)}, u32[]{:S(2)}) collective-permute-start(f32[528,128]{1,0:T(8,128)S(1)} %pad_maximum_fusion), channel_id=1, source_target_pairs={{0,8},{4,12},{8,0},{12,4},{16,24},{20,28},{24,16},{28,20},{1,9},{5... | collective-permute-start | bytes 811016 | tf_op jit(solution)/shard_map/ppermute | solution.py:254
  123.6 8.2 %collective-permute-start.6 = (f32[272,128]{1,0:T(8,128)S(1)}, f32[272,128]{1,0:T(8,128)S(1)}, u32[]{:S(2)}, u32[]{:S(2)}) collective-permute-start(f32[272,128]{1,0:T(8,128)S(1)} %pad_maximum_fusion.1), channel_id=1, source_target_pairs={{0,16},{4,20},{8,24},{12,28},{16,0},{20,4},{24,8},{28,12},{1,17},{... | collective-permute-start | bytes 417800 | tf_op jit(solution)/shard_map/ppermute | solution.py:254
  133.0 1.2 collective-permute-start.7
  134.2 3.7 %collective-permute-start.8 = (f32[16,128]{1,0:T(8,128)S(1)}, f32[16,128]{1,0:T(8,128)S(1)}, u32[]{:S(2)}, u32[]{:S(2)}) collective-permute-start(f32[16,128]{1,0:T(8,128)S(1)} %add.30), channel_id=1, source_target_pairs={{0,2},{1,3},{2,0},{3,1},{4,6},{5,7},{6,4},{7,5},{8,10},{9,11},{10,... | collective-permute-start | bytes 24584 | tf_op jit(solution)/shard_map/ppermute | solution.py:254
  137.8 3.7 %collective-permute-start.9 = (f32[16,128]{1,0:T(8,128)S(1)}, f32[16,128]{1,0:T(8,128)S(1)}, u32[]{:S(2)}, u32[]{:S(2)}) collective-permute-start(f32[16,128]{1,0:T(8,128)S(1)} %add.31), channel_id=1, source_target_pairs={{0,4},{4,0},{8,12},{12,8},{16,20},{20,16},{24,28},{28,24},{1,5},{5... | collective-permute-start | bytes 24584 | tf_op jit(solution)/shard_map/ppermute | solution.py:254
  141.5 3.7 %collective-permute-start.10 = (f32[16,128]{1,0:T(8,128)S(1)}, f32[16,128]{1,0:T(8,128)S(1)}, u32[]{:S(2)}, u32[]{:S(2)}) collective-permute-start(f32[16,128]{1,0:T(8,128)S(1)} %add.32), channel_id=1, source_target_pairs={{0,8},{4,12},{8,0},{12,4},{16,24},{20,28},{24,16},{28,20},{1,9},{5... | collective-permute-start | bytes 24584 | tf_op jit(solution)/shard_map/ppermute | solution.py:254
  145.1 4.5 %collective-permute-start.11 = (f32[16,128]{1,0:T(8,128)S(1)}, f32[16,128]{1,0:T(8,128)S(1)}, u32[]{:S(2)}, u32[]{:S(2)}) collective-permute-start(f32[16,128]{1,0:T(8,128)S(1)} %add.33.dots), channel_id=1, source_target_pairs={{0,16},{4,20},{8,24},{12,28},{16,0},{20,4},{24,8},{28,12},{1,17},{... | collective-permute-start | bytes 24584 | tf_op jit(solution)/shard_map/ppermute | solution.py:254
  149.7 0.9 copy-start.5

commit v2 on v1

--- a/solution.py
+++ b/solution.py
@@ -23,6 +23,18 @@
 
 def smem_spec():
     return pl.BlockSpec(memory_space=pltpu.SMEM)
+
+
+def any_spec():
+    return pl.BlockSpec(memory_space=pl.ANY)
+
+
+def hbm_spec():
+    return pl.BlockSpec(memory_space=pltpu.HBM)
+
+
+def entry(ref, base, offset):
+    return ref.at[pl.ds(base + offset, 1)][0]
 
 
 def params(megabytes):
@@ -56,9 +68,20 @@
         out[part * count : (part + 1) * count, :] = tile
 
 
-def gather_body(ids, vals, gram, *refs):
-    *pieces, out, table, rows = refs
+def chunk_copies(src, dst, sems):
+    n = sems.shape[0]
+    size = src.shape[0] // n
+    return [pltpu.make_async_copy(src.at[pl.ds(c * size, size)], dst.at[pl.ds(c * size, size)], sems.at[c]) for c in range(n)]
+
+
+def gather_body(ids_in, vals_in, gram, *refs):
+    *pieces, out, table, rows, vals, ids, vals_sems, ids_sems = refs
     count, active, width = vals.shape
+    copies = chunk_copies(vals_in, vals, vals_sems)
+    id_copies = chunk_copies(ids_in, ids, ids_sems)
+    for i, c in zip(id_copies, copies):
+        i.start()
+        c.start()
     at = 0
     for piece in pieces:
         size = piece.shape[0]
@@ -82,7 +105,7 @@
             for t in range(0, active, SUB):
                 pick = None
                 for s in range(SUB):
-                    row = table[pl.ds(ids[(t + s) * count + e], SUB, stride=0), :]
+                    row = table[pl.ds(entry(ids, e * active, t + s), SUB, stride=0), :]
                     pick = row if pick is None else jnp.where(masks[s], row, pick)
                 prod = pick * v[t : t + SUB]
                 total = prod if total is None else total + prod
@@ -91,7 +114,11 @@
         rows[pl.ds(pl.multiple_of(g * SUB, SUB), SUB), :] = tile
         return carry
 
-    lax.fori_loop(0, count // SUB, group, 0)
+    per = count // SUB // len(copies)
+    for i, (a, c) in enumerate(zip(id_copies, copies)):
+        a.wait()
+        c.wait()
+        lax.fori_loop(i * per, (i + 1) * per, group, 0)
     lines = count // width
     for b in range(lines):
         flipped = rows[b * width : (b + 1) * width, :].T
@@ -99,10 +126,16 @@
     out[lines : lines + gram.shape[0], :] = gram[...]
 
 
-def scatter_body(ids, resid, vals, gram, *refs, order, owned):
+def scatter_body(ids_in, resid, vals_in, gram, *refs, order, owned):
     n_out = 2
-    outs, accs = refs[:n_out], refs[n_out:]
+    outs, accs = refs[:n_out], refs[n_out:-4]
+    vals, ids, vals_sems, ids_sems = refs[-4:]
     count, active, width = vals.shape
+    copies = chunk_copies(vals_in, vals, vals_sems)
+    id_copies = chunk_copies(ids_in, ids, ids_sems)
+    for i, c in zip(id_copies, copies):
+        i.start()
+        c.start()
     blocks = accs[0].shape[0] // SUB
     masks = sublane_masks()
     zero = jnp.zeros((SUB * SUB, width), F32)
@@ -126,7 +159,7 @@
             for a, t in enumerate(tiles[first : first + n_acc]):
                 part = v[t : t + SUB]
                 for s in range(SUB):
-                    at = pl.ds(pl.multiple_of(ids[(t + s) * count + e] * SUB, SUB), SUB)
+                    at = pl.ds(pl.multiple_of(entry(ids, e * active, t + s), SUB), SUB)
                     batch.append((a, s, at, accs[a][at, :] + part))
             for a, s, at, value in batch:
                 pltpu.store(accs[a].at[at, :], value, mask=masks[s])
@@ -136,7 +169,11 @@
             example(g * unroll + u)
         return carry
 
-    lax.fori_loop(0, count // unroll, group, 0)
+    per = count // unroll // len(copies)
+    for i, (a, c) in enumerate(zip(id_copies, copies)):
+        a.wait()
+        c.wait()
+        lax.fori_loop(i * per, (i + 1) * per, group, 0)
 
     half = len(order) // 2
     for i, p in enumerate(order):
@@ -151,15 +188,16 @@
             out[pl.ds(pl.multiple_of(base + j * SUB, SUB), SUB), :] = jnp.sum(total, axis=1)
             return carry
 
-        lax.fori_loop(0, owned // SUB, fold, 0)
+        lax.fori_loop(0, owned // SUB, fold, 0, unroll=2)
     for out in outs:
         out[half * owned :, :] = gram[...]
 
 
-def dots_body(keep, recv, w, hist, grad, dots, gram):
+def dots_body(keep, recv, w, hist, result, grad, dots, gram):
     count, feats = hist.shape[1], hist.shape[2]
     rows, width = w.shape
     grad[...] = keep[:rows, :] + recv[:rows, :] + ridge * w[...]
+    result[...] = grad[...]
     gram[...] = keep[rows:, :] + recv[rows:, :]
 
     def step(j, accs):
@@ -263,6 +301,7 @@
     lines = count // width
     me = lax.axis_index("dp")
     w2 = weights.reshape(owned, width)
+    values = pltpu.with_memory_space_constraint(values, pltpu.HBM)
 
     pieces = [w2.astype(jnp.bfloat16)]
     order = [0]
@@ -274,13 +313,12 @@
     place = [0] * n_dp
     for at, p in enumerate(order):
         place[p] = at
-    ids_t = block_ids.T
-    owner = ids_t // owned
+    owner = block_ids // owned
     spot = owner ^ me
     where = jnp.zeros_like(spot)
     for p in range(n_dp):
         where = jnp.where(spot == p, place[p], where)
-    flat_ids = (where * owned + (ids_t - owner * owned)).reshape(-1)
+    flat_ids = (where * owned + (block_ids - owner * owned)).reshape(-1)
 
     gram = pl.pallas_call(
         gram_body,
@@ -290,13 +328,19 @@
         compiler_params=params(2 * mib(history) + 2),
     )(history)
 
+    streams = [
+        pltpu.VMEM(values.shape, values.dtype),
+        pltpu.SMEM((count * active,), jnp.int32),
+        pltpu.SemaphoreType.DMA((8,)),
+        pltpu.SemaphoreType.DMA((8,)),
+    ]
     table_mib = blocks * width * 4 / 2**20
     packed = pl.pallas_call(
         gather_body,
         out_shape=jax.ShapeDtypeStruct((lines + 2 * pairs, width), F32),
-        in_specs=[smem_spec(), vmem_spec(), vmem_spec()] + [vmem_spec()] * len(pieces),
+        in_specs=[any_spec(), hbm_spec(), vmem_spec()] + [vmem_spec()] * len(pieces),
         out_specs=vmem_spec(),
-        scratch_shapes=[pltpu.VMEM((blocks, width), F32), pltpu.VMEM((count, width), F32)],
+        scratch_shapes=[pltpu.VMEM((blocks, width), F32), pltpu.VMEM((count, width), F32)] + streams,
         compiler_params=params(mib(values) + 2 * table_mib + 6),
     )(flat_ids, values, gram, *pieces)
 
@@ -317,11 +361,11 @@
     send, keep = pl.pallas_call(
         functools.partial(scatter_body, order=slots, owned=owned),
         out_shape=[jax.ShapeDtypeStruct((half, width), F32)] * 2,
-        in_specs=[smem_spec(), smem_spec(), vmem_spec(), vmem_spec()],
+        in_specs=[any_spec(), smem_spec(), hbm_spec(), vmem_spec()],
         out_specs=[vmem_spec(), vmem_spec()],
-        scratch_shapes=[pltpu.VMEM((blocks * SUB, width), F32)] * n_acc,
+        scratch_shapes=[pltpu.VMEM((blocks * SUB, width), F32)] * n_acc + streams,
         compiler_params=params(mib(values) + table_mib + n_acc * acc_mib + 3),
-    )(flat_ids, resid, values, gram_rows)
+    )(flat_ids * SUB, resid, values, gram_rows)
 
     size = n_dp // 2
     tail = 2 * pairs
@@ -336,15 +380,16 @@
         send = jnp.concatenate([total[:cut], total_gram], axis=0)
         keep = jnp.concatenate([total[cut : 2 * cut], total_gram], axis=0)
 
-    grad, dots, gram_all = pl.pallas_call(
+    result, grad, dots, gram_all = pl.pallas_call(
         dots_body,
         out_shape=[
+            jax.ShapeDtypeStruct((owned, width), F32),
             jax.ShapeDtypeStruct((owned, width), F32),
             jax.ShapeDtypeStruct((2 * pairs, width), F32),
             jax.ShapeDtypeStruct((2 * pairs, width), F32),
         ],
         in_specs=[vmem_spec()] * 4,
-        out_specs=[vmem_spec()] * 3,
+        out_specs=[vmem_spec()] * 4,
         compiler_params=params(2 * mib(history) + 4),
     )(keep, came, w2, history)
 
@@ -369,7 +414,7 @@
         out_specs=vmem_spec(),
         compiler_params=params(2 * mib(history) + 4),
     )(steps, coef, dots, other, grad, w2, history)
-    return moved.reshape(-1), grad.reshape(-1)
+    return moved.reshape(-1), result.reshape(-1)
 
 
 def solution(mesh):

time: 152 us -> 118 us (0.78)
  Pallas kernels: 78.1 us -> 49.8 us
  local copies, waits for them, and re-layouts: 8.14 us -> 2.17 us
    pallas_call x1, Pallas kernels: 35.6 us -> 21.2 us  [local(): pl.pallas_call(gather_body, out_shape=jax.ShapeDtypeStruct((lines + 2 * p...]
    pallas_call x1, Pallas kernels: 36.3 us -> 22.5 us  [local(): pl.pallas_call(functools.partial(scatter_body, order=slots, owned=owned),...]
    unnamed x15 -> x8, local copies, waits for them, and re-layouts: 8.09 us -> 1.6 us
  transfers between devices with their start and end apart: 12 -> 12, of which waited for: 9 -> 10; matrix products, arithmetic and copies ran while one was open for 1% -> 1% of each run, Pallas kernels for 2% -> 3%
where the time goes in v2:
time: 118 us; the launch traced here: 117 us
  Pallas kernels  49.8 us (42%)
  waiting for transfers between devices  38.9 us (33%)
  starting transfers between devices  17.6 us (15%)
  blocking collectives  5.35 us (5%)
  local copies, waits for them, and re-layouts  2.17 us (2%)
  other arithmetic  2.11 us (2%)
  between operations  1.46 us (1%)
    ppermute x12, waiting for transfers between devices, xor_permute(): return lax.ppermute(x, axis, [(i, i ^ k) for i in range(n)])  38.9 us
    pallas_call x1, Pallas kernels, local(): pl.pallas_call(functools.partial(scatter_body, order=slots, owned=owned),...  22.5 us
    pallas_call x1, Pallas kernels, local(): pl.pallas_call(gather_body, out_shape=jax.ShapeDtypeStruct((lines + 2 * p...  21.2 us
    ppermute x12, starting transfers between devices, xor_permute(): return lax.ppermute(x, axis, [(i, i ^ k) for i in range(n)])  17.6 us
    all_gather x1, blocking collectives, local(): packed = jnp.sum(lax.all_gather(packed, 'mp', axis=0), axis=0)  5.35 us
    pallas_call x1, Pallas kernels, local(): pl.pallas_call(gram_body, out_shape=jax.ShapeDtypeStruct((2 * pairs, widt...  2.64 us
  transfers between devices with their start and end apart: 12, of which 10 were waited for; matrix products, arithmetic and copies ran while one was open for 1% of the time, Pallas kernels for 3%

profile of v2, /device:TPU:0, one launch (start us, length us, event | category | flops | bytes accessed | tf_op | source)
XLA Modules:
  0.0 117.4 jit_solution(6512332131790268913)
XLA Ops:
  0.6 0.0 copy-start.3
  0.6 0.9 bitcast_convert_fusion.refs_0_
  1.6 4.1 %collective-permute-start = (bf16[256,128]{1,0:T(8,128)(2,1)S(1)}, bf16[256,128]{1,0:T(8,128)(2,1)S(1)}, u32[]{:S(2)}, u32[]{:S(2)}) collective-permute-start(bf16[256,128]{1,0:T(8,128)(2,1)S(1)} %bitcast_convert_fusion.refs_0_), channel_id=1, source_target_pairs={{0,16},{4,20},{8,24},{12,28},{16,0},{20,4},{24,8},{28,12},{1,17},{... | collective-permute-start | bytes 196616 | tf_op jit(solution)/shard_map/ppermute | solution.py:292
  5.6 1.0 subtract_add_fusion
  6.6 0.2 copy.8
  6.8 0.3 reshape.23.ids_in
  7.2 2.1 %collective-permute-done.refs_1_ = bf16[256,128]{1,0:T(8,128)(2,1)S(1)} collective-permute-done((bf16[256,128]{1,0:T(8,128)(2,1)S(1)}, bf16[256,128]{1,0:T(8,128)(2,1)S(1)}, u32[]{:S(2)}, u32[]{:S(2)}) %collective-permute-start) | collective-permute-done | bytes 65568 | tf_op jit(solution)/shard_map/ppermute | solution.py:292
  9.3 1.8 %collective-permute-start.1 = (bf16[512,128]{1,0:T(8,128)(2,1)S(1)}, bf16[512,128]{1,0:T(8,128)(2,1)S(1)}, u32[]{:S(2)}, u32[]{:S(2)}) collective-permute-start(bf16[512,128]{1,0:T(8,128)(2,1)S(1)} %pad_maximum_fusion.2), channel_id=1, source_target_pairs={{0,4},{4,0},{8,12},{12,8},{16,20},{20,16},{24,28},{28,24},{1,5},{5... | collective-permute-start | bytes 393224 | tf_op jit(solution)/shard_map/ppermute | solution.py:292
  11.1 0.4 collective-permute-start.2
  11.4 1.4 %collective-permute-start.3 = (bf16[512,128]{1,0:T(8,128)(2,1)S(1)}, bf16[512,128]{1,0:T(8,128)(2,1)S(1)}, u32[]{:S(2)}, u32[]{:S(2)}) collective-permute-start(bf16[512,128]{1,0:T(8,128)(2,1)S(1)} %pad_maximum_fusion.2), channel_id=1, source_target_pairs={{0,12},{4,8},{8,4},{12,0},{16,28},{20,24},{24,20},{28,16},{1,13},{... | collective-permute-start | bytes 393224 | tf_op jit(solution)/shard_map/ppermute | solution.py:292
  12.8 0.0 copy-start
  12.9 1.6 %copy-done = f32[2,8,32768]{2,1,0:T(8,128)S(1)} copy-done((f32[2,8,32768]{2,1,0:T(8,128)S(1)}, f32[2,8,32768]{2,1,0:T(8,128)}, u32[]{:S(2)}) %copy-start) | copy-done | bytes 2097176
  14.4 2.6 %shard_map.77.gram = f32[16,128]{1,0:T(8,128)S(1)} custom-call(f32[2,8,32768]{2,1,0:T(8,128)S(1)} %copy-done), custom_call_target="tpu_custom_call" | custom-call | tf_op jit(solution)/shard_map/pallas_call | solution.py:323
  17.1 0.0 collective-permute-done.1.refs_2_
  17.1 0.0 collective-permute-done.2.refs_3_
  17.1 1.0 collective-permute-done.3.refs_4_
  18.1 21.2 %shard_map.78 = f32[24,128]{1,0:T(8,128)S(1)} custom-call(s32[24576]{0:T(1024)S(1)} %reshape.23.ids_in, bf16[1024,24,128]{2,1,0:T(8,128)(2,1)} %vals_in.3, f32[16,128]{1,0:T(8,128)S(1)} %shard_map.77.gram, bf16[256,128]{1,0:T(8,128)(2,1)S(1)} %bitcast_convert_fusion.refs_0_, bf16[256,128]{1,0:T(8,128)(2,1)S(1)} %collective-permute-done.refs_1_, ...), custom_call_target="tpu_custom_call" | custom-call | tf_op jit(solution)/shard_map/pallas_call | solution.py:338
  39.3 0.0 copy-start.1
  39.4 0.0 copy-start.2
  39.4 5.4 %all-gather = f32[96,128]{1,0:T(8,128)S(1)} all-gather(f32[24,128]{1,0:T(8,128)S(1)} %shard_map.78), channel_id=2, replica_groups=mesh['dp'=8,'mp'=4] {'mp'}, dimensions={0}, use_global_device_ids=true | all-gather | bytes 61440 | tf_op jit(solution)/shard_map/all_gather | solution.py:347
  44.7 0.0 copy-done.3
  44.8 22.5 %shard_map.79 = (f32[1040,128]{1,0:T(8,128)S(1)}, f32[1040,128]{1,0:T(8,128)S(1)}) custom-call(s32[24576]{0:T(1024)S(1)} %broadcast_multiply_fusion.ids_in, f32[1024]{0:T(1024)S(1)} %fusion.6.resid, bf16[1024,24,128]{2,1,0:T(8,128)(2,1)} %vals_in.3, f32[16,128]{1,0:T(8,128)S(1)} %slice.29.gram), custom_call_target="tpu_custom_call" | custom-call | tf_op jit(solution)/shard_map/pallas_call | solution.py:361
  67.2 0.9 collective-permute-start.4
  68.1 13.6 %collective-permute-done.4 = f32[1040,128]{1,0:T(8,128)S(1)} collective-permute-done((f32[1040,128]{1,0:T(8,128)S(1)}, f32[1040,128]{1,0:T(8,128)S(1)}, u32[]{:S(2)}, u32[]{:S(2)}) %collective-permute-start.4) | collective-permute-done | bytes 532512 | tf_op jit(solution)/shard_map/ppermute | solution.py:292
  81.6 0.1 add.28
  81.8 0.9 collective-permute-start.5
  82.7 7.0 %collective-permute-done.5 = f32[528,128]{1,0:T(8,128)S(1)} collective-permute-done((f32[528,128]{1,0:T(8,128)S(1)}, f32[528,128]{1,0:T(8,128)S(1)}, u32[]{:S(2)}, u32[]{:S(2)}) %collective-permute-start.5) | collective-permute-done | bytes 270368 | tf_op jit(solution)/shard_map/ppermute | solution.py:292
  89.8 2.6 %collective-permute-start.6 = (f32[272,128]{1,0:T(8,128)S(1)}, f32[272,128]{1,0:T(8,128)S(1)}, u32[]{:S(2)}, u32[]{:S(2)}) collective-permute-start(f32[272,128]{1,0:T(8,128)S(1)} %pad_maximum_fusion.1), channel_id=1, source_target_pairs={{0,16},{4,20},{8,24},{12,28},{16,0},{20,4},{24,8},{28,12},{1,17},{... | collective-permute-start | bytes 417800 | tf_op jit(solution)/shard_map/ppermute | solution.py:292
  92.5 5.5 %collective-permute-done.6.recv = f32[272,128]{1,0:T(8,128)S(1)} collective-permute-done((f32[272,128]{1,0:T(8,128)S(1)}, f32[272,128]{1,0:T(8,128)S(1)}, u32[]{:S(2)}, u32[]{:S(2)}) %collective-permute-start.6) | collective-permute-done | bytes 139296 | tf_op jit(solution)/shard_map/ppermute | solution.py:292
  98.0 0.0 copy-done.1
  98.0 0.0 copy-done.2
  98.0 1.2 %shard_map.80 = (f32[256,128]{1,0:T(8,128)}, f32[256,128]{1,0:T(8,128)S(1)}, f32[16,128]{1,0:T(8,128)S(1)}, f32[16,128]{1,0:T(8,128)S(1)}) custom-call(f32[272,128]{1,0:T(8,128)S(1)} %concatenate.21.keep, f32[272,128]{1,0:T(8,128)S(1)} %collective-permute-done.6.recv, f32[256,128]{1,0:T(8,128)S(1)} %bitcast.9, f32[2,8,32768]{2,1,0:T(8,128)S(1)} %copy-done.1), custom_call_target="tpu_custom_call" | custom-call | tf_op jit(solution)/shard_map/pallas_call | solution.py:383
  99.2 0.0 collective-permute-start.7
  99.2 1.2 collective-permute-done.7
  100.4 1.5 %collective-permute-start.8 = (f32[16,128]{1,0:T(8,128)S(1)}, f32[16,128]{1,0:T(8,128)S(1)}, u32[]{:S(2)}, u32[]{:S(2)}) collective-permute-start(f32[16,128]{1,0:T(8,128)S(1)} %add.30), channel_id=1, source_target_pairs={{0,2},{1,3},{2,0},{3,1},{4,6},{5,7},{6,4},{7,5},{8,10},{9,11},{10,... | collective-permute-start | bytes 24584 | tf_op jit(solution)/shard_map/ppermute | solution.py:292
  101.9 2.1 %collective-permute-done.8 = f32[16,128]{1,0:T(8,128)S(1)} collective-permute-done((f32[16,128]{1,0:T(8,128)S(1)}, f32[16,128]{1,0:T(8,128)S(1)}, u32[]{:S(2)}, u32[]{:S(2)}) %collective-permute-start.8) | collective-permute-done | bytes 8224 | tf_op jit(solution)/shard_map/ppermute | solution.py:292
  104.0 1.4 %collective-permute-start.9 = (f32[16,128]{1,0:T(8,128)S(1)}, f32[16,128]{1,0:T(8,128)S(1)}, u32[]{:S(2)}, u32[]{:S(2)}) collective-permute-start(f32[16,128]{1,0:T(8,128)S(1)} %add.31), channel_id=1, source_target_pairs={{0,4},{4,0},{8,12},{12,8},{16,20},{20,16},{24,28},{28,24},{1,5},{5... | collective-permute-start | bytes 24584 | tf_op jit(solution)/shard_map/ppermute | solution.py:292
  105.4 2.3 %collective-permute-done.9 = f32[16,128]{1,0:T(8,128)S(1)} collective-permute-done((f32[16,128]{1,0:T(8,128)S(1)}, f32[16,128]{1,0:T(8,128)S(1)}, u32[]{:S(2)}, u32[]{:S(2)}) %collective-permute-start.9) | collective-permute-done | bytes 8224 | tf_op jit(solution)/shard_map/ppermute | solution.py:292
  107.7 0.6 collective-permute-start.10
  108.3 3.0 %collective-permute-done.10 = f32[16,128]{1,0:T(8,128)S(1)} collective-permute-done((f32[16,128]{1,0:T(8,128)S(1)}, f32[16,128]{1,0:T(8,128)S(1)}, u32[]{:S(2)}, u32[]{:S(2)}) %collective-permute-start.10) | collective-permute-done | bytes 8224 | tf_op jit(solution)/shard_map/ppermute | solution.py:292
  111.3 2.0 %collective-permute-start.11 = (f32[16,128]{1,0:T(8,128)S(1)}, f32[16,128]{1,0:T(8,128)S(1)}, u32[]{:S(2)}, u32[]{:S(2)}) collective-permute-start(f32[16,128]{1,0:T(8,128)S(1)} %add.33.dots), channel_id=1, source_target_pairs={{0,16},{4,20},{8,24},{12,28},{16,0},{20,4},{24,8},{28,12},{1,17},{... | collective-permute-start | bytes 24584 | tf_op jit(solution)/shard_map/ppermute | solution.py:292
  114.0 0.8 shard_map.81.coef
  114.7 1.1 collective-permute-done.11.recv
  115.9 1.6 %shard_map.82 = f32[256,128]{1,0:T(8,128)} custom-call(f32[1]{0:T(128)S(6)} %copy.9.steps, f32[24,128]{1,0:T(8,128)S(1)} %shard_map.81.coef, f32[16,128]{1,0:T(8,128)S(1)} %add.33.dots, f32[16,128]{1,0:T(8,128)S(1)} %collective-permute-done.11.recv, f32[256,128]{1,0:T(8,128)S(1)} %get-tuple-element.12.grad, f32[256,128]{1,0:T(8,128)S(1)} %bitcast.10, ...), custom_call_target="tpu_custom_call" | custom-call | tf_op jit(solution)/shard_map/pallas_call | solution.py:410
  (17 shorter events, 0.2 us)
Async XLA Ops:
  0.6 44.1 %copy-start.3 = (s32[1024]{0:T(1024)S(1)}, s32[1024]{0:T(1024)}, u32[]{:S(2)}) copy-start(s32[1024]{0:T(1024)} %param.8) | copy-start | bytes 12292
  1.6 7.7 %collective-permute-start = (bf16[256,128]{1,0:T(8,128)(2,1)S(1)}, bf16[256,128]{1,0:T(8,128)(2,1)S(1)}, u32[]{:S(2)}, u32[]{:S(2)}) collective-permute-start(bf16[256,128]{1,0:T(8,128)(2,1)S(1)} %bitcast_convert_fusion.refs_0_), channel_id=1, source_target_pairs={{0,16},{4,20},{8,24},{12,28},{16,0},{20,4},{24,8},{28,12},{1,17},{... | collective-permute-start | bytes 196616 | tf_op jit(solution)/shard_map/ppermute | solution.py:292
  9.3 7.8 %collective-permute-start.1 = (bf16[512,128]{1,0:T(8,128)(2,1)S(1)}, bf16[512,128]{1,0:T(8,128)(2,1)S(1)}, u32[]{:S(2)}, u32[]{:S(2)}) collective-permute-start(bf16[512,128]{1,0:T(8,128)(2,1)S(1)} %pad_maximum_fusion.2), channel_id=1, source_target_pairs={{0,4},{4,0},{8,12},{12,8},{16,20},{20,16},{24,28},{28,24},{1,5},{5... | collective-permute-start | bytes 393224 | tf_op jit(solution)/shard_map/ppermute | solution.py:292
  11.1 6.1 %collective-permute-start.2 = (bf16[512,128]{1,0:T(8,128)(2,1)S(1)}, bf16[512,128]{1,0:T(8,128)(2,1)S(1)}, u32[]{:S(2)}, u32[]{:S(2)}) collective-permute-start(bf16[512,128]{1,0:T(8,128)(2,1)S(1)} %pad_maximum_fusion.2), channel_id=1, source_target_pairs={{0,8},{4,12},{8,0},{12,4},{16,24},{20,28},{24,16},{28,20},{1,9},{5... | collective-permute-start | bytes 393224 | tf_op jit(solution)/shard_map/ppermute | solution.py:292
  11.4 6.7 %collective-permute-start.3 = (bf16[512,128]{1,0:T(8,128)(2,1)S(1)}, bf16[512,128]{1,0:T(8,128)(2,1)S(1)}, u32[]{:S(2)}, u32[]{:S(2)}) collective-permute-start(bf16[512,128]{1,0:T(8,128)(2,1)S(1)} %pad_maximum_fusion.2), channel_id=1, source_target_pairs={{0,12},{4,8},{8,4},{12,0},{16,28},{20,24},{24,20},{28,16},{1,13},{... | collective-permute-start | bytes 393224 | tf_op jit(solution)/shard_map/ppermute | solution.py:292
  12.8 1.6 %copy-start = (f32[2,8,32768]{2,1,0:T(8,128)S(1)}, f32[2,8,32768]{2,1,0:T(8,128)}, u32[]{:S(2)}) copy-start(f32[2,8,32768]{2,1,0:T(8,128)} %hist.5) | copy-start | bytes 6291460
  39.3 58.6 %copy-start.1 = (f32[2,8,32768]{2,1,0:T(8,128)S(1)}, f32[2,8,32768]{2,1,0:T(8,128)}, u32[]{:S(2)}) copy-start(f32[2,8,32768]{2,1,0:T(8,128)} %hist.5) | copy-start | bytes 6291460
  39.4 58.6 %copy-start.2 = (f32[32768]{0:T(1024)S(1)}, f32[32768]{0:T(1024)}, u32[]{:S(2)}) copy-start(f32[32768]{0:T(1024)} %param.9) | copy-start | bytes 393220
  67.2 14.4 %collective-permute-start.4 = (f32[1040,128]{1,0:T(8,128)S(1)}, f32[1040,128]{1,0:T(8,128)S(1)}, u32[]{:S(2)}, u32[]{:S(2)}) collective-permute-start(f32[1040,128]{1,0:T(8,128)S(1)} %get-tuple-element.9), channel_id=1, source_target_pairs={{0,4},{4,0},{8,12},{12,8},{16,20},{20,16},{24,28},{28,24},{1,5},{5... | collective-permute-start | bytes 1597448 | tf_op jit(solution)/shard_map/ppermute | solution.py:292
  81.8 7.9 %collective-permute-start.5 = (f32[528,128]{1,0:T(8,128)S(1)}, f32[528,128]{1,0:T(8,128)S(1)}, u32[]{:S(2)}, u32[]{:S(2)}) collective-permute-start(f32[528,128]{1,0:T(8,128)S(1)} %pad_maximum_fusion), channel_id=1, source_target_pairs={{0,8},{4,12},{8,0},{12,4},{16,24},{20,28},{24,16},{28,20},{1,9},{5... | collective-permute-start | bytes 811016 | tf_op jit(solution)/shard_map/ppermute | solution.py:292
  89.8 8.2 %collective-permute-start.6 = (f32[272,128]{1,0:T(8,128)S(1)}, f32[272,128]{1,0:T(8,128)S(1)}, u32[]{:S(2)}, u32[]{:S(2)}) collective-permute-start(f32[272,128]{1,0:T(8,128)S(1)} %pad_maximum_fusion.1), channel_id=1, source_target_pairs={{0,16},{4,20},{8,24},{12,28},{16,0},{20,4},{24,8},{28,12},{1,17},{... | collective-permute-start | bytes 417800 | tf_op jit(solution)/shard_map/ppermute | solution.py:292
  99.2 1.2 collective-permute-start.7
  100.4 3.7 %collective-permute-start.8 = (f32[16,128]{1,0:T(8,128)S(1)}, f32[16,128]{1,0:T(8,128)S(1)}, u32[]{:S(2)}, u32[]{:S(2)}) collective-permute-start(f32[16,128]{1,0:T(8,128)S(1)} %add.30), channel_id=1, source_target_pairs={{0,2},{1,3},{2,0},{3,1},{4,6},{5,7},{6,4},{7,5},{8,10},{9,11},{10,... | collective-permute-start | bytes 24584 | tf_op jit(solution)/shard_map/ppermute | solution.py:292
  104.0 3.7 %collective-permute-start.9 = (f32[16,128]{1,0:T(8,128)S(1)}, f32[16,128]{1,0:T(8,128)S(1)}, u32[]{:S(2)}, u32[]{:S(2)}) collective-permute-start(f32[16,128]{1,0:T(8,128)S(1)} %add.31), channel_id=1, source_target_pairs={{0,4},{4,0},{8,12},{12,8},{16,20},{20,16},{24,28},{28,24},{1,5},{5... | collective-permute-start | bytes 24584 | tf_op jit(solution)/shard_map/ppermute | solution.py:292
  107.7 3.7 %collective-permute-start.10 = (f32[16,128]{1,0:T(8,128)S(1)}, f32[16,128]{1,0:T(8,128)S(1)}, u32[]{:S(2)}, u32[]{:S(2)}) collective-permute-start(f32[16,128]{1,0:T(8,128)S(1)} %add.32), channel_id=1, source_target_pairs={{0,8},{4,12},{8,0},{12,4},{16,24},{20,28},{24,16},{28,20},{1,9},{5... | collective-permute-start | bytes 24584 | tf_op jit(solution)/shard_map/ppermute | solution.py:292
  111.3 4.5 %collective-permute-start.11 = (f32[16,128]{1,0:T(8,128)S(1)}, f32[16,128]{1,0:T(8,128)S(1)}, u32[]{:S(2)}, u32[]{:S(2)}) collective-permute-start(f32[16,128]{1,0:T(8,128)S(1)} %add.33.dots), channel_id=1, source_target_pairs={{0,16},{4,20},{8,24},{12,28},{16,0},{20,4},{24,8},{28,12},{1,17},{... | collective-permute-start | bytes 24584 | tf_op jit(solution)/shard_map/ppermute | solution.py:292

commit v3 on v2

--- a/solution.py
+++ b/solution.py
@@ -9,6 +9,7 @@
 
 ridge = 0.2
 SUB = 8
+MAX_ACC = 3
 F32 = jnp.float32
 
 
@@ -68,20 +69,60 @@
         out[part * count : (part + 1) * count, :] = tile
 
 
-def chunk_copies(src, dst, sems):
-    n = sems.shape[0]
-    size = src.shape[0] // n
-    return [pltpu.make_async_copy(src.at[pl.ds(c * size, size)], dst.at[pl.ds(c * size, size)], sems.at[c]) for c in range(n)]
+def chunk_copies(srcs, dsts, sems, c):
+    n = sems.shape[1]
+    copies = []
+    for i, (src, dst) in enumerate(zip(srcs, dsts)):
+        size = src.shape[0] // n
+        at = pl.ds(c * size, size)
+        copies.append(pltpu.make_async_copy(src.at[at], dst.at[at], sems.at[i, c]))
+    return copies
+
+
+def start_chunks(srcs, dsts, sems):
+    for c in range(sems.shape[1]):
+        for copy in chunk_copies(srcs, dsts, sems, c):
+            copy.start()
+
+
+def run_chunks(srcs, dsts, sems, trips, body):
+    per = trips // sems.shape[1]
+
+    def chunk(c, carry):
+        for copy in chunk_copies(srcs, dsts, sems, c):
+            copy.wait()
+        return lax.fori_loop(c * per, (c + 1) * per, body, carry)
+
+    lax.fori_loop(0, sems.shape[1], chunk, 0)
+
+
+def fold_tiles(tiles):
+    sub = lax.broadcasted_iota(jnp.int32, tiles[0].shape, 0)
+    half = SUB // 2
+    low = (sub & half) == 0
+    tiles = [
+        jnp.where(low, tiles[k], tiles[k + half]) + pltpu.roll(jnp.where(low, tiles[k + half], tiles[k]), half, 0)
+        for k in range(half)
+    ]
+    while half > 1:
+        half //= 2
+        odd = (sub & half) != 0
+        tiles = [
+            jnp.where(
+                odd,
+                tiles[k + half] + pltpu.roll(tiles[k + half], half, 0),
+                tiles[k] + pltpu.roll(tiles[k], SUB - half, 0),
+            )
+            for k in range(half)
+        ]
+    return tiles[0]
 
 
 def gather_body(ids_in, vals_in, gram, *refs):
-    *pieces, out, table, rows, vals, ids, vals_sems, ids_sems = refs
+    *pieces, out, table, rows, vals, ids, sems = refs
+    srcs, dsts = (ids_in, vals_in), (ids, vals)
     count, active, width = vals.shape
-    copies = chunk_copies(vals_in, vals, vals_sems)
-    id_copies = chunk_copies(ids_in, ids, ids_sems)
-    for i, c in zip(id_copies, copies):
-        i.start()
-        c.start()
+    start_chunks(srcs, dsts, sems)
     at = 0
     for piece in pieces:
         size = piece.shape[0]
@@ -97,7 +138,6 @@
     masks = sublane_masks()
 
     def group(g, carry):
-        tile = jnp.zeros((SUB, width), F32)
         for u in range(SUB):
             e = g * SUB + u
             v = vals[e].astype(F32)
@@ -109,16 +149,10 @@
                     pick = row if pick is None else jnp.where(masks[s], row, pick)
                 prod = pick * v[t : t + SUB]
                 total = prod if total is None else total + prod
-            total = jnp.sum(total, axis=0, keepdims=True)
-            tile = jnp.where(masks[u], jnp.broadcast_to(total, (SUB, width)), tile)
-        rows[pl.ds(pl.multiple_of(g * SUB, SUB), SUB), :] = tile
+            rows[pl.ds(e, 1), :] = jnp.sum(total, axis=0, keepdims=True)
         return carry
 
-    per = count // SUB // len(copies)
-    for i, (a, c) in enumerate(zip(id_copies, copies)):
-        a.wait()
-        c.wait()
-        lax.fori_loop(i * per, (i + 1) * per, group, 0)
+    run_chunks(srcs, dsts, sems, count // SUB, group)
     lines = count // width
     for b in range(lines):
         flipped = rows[b * width : (b + 1) * width, :].T
@@ -128,14 +162,11 @@
 
 def scatter_body(ids_in, resid, vals_in, gram, *refs, order, owned):
     n_out = 2
-    outs, accs = refs[:n_out], refs[n_out:-4]
-    vals, ids, vals_sems, ids_sems = refs[-4:]
+    outs, accs = refs[:n_out], refs[n_out:-3]
+    vals, ids, sems = refs[-3:]
+    srcs, dsts = (ids_in, vals_in), (ids, vals)
     count, active, width = vals.shape
-    copies = chunk_copies(vals_in, vals, vals_sems)
-    id_copies = chunk_copies(ids_in, ids, ids_sems)
-    for i, c in zip(id_copies, copies):
-        i.start()
-        c.start()
+    start_chunks(srcs, dsts, sems)
     blocks = accs[0].shape[0] // SUB
     masks = sublane_masks()
     zero = jnp.zeros((SUB * SUB, width), F32)
@@ -147,45 +178,39 @@
         return carry
 
     lax.fori_loop(0, blocks // SUB, clear, 0)
-    n_acc = len(accs)
-    unroll = 4
-
-    def example(e):
-        r = resid[e]
-        v = vals[e].astype(F32) * r
-        tiles = list(range(0, active, SUB))
-        for first in range(0, len(tiles), n_acc):
-            batch = []
-            for a, t in enumerate(tiles[first : first + n_acc]):
-                part = v[t : t + SUB]
+    unroll = 8
+
+    def group(g, carry):
+        turn = 0
+        for u in range(unroll):
+            e = g * unroll + u
+            v = vals[e].astype(F32) * resid[e]
+            for t in range(0, active, SUB):
+                acc = accs[turn % len(accs)]
+                turn += 1
+                batch = []
                 for s in range(SUB):
                     at = pl.ds(pl.multiple_of(entry(ids, e * active, t + s), SUB), SUB)
-                    batch.append((a, s, at, accs[a][at, :] + part))
-            for a, s, at, value in batch:
-                pltpu.store(accs[a].at[at, :], value, mask=masks[s])
-
-    def group(g, carry):
-        for u in range(unroll):
-            example(g * unroll + u)
+                    batch.append((at, acc[at, :] + v[t : t + SUB]))
+                for s, (at, value) in enumerate(batch):
+                    pltpu.store(acc.at[at, :], value, mask=masks[s])
         return carry
 
-    per = count // unroll // len(copies)
-    for i, (a, c) in enumerate(zip(id_copies, copies)):
-        a.wait()
-        c.wait()
-        lax.fori_loop(i * per, (i + 1) * per, group, 0)
+    run_chunks(srcs, dsts, sems, count // unroll, group)
 
     half = len(order) // 2
     for i, p in enumerate(order):
         out = outs[0] if i < half else outs[1]
 
         def fold(j, carry, p=p, out=out, base=(i % half) * owned):
-            total = None
-            at = pl.ds(pl.multiple_of((p * owned + j * SUB) * SUB, SUB * SUB), SUB * SUB)
-            for acc in accs:
-                x = acc[at, :].reshape(SUB, SUB, width)
-                total = x if total is None else total + x
-            out[pl.ds(pl.multiple_of(base + j * SUB, SUB), SUB), :] = jnp.sum(total, axis=1)
+            tiles = []
+            for i in range(SUB):
+                at = pl.ds(pl.multiple_of((p * owned + j * SUB + i) * SUB, SUB), SUB)
+                total = accs[0][at, :]
+                for acc in accs[1:]:
+                    total = total + acc[at, :]
+                tiles.append(total)
+            out[pl.ds(pl.multiple_of(base + j * SUB, SUB), SUB), :] = fold_tiles(tiles)
             return carry
 
         lax.fori_loop(0, owned // SUB, fold, 0, unroll=2)
@@ -331,8 +356,7 @@
     streams = [
         pltpu.VMEM(values.shape, values.dtype),
         pltpu.SMEM((count * active,), jnp.int32),
-        pltpu.SemaphoreType.DMA((8,)),
-        pltpu.SemaphoreType.DMA((8,)),
+        pltpu.SemaphoreType.DMA((2, 8)),
     ]
     table_mib = blocks * width * 4 / 2**20
     packed = pl.pallas_call(
@@ -356,7 +380,7 @@
 
     acc_mib = SUB * table_mib
     room = (60 * 1024) / 1024 - mib(values) - table_mib - 6
-    n_acc = max(1, min(active // SUB, int(room // acc_mib)))
+    n_acc = max(1, min(MAX_ACC, int(room // acc_mib)))
     half = n_dp // 2 * owned + 2 * pairs
     send, keep = pl.pallas_call(
         functools.partial(scatter_body, order=slots, owned=owned),

time: 118 us -> 112 us (0.949)
  Pallas kernels: 49.8 us -> 44.7 us
    pallas_call x1, Pallas kernels: 21.2 us -> 17 us  [local(): pl.pallas_call(gather_body, out_shape=jax.ShapeDtypeStruct((lines + 2 * p...]
where the time goes in v3:
time: 112 us
  Pallas kernels  44.7 us (40%)
  waiting for transfers between devices  38.9 us (35%)
  starting transfers between devices  17.6 us (16%)
  blocking collectives  5.35 us (5%)
  local copies, waits for them, and re-layouts  2.17 us (2%)
  other arithmetic  2.11 us (2%)
  between operations  1.46 us (1%)
    ppermute x12, waiting for transfers between devices, xor_permute(): return lax.ppermute(x, axis, [(i, i ^ k) for i in range(n)])  38.9 us
    pallas_call x1, Pallas kernels, local(): pl.pallas_call(functools.partial(scatter_body, order=slots, owned=owned),...  21.5 us
    ppermute x12, starting transfers between devices, xor_permute(): return lax.ppermute(x, axis, [(i, i ^ k) for i in range(n)])  17.6 us
    pallas_call x1, Pallas kernels, local(): pl.pallas_call(gather_body, out_shape=jax.ShapeDtypeStruct((lines + 2 * p...  17 us
    all_gather x1, blocking collectives, local(): packed = jnp.sum(lax.all_gather(packed, 'mp', axis=0), axis=0)  5.35 us
    pallas_call x1, Pallas kernels, local(): pl.pallas_call(gram_body, out_shape=jax.ShapeDtypeStruct((2 * pairs, widt...  2.64 us
  transfers between devices with their start and end apart: 12, of which 10 were waited for; matrix products, arithmetic and copies ran while one was open for 1% of the time, Pallas kernels for 3%

profile of v3, /device:TPU:0, one launch (start us, length us, event | category | flops | bytes accessed | tf_op | source)
XLA Modules:
  0.0 112.2 jit_solution(13571196925291657661)
XLA Ops:
  0.6 0.0 copy-start.3
  0.6 0.9 bitcast_convert_fusion.refs_0_
  1.6 4.1 %collective-permute-start = (bf16[256,128]{1,0:T(8,128)(2,1)S(1)}, bf16[256,128]{1,0:T(8,128)(2,1)S(1)}, u32[]{:S(2)}, u32[]{:S(2)}) collective-permute-start(bf16[256,128]{1,0:T(8,128)(2,1)S(1)} %bitcast_convert_fusion.refs_0_), channel_id=1, source_target_pairs={{0,16},{4,20},{8,24},{12,28},{16,0},{20,4},{24,8},{28,12},{1,17},{... | collective-permute-start | bytes 196616 | tf_op jit(solution)/shard_map/ppermute | solution.py:317
  5.6 1.0 subtract_add_fusion
  6.6 0.2 copy.8
  6.8 0.3 reshape.23.ids_in
  7.2 2.1 %collective-permute-done.refs_1_ = bf16[256,128]{1,0:T(8,128)(2,1)S(1)} collective-permute-done((bf16[256,128]{1,0:T(8,128)(2,1)S(1)}, bf16[256,128]{1,0:T(8,128)(2,1)S(1)}, u32[]{:S(2)}, u32[]{:S(2)}) %collective-permute-start) | collective-permute-done | bytes 65568 | tf_op jit(solution)/shard_map/ppermute | solution.py:317
  9.3 1.8 %collective-permute-start.1 = (bf16[512,128]{1,0:T(8,128)(2,1)S(1)}, bf16[512,128]{1,0:T(8,128)(2,1)S(1)}, u32[]{:S(2)}, u32[]{:S(2)}) collective-permute-start(bf16[512,128]{1,0:T(8,128)(2,1)S(1)} %pad_maximum_fusion.2), channel_id=1, source_target_pairs={{0,4},{4,0},{8,12},{12,8},{16,20},{20,16},{24,28},{28,24},{1,5},{5... | collective-permute-start | bytes 393224 | tf_op jit(solution)/shard_map/ppermute | solution.py:317
  11.1 0.4 collective-permute-start.2
  11.4 1.4 %collective-permute-start.3 = (bf16[512,128]{1,0:T(8,128)(2,1)S(1)}, bf16[512,128]{1,0:T(8,128)(2,1)S(1)}, u32[]{:S(2)}, u32[]{:S(2)}) collective-permute-start(bf16[512,128]{1,0:T(8,128)(2,1)S(1)} %pad_maximum_fusion.2), channel_id=1, source_target_pairs={{0,12},{4,8},{8,4},{12,0},{16,28},{20,24},{24,20},{28,16},{1,13},{... | collective-permute-start | bytes 393224 | tf_op jit(solution)/shard_map/ppermute | solution.py:317
  12.8 0.0 copy-start
  12.9 1.6 %copy-done = f32[2,8,32768]{2,1,0:T(8,128)S(1)} copy-done((f32[2,8,32768]{2,1,0:T(8,128)S(1)}, f32[2,8,32768]{2,1,0:T(8,128)}, u32[]{:S(2)}) %copy-start) | copy-done | bytes 2097176
  14.4 2.6 %shard_map.77.gram = f32[16,128]{1,0:T(8,128)S(1)} custom-call(f32[2,8,32768]{2,1,0:T(8,128)S(1)} %copy-done), custom_call_target="tpu_custom_call" | custom-call | tf_op jit(solution)/shard_map/pallas_call | solution.py:348
  17.1 0.0 collective-permute-done.1.refs_2_
  17.1 0.0 collective-permute-done.2.refs_3_
  17.1 1.0 collective-permute-done.3.refs_4_
  18.1 17.0 %shard_map.78 = f32[24,128]{1,0:T(8,128)S(1)} custom-call(s32[24576]{0:T(1024)S(1)} %reshape.23.ids_in, bf16[1024,24,128]{2,1,0:T(8,128)(2,1)} %vals_in.3, f32[16,128]{1,0:T(8,128)S(1)} %shard_map.77.gram, bf16[256,128]{1,0:T(8,128)(2,1)S(1)} %bitcast_convert_fusion.refs_0_, bf16[256,128]{1,0:T(8,128)(2,1)S(1)} %collective-permute-done.refs_1_, ...), custom_call_target="tpu_custom_call" | custom-call | tf_op jit(solution)/shard_map/pallas_call | solution.py:362
  35.1 0.0 copy-start.1
  35.1 0.0 copy-start.2
  35.1 5.4 %all-gather = f32[96,128]{1,0:T(8,128)S(1)} all-gather(f32[24,128]{1,0:T(8,128)S(1)} %shard_map.78), channel_id=2, replica_groups=mesh['dp'=8,'mp'=4] {'mp'}, dimensions={0}, use_global_device_ids=true | all-gather | bytes 61440 | tf_op jit(solution)/shard_map/all_gather | solution.py:371
  40.5 0.0 copy-done.3
  40.5 21.5 %shard_map.79 = (f32[1040,128]{1,0:T(8,128)S(1)}, f32[1040,128]{1,0:T(8,128)S(1)}) custom-call(s32[24576]{0:T(1024)S(1)} %broadcast_multiply_fusion.ids_in, f32[1024]{0:T(1024)S(1)} %fusion.6.resid, bf16[1024,24,128]{2,1,0:T(8,128)(2,1)} %vals_in.3, f32[16,128]{1,0:T(8,128)S(1)} %slice.29.gram), custom_call_target="tpu_custom_call" | custom-call | tf_op jit(solution)/shard_map/pallas_call | solution.py:385
  62.0 0.9 collective-permute-start.4
  62.9 13.6 %collective-permute-done.4 = f32[1040,128]{1,0:T(8,128)S(1)} collective-permute-done((f32[1040,128]{1,0:T(8,128)S(1)}, f32[1040,128]{1,0:T(8,128)S(1)}, u32[]{:S(2)}, u32[]{:S(2)}) %collective-permute-start.4) | collective-permute-done | bytes 532512 | tf_op jit(solution)/shard_map/ppermute | solution.py:317
  76.4 0.1 add.28
  76.6 0.9 collective-permute-start.5
  77.5 7.0 %collective-permute-done.5 = f32[528,128]{1,0:T(8,128)S(1)} collective-permute-done((f32[528,128]{1,0:T(8,128)S(1)}, f32[528,128]{1,0:T(8,128)S(1)}, u32[]{:S(2)}, u32[]{:S(2)}) %collective-permute-start.5) | collective-permute-done | bytes 270368 | tf_op jit(solution)/shard_map/ppermute | solution.py:317
  84.6 2.6 %collective-permute-start.6 = (f32[272,128]{1,0:T(8,128)S(1)}, f32[272,128]{1,0:T(8,128)S(1)}, u32[]{:S(2)}, u32[]{:S(2)}) collective-permute-start(f32[272,128]{1,0:T(8,128)S(1)} %pad_maximum_fusion.1), channel_id=1, source_target_pairs={{0,16},{4,20},{8,24},{12,28},{16,0},{20,4},{24,8},{28,12},{1,17},{... | collective-permute-start | bytes 417800 | tf_op jit(solution)/shard_map/ppermute | solution.py:317
  87.3 5.5 %collective-permute-done.6.recv = f32[272,128]{1,0:T(8,128)S(1)} collective-permute-done((f32[272,128]{1,0:T(8,128)S(1)}, f32[272,128]{1,0:T(8,128)S(1)}, u32[]{:S(2)}, u32[]{:S(2)}) %collective-permute-start.6) | collective-permute-done | bytes 139296 | tf_op jit(solution)/shard_map/ppermute | solution.py:317
  92.8 0.0 copy-done.1
  92.8 0.0 copy-done.2
  92.8 1.2 %shard_map.80 = (f32[256,128]{1,0:T(8,128)}, f32[256,128]{1,0:T(8,128)S(1)}, f32[16,128]{1,0:T(8,128)S(1)}, f32[16,128]{1,0:T(8,128)S(1)}) custom-call(f32[272,128]{1,0:T(8,128)S(1)} %concatenate.21.keep, f32[272,128]{1,0:T(8,128)S(1)} %collective-permute-done.6.recv, f32[256,128]{1,0:T(8,128)S(1)} %bitcast.9, f32[2,8,32768]{2,1,0:T(8,128)S(1)} %copy-done.1), custom_call_target="tpu_custom_call" | custom-call | tf_op jit(solution)/shard_map/pallas_call | solution.py:407
  94.0 0.0 collective-permute-start.7
  94.0 1.2 %collective-permute-done.7 = f32[16,128]{1,0:T(8,128)S(1)} collective-permute-done((f32[16,128]{1,0:T(8,128)S(1)}, f32[16,128]{1,0:T(8,128)S(1)}, u32[]{:S(2)}, u32[]{:S(2)}) %collective-permute-start.7) | collective-permute-done | bytes 8224 | tf_op jit(solution)/shard_map/ppermute | solution.py:317
  95.2 1.5 %collective-permute-start.8 = (f32[16,128]{1,0:T(8,128)S(1)}, f32[16,128]{1,0:T(8,128)S(1)}, u32[]{:S(2)}, u32[]{:S(2)}) collective-permute-start(f32[16,128]{1,0:T(8,128)S(1)} %add.30), channel_id=1, source_target_pairs={{0,2},{1,3},{2,0},{3,1},{4,6},{5,7},{6,4},{7,5},{8,10},{9,11},{10,... | collective-permute-start | bytes 24584 | tf_op jit(solution)/shard_map/ppermute | solution.py:317
  96.7 2.1 %collective-permute-done.8 = f32[16,128]{1,0:T(8,128)S(1)} collective-permute-done((f32[16,128]{1,0:T(8,128)S(1)}, f32[16,128]{1,0:T(8,128)S(1)}, u32[]{:S(2)}, u32[]{:S(2)}) %collective-permute-start.8) | collective-permute-done | bytes 8224 | tf_op jit(solution)/shard_map/ppermute | solution.py:317
  98.8 1.4 %collective-permute-start.9 = (f32[16,128]{1,0:T(8,128)S(1)}, f32[16,128]{1,0:T(8,128)S(1)}, u32[]{:S(2)}, u32[]{:S(2)}) collective-permute-start(f32[16,128]{1,0:T(8,128)S(1)} %add.31), channel_id=1, source_target_pairs={{0,4},{4,0},{8,12},{12,8},{16,20},{20,16},{24,28},{28,24},{1,5},{5... | collective-permute-start | bytes 24584 | tf_op jit(solution)/shard_map/ppermute | solution.py:317
  100.2 2.3 %collective-permute-done.9 = f32[16,128]{1,0:T(8,128)S(1)} collective-permute-done((f32[16,128]{1,0:T(8,128)S(1)}, f32[16,128]{1,0:T(8,128)S(1)}, u32[]{:S(2)}, u32[]{:S(2)}) %collective-permute-start.9) | collective-permute-done | bytes 8224 | tf_op jit(solution)/shard_map/ppermute | solution.py:317
  102.5 0.6 collective-permute-start.10
  103.1 3.0 %collective-permute-done.10 = f32[16,128]{1,0:T(8,128)S(1)} collective-permute-done((f32[16,128]{1,0:T(8,128)S(1)}, f32[16,128]{1,0:T(8,128)S(1)}, u32[]{:S(2)}, u32[]{:S(2)}) %collective-permute-start.10) | collective-permute-done | bytes 8224 | tf_op jit(solution)/shard_map/ppermute | solution.py:317
  106.1 2.0 %collective-permute-start.11 = (f32[16,128]{1,0:T(8,128)S(1)}, f32[16,128]{1,0:T(8,128)S(1)}, u32[]{:S(2)}, u32[]{:S(2)}) collective-permute-start(f32[16,128]{1,0:T(8,128)S(1)} %add.33.dots), channel_id=1, source_target_pairs={{0,16},{4,20},{8,24},{12,28},{16,0},{20,4},{24,8},{28,12},{1,17},{... | collective-permute-start | bytes 24584 | tf_op jit(solution)/shard_map/ppermute | solution.py:317
  108.8 0.8 shard_map.81.coef
  109.6 1.1 %collective-permute-done.11.recv = f32[16,128]{1,0:T(8,128)S(1)} collective-permute-done((f32[16,128]{1,0:T(8,128)S(1)}, f32[16,128]{1,0:T(8,128)S(1)}, u32[]{:S(2)}, u32[]{:S(2)}) %collective-permute-start.11) | collective-permute-done | bytes 8224 | tf_op jit(solution)/shard_map/ppermute | solution.py:317
  110.7 1.6 %shard_map.82 = f32[256,128]{1,0:T(8,128)} custom-call(f32[1]{0:T(128)S(6)} %copy.9.steps, f32[24,128]{1,0:T(8,128)S(1)} %shard_map.81.coef, f32[16,128]{1,0:T(8,128)S(1)} %add.33.dots, f32[16,128]{1,0:T(8,128)S(1)} %collective-permute-done.11.recv, f32[256,128]{1,0:T(8,128)S(1)} %get-tuple-element.12.grad, f32[256,128]{1,0:T(8,128)S(1)} %bitcast.10, ...), custom_call_target="tpu_custom_call" | custom-call | tf_op jit(solution)/shard_map/pallas_call | solution.py:434
  (17 shorter events, 0.2 us)
Async XLA Ops:
  0.6 39.8 %copy-start.3 = (s32[1024]{0:T(1024)S(1)}, s32[1024]{0:T(1024)}, u32[]{:S(2)}) copy-start(s32[1024]{0:T(1024)} %param.8) | copy-start | bytes 12292
  1.6 7.7 %collective-permute-start = (bf16[256,128]{1,0:T(8,128)(2,1)S(1)}, bf16[256,128]{1,0:T(8,128)(2,1)S(1)}, u32[]{:S(2)}, u32[]{:S(2)}) collective-permute-start(bf16[256,128]{1,0:T(8,128)(2,1)S(1)} %bitcast_convert_fusion.refs_0_), channel_id=1, source_target_pairs={{0,16},{4,20},{8,24},{12,28},{16,0},{20,4},{24,8},{28,12},{1,17},{... | collective-permute-start | bytes 196616 | tf_op jit(solution)/shard_map/ppermute | solution.py:317
  9.3 7.8 %collective-permute-start.1 = (bf16[512,128]{1,0:T(8,128)(2,1)S(1)}, bf16[512,128]{1,0:T(8,128)(2,1)S(1)}, u32[]{:S(2)}, u32[]{:S(2)}) collective-permute-start(bf16[512,128]{1,0:T(8,128)(2,1)S(1)} %pad_maximum_fusion.2), channel_id=1, source_target_pairs={{0,4},{4,0},{8,12},{12,8},{16,20},{20,16},{24,28},{28,24},{1,5},{5... | collective-permute-start | bytes 393224 | tf_op jit(solution)/shard_map/ppermute | solution.py:317
  11.1 6.1 %collective-permute-start.2 = (bf16[512,128]{1,0:T(8,128)(2,1)S(1)}, bf16[512,128]{1,0:T(8,128)(2,1)S(1)}, u32[]{:S(2)}, u32[]{:S(2)}) collective-permute-start(bf16[512,128]{1,0:T(8,128)(2,1)S(1)} %pad_maximum_fusion.2), channel_id=1, source_target_pairs={{0,8},{4,12},{8,0},{12,4},{16,24},{20,28},{24,16},{28,20},{1,9},{5... | collective-permute-start | bytes 393224 | tf_op jit(solution)/shard_map/ppermute | solution.py:317
  11.4 6.7 %collective-permute-start.3 = (bf16[512,128]{1,0:T(8,128)(2,1)S(1)}, bf16[512,128]{1,0:T(8,128)(2,1)S(1)}, u32[]{:S(2)}, u32[]{:S(2)}) collective-permute-start(bf16[512,128]{1,0:T(8,128)(2,1)S(1)} %pad_maximum_fusion.2), channel_id=1, source_target_pairs={{0,12},{4,8},{8,4},{12,0},{16,28},{20,24},{24,20},{28,16},{1,13},{... | collective-permute-start | bytes 393224 | tf_op jit(solution)/shard_map/ppermute | solution.py:317
  12.8 1.6 %copy-start = (f32[2,8,32768]{2,1,0:T(8,128)S(1)}, f32[2,8,32768]{2,1,0:T(8,128)}, u32[]{:S(2)}) copy-start(f32[2,8,32768]{2,1,0:T(8,128)} %hist.5) | copy-start | bytes 6291460
  35.1 57.7 %copy-start.1 = (f32[2,8,32768]{2,1,0:T(8,128)S(1)}, f32[2,8,32768]{2,1,0:T(8,128)}, u32[]{:S(2)}) copy-start(f32[2,8,32768]{2,1,0:T(8,128)} %hist.5) | copy-start | bytes 6291460
  35.1 57.7 %copy-start.2 = (f32[32768]{0:T(1024)S(1)}, f32[32768]{0:T(1024)}, u32[]{:S(2)}) copy-start(f32[32768]{0:T(1024)} %param.9) | copy-start | bytes 393220
  62.0 14.4 %collective-permute-start.4 = (f32[1040,128]{1,0:T(8,128)S(1)}, f32[1040,128]{1,0:T(8,128)S(1)}, u32[]{:S(2)}, u32[]{:S(2)}) collective-permute-start(f32[1040,128]{1,0:T(8,128)S(1)} %get-tuple-element.9), channel_id=1, source_target_pairs={{0,4},{4,0},{8,12},{12,8},{16,20},{20,16},{24,28},{28,24},{1,5},{5... | collective-permute-start | bytes 1597448 | tf_op jit(solution)/shard_map/ppermute | solution.py:317
  76.6 7.9 %collective-permute-start.5 = (f32[528,128]{1,0:T(8,128)S(1)}, f32[528,128]{1,0:T(8,128)S(1)}, u32[]{:S(2)}, u32[]{:S(2)}) collective-permute-start(f32[528,128]{1,0:T(8,128)S(1)} %pad_maximum_fusion), channel_id=1, source_target_pairs={{0,8},{4,12},{8,0},{12,4},{16,24},{20,28},{24,16},{28,20},{1,9},{5... | collective-permute-start | bytes 811016 | tf_op jit(solution)/shard_map/ppermute | solution.py:317
  84.6 8.2 %collective-permute-start.6 = (f32[272,128]{1,0:T(8,128)S(1)}, f32[272,128]{1,0:T(8,128)S(1)}, u32[]{:S(2)}, u32[]{:S(2)}) collective-permute-start(f32[272,128]{1,0:T(8,128)S(1)} %pad_maximum_fusion.1), channel_id=1, source_target_pairs={{0,16},{4,20},{8,24},{12,28},{16,0},{20,4},{24,8},{28,12},{1,17},{... | collective-permute-start | bytes 417800 | tf_op jit(solution)/shard_map/ppermute | solution.py:317
  94.0 1.2 %collective-permute-start.7 = (f32[16,128]{1,0:T(8,128)S(1)}, f32[16,128]{1,0:T(8,128)S(1)}, u32[]{:S(2)}, u32[]{:S(2)}) collective-permute-start(f32[16,128]{1,0:T(8,128)S(1)} %get-tuple-element.11), channel_id=1, source_target_pairs={{0,1},{1,0},{2,3},{3,2},{4,5},{5,4},{6,7},{7,6},{8,9},{9,8},{10,11... | collective-permute-start | bytes 24584 | tf_op jit(solution)/shard_map/ppermute | solution.py:317
  95.2 3.7 %collective-permute-start.8 = (f32[16,128]{1,0:T(8,128)S(1)}, f32[16,128]{1,0:T(8,128)S(1)}, u32[]{:S(2)}, u32[]{:S(2)}) collective-permute-start(f32[16,128]{1,0:T(8,128)S(1)} %add.30), channel_id=1, source_target_pairs={{0,2},{1,3},{2,0},{3,1},{4,6},{5,7},{6,4},{7,5},{8,10},{9,11},{10,... | collective-permute-start | bytes 24584 | tf_op jit(solution)/shard_map/ppermute | solution.py:317
  98.8 3.7 %collective-permute-start.9 = (f32[16,128]{1,0:T(8,128)S(1)}, f32[16,128]{1,0:T(8,128)S(1)}, u32[]{:S(2)}, u32[]{:S(2)}) collective-permute-start(f32[16,128]{1,0:T(8,128)S(1)} %add.31), channel_id=1, source_target_pairs={{0,4},{4,0},{8,12},{12,8},{16,20},{20,16},{24,28},{28,24},{1,5},{5... | collective-permute-start | bytes 24584 | tf_op jit(solution)/shard_map/ppermute | solution.py:317
  102.5 3.7 %collective-permute-start.10 = (f32[16,128]{1,0:T(8,128)S(1)}, f32[16,128]{1,0:T(8,128)S(1)}, u32[]{:S(2)}, u32[]{:S(2)}) collective-permute-start(f32[16,128]{1,0:T(8,128)S(1)} %add.32), channel_id=1, source_target_pairs={{0,8},{4,12},{8,0},{12,4},{16,24},{20,28},{24,16},{28,20},{1,9},{5... | collective-permute-start | bytes 24584 | tf_op jit(solution)/shard_map/ppermute | solution.py:317
  106.1 4.5 %collective-permute-start.11 = (f32[16,128]{1,0:T(8,128)S(1)}, f32[16,128]{1,0:T(8,128)S(1)}, u32[]{:S(2)}, u32[]{:S(2)}) collective-permute-start(f32[16,128]{1,0:T(8,128)S(1)} %add.33.dots), channel_id=1, source_target_pairs={{0,16},{4,20},{8,24},{12,28},{16,0},{20,4},{24,8},{28,12},{1,17},{... | collective-permute-start | bytes 24584 | tf_op jit(solution)/shard_map/ppermute | solution.py:317

commit v4 on v3

--- a/solution.py
+++ b/solution.py
@@ -10,6 +10,7 @@
 ridge = 0.2
 SUB = 8
 MAX_ACC = 3
+VALUE_MAX = 0.3
 F32 = jnp.float32
 
 
@@ -160,7 +161,7 @@
     out[lines : lines + gram.shape[0], :] = gram[...]
 
 
-def scatter_body(ids_in, resid, vals_in, gram, *refs, order, owned):
+def scatter_body(ids_in, resid, vals_in, *refs, order, owned):
     n_out = 2
     outs, accs = refs[:n_out], refs[n_out:-3]
     vals, ids, sems = refs[-3:]
@@ -214,16 +215,13 @@
             return carry
 
         lax.fori_loop(0, owned // SUB, fold, 0, unroll=2)
-    for out in outs:
-        out[half * owned :, :] = gram[...]
-
-
-def dots_body(keep, recv, w, hist, result, grad, dots, gram):
+
+
+def dots_body(keep, recv, gram, w, hist, result, grad, dots):
     count, feats = hist.shape[1], hist.shape[2]
     rows, width = w.shape
-    grad[...] = keep[:rows, :] + recv[:rows, :] + ridge * w[...]
+    grad[...] = keep[...] + recv[...] + ridge * w[...]
     result[...] = grad[...]
-    gram[...] = keep[rows:, :] + recv[rows:, :]
 
     def step(j, accs):
         at = pl.ds(pl.multiple_of(j * width, width), width)
@@ -233,7 +231,8 @@
     zero = jnp.zeros((count, width), F32)
     accs = lax.fori_loop(0, feats // width, step, (zero, zero), unroll=8)
     dots[:count, :] = accs[0]
-    dots[count:, :] = accs[1]
+    dots[count : 2 * count, :] = accs[1]
+    dots[2 * count :, :] = gram[...]
 
 
 def coefficient_body(gram, out):
@@ -381,41 +380,44 @@
     acc_mib = SUB * table_mib
     room = (60 * 1024) / 1024 - mib(values) - table_mib - 6
     n_acc = max(1, min(MAX_ACC, int(room // acc_mib)))
-    half = n_dp // 2 * owned + 2 * pairs
+    half = n_dp // 2 * owned
     send, keep = pl.pallas_call(
         functools.partial(scatter_body, order=slots, owned=owned),
         out_shape=[jax.ShapeDtypeStruct((half, width), F32)] * 2,
-        in_specs=[any_spec(), smem_spec(), hbm_spec(), vmem_spec()],
+        in_specs=[any_spec(), smem_spec(), hbm_spec()],
         out_specs=[vmem_spec(), vmem_spec()],
         scratch_shapes=[pltpu.VMEM((blocks * SUB, width), F32)] * n_acc + streams,
         compiler_params=params(mib(values) + table_mib + n_acc * acc_mib + 3),
-    )(flat_ids * SUB, resid, values, gram_rows)
-
-    size = n_dp // 2
-    tail = 2 * pairs
+    )(flat_ids * SUB, resid, values)
+
+    scale, bound = 1.0, VALUE_MAX * count * active * max(1, n_dp // 2)
+    while bound * scale > 60000:
+        scale /= 2
     for b in bits:
-        came = xor_permute(send, "dp", n_dp, b)
-        if size == 1:
+        sent = send if scale == 1.0 else send * scale
+        came = xor_permute(sent.astype(jnp.float16), "dp", n_dp, b).astype(F32)
+        came = came if scale == 1.0 else came / scale
+        if b == bits[-1]:
             break
         total = keep + came
-        size //= 2
-        cut = size * owned
-        total_gram = total[2 * cut :]
-        send = jnp.concatenate([total[:cut], total_gram], axis=0)
-        keep = jnp.concatenate([total[cut : 2 * cut], total_gram], axis=0)
-
-    result, grad, dots, gram_all = pl.pallas_call(
+        cut = total.shape[0] // 2
+        send, keep = total[:cut], total[cut:]
+
+    result, grad, dots = pl.pallas_call(
         dots_body,
         out_shape=[
             jax.ShapeDtypeStruct((owned, width), F32),
             jax.ShapeDtypeStruct((owned, width), F32),
-            jax.ShapeDtypeStruct((2 * pairs, width), F32),
-            jax.ShapeDtypeStruct((2 * pairs, width), F32),
+            jax.ShapeDtypeStruct((4 * pairs, width), F32),
         ],
-        in_specs=[vmem_spec()] * 4,
-        out_specs=[vmem_spec()] * 4,
+        in_specs=[vmem_spec()] * 5,
+        out_specs=[vmem_spec()] * 3,
         compiler_params=params(2 * mib(history) + 4),
-    )(keep, came, w2, history)
+    )(keep, came, gram_rows, w2, history)
+
+    for b in bits:
+        dots = dots + xor_permute(dots, "dp", n_dp, b)
+    dots, gram_all = dots[: 2 * pairs], dots[2 * pairs :]
 
     coef = pl.pallas_call(
         coefficient_body,
@@ -425,11 +427,10 @@
         compiler_params=params(4),
     )(gram_all)
 
-    hops = [("mp", n_mp, b) for b in reduce_bits(n_mp)] + [("dp", n_dp, b) for b in bits]
-    for axis, n, b in hops[:-1]:
-        dots = dots + xor_permute(dots, axis, n, b)
-    axis, n, b = hops[-1]
-    other = xor_permute(dots, axis, n, b)
+    hops = reduce_bits(n_mp)
+    for b in hops[:-1]:
+        dots = dots + xor_permute(dots, "mp", n_mp, b)
+    other = xor_permute(dots, "mp", n_mp, hops[-1])
 
     moved = pl.pallas_call(
         move_body,

time: 112 us -> 101 us (0.902)
  waiting for transfers between devices: 38.9 us -> 23.8 us
  starting transfers between devices: 17.6 us -> 20.9 us
    ppermute x12, waiting for transfers between devices: 38.9 us -> 23.8 us  [xor_permute(): return lax.ppermute(x, axis, [(i, i ^ k) for i in range(n)])]
    ppermute x12, starting transfers between devices: 17.6 us -> 20.9 us  [xor_permute(): return lax.ppermute(x, axis, [(i, i ^ k) for i in range(n)])]
  transfers between devices with their start and end apart: 12 -> 12, of which waited for: 10 -> 10; matrix products, arithmetic and copies ran while one was open for 1% -> 2% of each run, Pallas kernels for 3% -> 3%
where the time goes in v4:
time: 101 us; the launch traced here: 100 us
  Pallas kernels  44.6 us (44%)
  waiting for transfers between devices  23.8 us (24%)
  starting transfers between devices  20.9 us (21%)
  blocking collectives  5.35 us (5%)
  other arithmetic  2.15 us (2%)
  local copies, waits for them, and re-layouts  2.13 us (2%)
  between operations  1.45 us (1%)
    ppermute x12, waiting for transfers between devices, xor_permute(): return lax.ppermute(x, axis, [(i, i ^ k) for i in range(n)])  23.8 us
    pallas_call x1, Pallas kernels, local(): pl.pallas_call(functools.partial(scatter_body, order=slots, owned=owned),...  21.5 us
    ppermute x12, starting transfers between devices, xor_permute(): return lax.ppermute(x, axis, [(i, i ^ k) for i in range(n)])  20.9 us
    pallas_call x1, Pallas kernels, local(): pl.pallas_call(gather_body, out_shape=jax.ShapeDtypeStruct((lines + 2 * p...  17 us
    all_gather x1, blocking collectives, local(): packed = jnp.sum(lax.all_gather(packed, 'mp', axis=0), axis=0)  5.35 us
    pallas_call x1, Pallas kernels, local(): pl.pallas_call(gram_body, out_shape=jax.ShapeDtypeStruct((2 * pairs, widt...  2.64 us
  transfers between devices with their start and end apart: 12, of which 10 were waited for; matrix products, arithmetic and copies ran while one was open for 2% of the time, Pallas kernels for 3%

profile of v4, /device:TPU:0, one launch (start us, length us, event | category | flops | bytes accessed | tf_op | source)
XLA Modules:
  0.0 100.4 jit_solution(10353325557434301754)
XLA Ops:
  0.6 0.0 copy-start.3
  0.6 0.9 bitcast_convert_fusion.refs_0_
  1.6 4.1 %collective-permute-start = (bf16[256,128]{1,0:T(8,128)(2,1)S(1)}, bf16[256,128]{1,0:T(8,128)(2,1)S(1)}, u32[]{:S(2)}, u32[]{:S(2)}) collective-permute-start(bf16[256,128]{1,0:T(8,128)(2,1)S(1)} %bitcast_convert_fusion.refs_0_), channel_id=1, source_target_pairs={{0,16},{4,20},{8,24},{12,28},{16,0},{20,4},{24,8},{28,12},{1,17},{... | collective-permute-start | bytes 196616 | tf_op jit(solution)/shard_map/ppermute | solution.py:316
  5.6 1.0 %subtract_add_fusion = s32[1024,24]{0,1:T(8,128)S(1)} fusion(s32[1024,24]{0,1:T(8,128)} %param.7, s32[]{:T(128)S(6)} %axis_index.15), kind=kLoop, calls=%fused_computation.10 | loop fusion | flops 835584 | bytes 196612 | tf_op jit(solution)/shard_map/add | solution.py:345
  6.6 0.2 copy.8
  6.8 0.3 reshape.23.ids_in
  7.2 2.1 %collective-permute-done.refs_1_ = bf16[256,128]{1,0:T(8,128)(2,1)S(1)} collective-permute-done((bf16[256,128]{1,0:T(8,128)(2,1)S(1)}, bf16[256,128]{1,0:T(8,128)(2,1)S(1)}, u32[]{:S(2)}, u32[]{:S(2)}) %collective-permute-start) | collective-permute-done | bytes 65568 | tf_op jit(solution)/shard_map/ppermute | solution.py:316
  9.3 1.6 %collective-permute-start.3 = (bf16[512,128]{1,0:T(8,128)(2,1)S(1)}, bf16[512,128]{1,0:T(8,128)(2,1)S(1)}, u32[]{:S(2)}, u32[]{:S(2)}) collective-permute-start(bf16[512,128]{1,0:T(8,128)(2,1)S(1)} %pad_maximum_fusion), channel_id=1, source_target_pairs={{0,12},{4,8},{8,4},{12,0},{16,28},{20,24},{24,20},{28,16},{1,13},{... | collective-permute-start | bytes 393224 | tf_op jit(solution)/shard_map/ppermute | solution.py:316
  10.8 1.7 %collective-permute-start.2 = (bf16[512,128]{1,0:T(8,128)(2,1)S(1)}, bf16[512,128]{1,0:T(8,128)(2,1)S(1)}, u32[]{:S(2)}, u32[]{:S(2)}) collective-permute-start(bf16[512,128]{1,0:T(8,128)(2,1)S(1)} %pad_maximum_fusion), channel_id=1, source_target_pairs={{0,8},{4,12},{8,0},{12,4},{16,24},{20,28},{24,16},{28,20},{1,9},{5... | collective-permute-start | bytes 393224 | tf_op jit(solution)/shard_map/ppermute | solution.py:316
  12.5 0.3 collective-permute-start.1
  12.8 0.0 copy-start
  12.9 1.6 %copy-done = f32[2,8,32768]{2,1,0:T(8,128)S(1)} copy-done((f32[2,8,32768]{2,1,0:T(8,128)S(1)}, f32[2,8,32768]{2,1,0:T(8,128)}, u32[]{:S(2)}) %copy-start) | copy-done | bytes 2097176
  14.4 2.6 %shard_map.77.gram = f32[16,128]{1,0:T(8,128)S(1)} custom-call(f32[2,8,32768]{2,1,0:T(8,128)S(1)} %copy-done), custom_call_target="tpu_custom_call" | custom-call | tf_op jit(solution)/shard_map/pallas_call | solution.py:347
  17.1 0.0 collective-permute-done.3.refs_4_
  17.1 0.0 collective-permute-done.2.refs_3_
  17.1 0.4 collective-permute-done.1.refs_2_
  17.5 17.0 %shard_map.78 = f32[24,128]{1,0:T(8,128)S(1)} custom-call(s32[24576]{0:T(1024)S(1)} %reshape.23.ids_in, bf16[1024,24,128]{2,1,0:T(8,128)(2,1)} %vals_in.3, f32[16,128]{1,0:T(8,128)S(1)} %shard_map.77.gram, bf16[256,128]{1,0:T(8,128)(2,1)S(1)} %bitcast_convert_fusion.refs_0_, bf16[256,128]{1,0:T(8,128)(2,1)S(1)} %collective-permute-done.refs_1_, ...), custom_call_target="tpu_custom_call" | custom-call | tf_op jit(solution)/shard_map/pallas_call | solution.py:361
  34.5 0.0 copy-start.1
  34.5 0.0 copy-start.2
  34.5 5.4 %all-gather = f32[96,128]{1,0:T(8,128)S(1)} all-gather(f32[24,128]{1,0:T(8,128)S(1)} %shard_map.78), channel_id=2, replica_groups=mesh['dp'=8,'mp'=4] {'mp'}, dimensions={0}, use_global_device_ids=true | all-gather | bytes 61440 | tf_op jit(solution)/shard_map/all_gather | solution.py:370
  39.8 0.0 copy-done.3
  39.9 21.5 %shard_map.79 = (f32[1024,128]{1,0:T(8,128)S(1)}, f32[1024,128]{1,0:T(8,128)S(1)}) custom-call(s32[24576]{0:T(1024)S(1)} %broadcast_multiply_fusion.ids_in, f32[1024]{0:T(1024)S(1)} %fusion.6.resid, bf16[1024,24,128]{2,1,0:T(8,128)(2,1)} %vals_in.3), custom_call_target="tpu_custom_call" | custom-call | tf_op jit(solution)/shard_map/pallas_call | solution.py:384
  61.4 1.4 %collective-permute-start.4 = (f16[1024,128]{1,0:T(8,128)(2,1)S(1)}, f16[1024,128]{1,0:T(8,128)(2,1)S(1)}, u32[]{:S(2)}, u32[]{:S(2)}) collective-permute-start(f16[1024,128]{1,0:T(8,128)(2,1)S(1)} %convert_element_type.22), channel_id=1, source_target_pairs={{0,4},{4,0},{8,12},{12,8},{16,20},{20,16},{24,28},{28,24},{1,5},{5... | collective-permute-start | bytes 786440 | tf_op jit(solution)/shard_map/ppermute | solution.py:316
  62.9 7.2 %collective-permute-done.4 = f16[1024,128]{1,0:T(8,128)(2,1)S(1)} collective-permute-done((f16[1024,128]{1,0:T(8,128)(2,1)S(1)}, f16[1024,128]{1,0:T(8,128)(2,1)S(1)}, u32[]{:S(2)}, u32[]{:S(2)}) %collective-permute-start.4) | collective-permute-done | bytes 262176 | tf_op jit(solution)/shard_map/ppermute | solution.py:316
  70.1 0.1 convert_add_fusion
  70.2 1.2 %collective-permute-start.5 = (f16[512,128]{1,0:T(8,128)(2,1)S(1)}, f16[512,128]{1,0:T(8,128)(2,1)S(1)}, u32[]{:S(2)}, u32[]{:S(2)}) collective-permute-start(f16[512,128]{1,0:T(8,128)(2,1)S(1)} %slice_convert_fusion), channel_id=1, source_target_pairs={{0,8},{4,12},{8,0},{12,4},{16,24},{20,28},{24,16},{28,20},{1,9},{5... | collective-permute-start | bytes 393224 | tf_op jit(solution)/shard_map/ppermute | solution.py:316
  71.4 3.8 %collective-permute-done.5 = f16[512,128]{1,0:T(8,128)(2,1)S(1)} collective-permute-done((f16[512,128]{1,0:T(8,128)(2,1)S(1)}, f16[512,128]{1,0:T(8,128)(2,1)S(1)}, u32[]{:S(2)}, u32[]{:S(2)}) %collective-permute-start.5) | collective-permute-done | bytes 131104 | tf_op jit(solution)/shard_map/ppermute | solution.py:316
  75.3 3.0 %collective-permute-start.6 = (f16[256,128]{1,0:T(8,128)(2,1)S(1)}, f16[256,128]{1,0:T(8,128)(2,1)S(1)}, u32[]{:S(2)}, u32[]{:S(2)}) collective-permute-start(f16[256,128]{1,0:T(8,128)(2,1)S(1)} %get-tuple-element.12), channel_id=1, source_target_pairs={{0,16},{4,20},{8,24},{12,28},{16,0},{20,4},{24,8},{28,12},{1,17},{... | collective-permute-start | bytes 196616 | tf_op jit(solution)/shard_map/ppermute | solution.py:316
  78.2 2.3 %collective-permute-done.6 = f16[256,128]{1,0:T(8,128)(2,1)S(1)} collective-permute-done((f16[256,128]{1,0:T(8,128)(2,1)S(1)}, f16[256,128]{1,0:T(8,128)(2,1)S(1)}, u32[]{:S(2)}, u32[]{:S(2)}) %collective-permute-start.6) | collective-permute-done | bytes 65568 | tf_op jit(solution)/shard_map/ppermute | solution.py:316
  80.5 0.0 copy-done.1
  80.5 0.0 copy-done.2
  80.5 1.2 %shard_map.80 = (f32[256,128]{1,0:T(8,128)}, f32[256,128]{1,0:T(8,128)S(1)}, f32[32,128]{1,0:T(8,128)S(1)}) custom-call(f32[256,128]{1,0:T(8,128)S(1)} %get-tuple-element.13.keep, f32[256,128]{1,0:T(8,128)S(1)} %convert_element_type.25.recv, f32[16,128]{1,0:T(8,128)S(1)} %slice.39.gram, f32[256,128]{1,0:T(8,128)S(1)} %bitcast.9, f32[2,8,32768]{2,1,0:T(8,128)S(1)} %copy-done.1), custom_call_target="tpu_custom_call" | custom-call | tf_op jit(solution)/shard_map/pallas_call | solution.py:406
  81.7 1.4 %collective-permute-start.7 = (f32[32,128]{1,0:T(8,128)S(1)}, f32[32,128]{1,0:T(8,128)S(1)}, u32[]{:S(2)}, u32[]{:S(2)}) collective-permute-start(f32[32,128]{1,0:T(8,128)S(1)} %get-tuple-element.9), channel_id=1, source_target_pairs={{0,4},{4,0},{8,12},{12,8},{16,20},{20,16},{24,28},{28,24},{1,5},{5... | collective-permute-start | bytes 49160 | tf_op jit(solution)/shard_map/ppermute | solution.py:316
  83.1 2.4 %collective-permute-done.7 = f32[32,128]{1,0:T(8,128)S(1)} collective-permute-done((f32[32,128]{1,0:T(8,128)S(1)}, f32[32,128]{1,0:T(8,128)S(1)}, u32[]{:S(2)}, u32[]{:S(2)}) %collective-permute-start.7) | collective-permute-done | bytes 16416 | tf_op jit(solution)/shard_map/ppermute | solution.py:316
  85.5 1.7 %collective-permute-start.8 = (f32[32,128]{1,0:T(8,128)S(1)}, f32[32,128]{1,0:T(8,128)S(1)}, u32[]{:S(2)}, u32[]{:S(2)}) collective-permute-start(f32[32,128]{1,0:T(8,128)S(1)} %add.30), channel_id=1, source_target_pairs={{0,8},{4,12},{8,0},{12,4},{16,24},{20,28},{24,16},{28,20},{1,9},{5... | collective-permute-start | bytes 49160 | tf_op jit(solution)/shard_map/ppermute | solution.py:316
  87.2 2.0 %collective-permute-done.8 = f32[32,128]{1,0:T(8,128)S(1)} collective-permute-done((f32[32,128]{1,0:T(8,128)S(1)}, f32[32,128]{1,0:T(8,128)S(1)}, u32[]{:S(2)}, u32[]{:S(2)}) %collective-permute-start.8) | collective-permute-done | bytes 16416 | tf_op jit(solution)/shard_map/ppermute | solution.py:316
  89.2 3.0 %collective-permute-start.9 = (f32[32,128]{1,0:T(8,128)S(1)}, f32[32,128]{1,0:T(8,128)S(1)}, u32[]{:S(2)}, u32[]{:S(2)}) collective-permute-start(f32[32,128]{1,0:T(8,128)S(1)} %add.31), channel_id=1, source_target_pairs={{0,16},{4,20},{8,24},{12,28},{16,0},{20,4},{24,8},{28,12},{1,17},{... | collective-permute-start | bytes 49160 | tf_op jit(solution)/shard_map/ppermute | solution.py:316
  92.2 1.7 %collective-permute-done.9 = f32[32,128]{1,0:T(8,128)S(1)} collective-permute-done((f32[32,128]{1,0:T(8,128)S(1)}, f32[32,128]{1,0:T(8,128)S(1)}, u32[]{:S(2)}, u32[]{:S(2)}) %collective-permute-start.9) | collective-permute-done | bytes 16416 | tf_op jit(solution)/shard_map/ppermute | solution.py:316
  94.0 0.0 collective-permute-start.10
  94.0 1.2 %collective-permute-done.10 = f32[16,128]{1,0:T(8,128)S(1)} collective-permute-done((f32[16,128]{1,0:T(8,128)S(1)}, f32[16,128]{1,0:T(8,128)S(1)}, u32[]{:S(2)}, u32[]{:S(2)}) %collective-permute-start.10) | collective-permute-done | bytes 8224 | tf_op jit(solution)/shard_map/ppermute | solution.py:316
  95.1 1.5 %collective-permute-start.11 = (f32[16,128]{1,0:T(8,128)S(1)}, f32[16,128]{1,0:T(8,128)S(1)}, u32[]{:S(2)}, u32[]{:S(2)}) collective-permute-start(f32[16,128]{1,0:T(8,128)S(1)} %get-tuple-element.14.dots), channel_id=1, source_target_pairs={{0,2},{1,3},{2,0},{3,1},{4,6},{5,7},{6,4},{7,5},{8,10},{9,11},{10,... | collective-permute-start | bytes 24584 | tf_op jit(solution)/shard_map/ppermute | solution.py:316
  97.3 0.8 shard_map.81.coef
  98.1 0.7 collective-permute-done.11.recv
  98.8 1.6 %shard_map.82 = f32[256,128]{1,0:T(8,128)} custom-call(f32[1]{0:T(128)S(6)} %copy.9.steps, f32[24,128]{1,0:T(8,128)S(1)} %shard_map.81.coef, f32[16,128]{1,0:T(8,128)S(1)} %get-tuple-element.14.dots, f32[16,128]{1,0:T(8,128)S(1)} %collective-permute-done.11.recv, f32[256,128]{1,0:T(8,128)S(1)} %get-tuple-element.10.grad, f32[256,128]{1,0:T(8,128)S(1)} %bitcast.10, ...), custom_call_target="tpu_custom_call" | custom-call | tf_op jit(solution)/shard_map/pallas_call | solution.py:435
  (15 shorter events, 0.2 us)
Async XLA Ops:
  0.6 39.2 %copy-start.3 = (s32[1024]{0:T(1024)S(1)}, s32[1024]{0:T(1024)}, u32[]{:S(2)}) copy-start(s32[1024]{0:T(1024)} %param.8) | copy-start | bytes 12292
  1.6 7.7 %collective-permute-start = (bf16[256,128]{1,0:T(8,128)(2,1)S(1)}, bf16[256,128]{1,0:T(8,128)(2,1)S(1)}, u32[]{:S(2)}, u32[]{:S(2)}) collective-permute-start(bf16[256,128]{1,0:T(8,128)(2,1)S(1)} %bitcast_convert_fusion.refs_0_), channel_id=1, source_target_pairs={{0,16},{4,20},{8,24},{12,28},{16,0},{20,4},{24,8},{28,12},{1,17},{... | collective-permute-start | bytes 196616 | tf_op jit(solution)/shard_map/ppermute | solution.py:316
  9.3 7.8 %collective-permute-start.3 = (bf16[512,128]{1,0:T(8,128)(2,1)S(1)}, bf16[512,128]{1,0:T(8,128)(2,1)S(1)}, u32[]{:S(2)}, u32[]{:S(2)}) collective-permute-start(bf16[512,128]{1,0:T(8,128)(2,1)S(1)} %pad_maximum_fusion), channel_id=1, source_target_pairs={{0,12},{4,8},{8,4},{12,0},{16,28},{20,24},{24,20},{28,16},{1,13},{... | collective-permute-start | bytes 393224 | tf_op jit(solution)/shard_map/ppermute | solution.py:316
  10.8 6.3 %collective-permute-start.2 = (bf16[512,128]{1,0:T(8,128)(2,1)S(1)}, bf16[512,128]{1,0:T(8,128)(2,1)S(1)}, u32[]{:S(2)}, u32[]{:S(2)}) collective-permute-start(bf16[512,128]{1,0:T(8,128)(2,1)S(1)} %pad_maximum_fusion), channel_id=1, source_target_pairs={{0,8},{4,12},{8,0},{12,4},{16,24},{20,28},{24,16},{28,20},{1,9},{5... | collective-permute-start | bytes 393224 | tf_op jit(solution)/shard_map/ppermute | solution.py:316
  12.5 5.0 %collective-permute-start.1 = (bf16[512,128]{1,0:T(8,128)(2,1)S(1)}, bf16[512,128]{1,0:T(8,128)(2,1)S(1)}, u32[]{:S(2)}, u32[]{:S(2)}) collective-permute-start(bf16[512,128]{1,0:T(8,128)(2,1)S(1)} %pad_maximum_fusion), channel_id=1, source_target_pairs={{0,4},{4,0},{8,12},{12,8},{16,20},{20,16},{24,28},{28,24},{1,5},{5... | collective-permute-start | bytes 393224 | tf_op jit(solution)/shard_map/ppermute | solution.py:316
  12.8 1.6 %copy-start = (f32[2,8,32768]{2,1,0:T(8,128)S(1)}, f32[2,8,32768]{2,1,0:T(8,128)}, u32[]{:S(2)}) copy-start(f32[2,8,32768]{2,1,0:T(8,128)} %hist.5) | copy-start | bytes 6291460
  34.5 46.0 %copy-start.1 = (f32[2,8,32768]{2,1,0:T(8,128)S(1)}, f32[2,8,32768]{2,1,0:T(8,128)}, u32[]{:S(2)}) copy-start(f32[2,8,32768]{2,1,0:T(8,128)} %hist.5) | copy-start | bytes 6291460
  34.5 46.0 %copy-start.2 = (f32[32768]{0:T(1024)S(1)}, f32[32768]{0:T(1024)}, u32[]{:S(2)}) copy-start(f32[32768]{0:T(1024)} %param.9) | copy-start | bytes 393220
  61.4 8.6 %collective-permute-start.4 = (f16[1024,128]{1,0:T(8,128)(2,1)S(1)}, f16[1024,128]{1,0:T(8,128)(2,1)S(1)}, u32[]{:S(2)}, u32[]{:S(2)}) collective-permute-start(f16[1024,128]{1,0:T(8,128)(2,1)S(1)} %convert_element_type.22), channel_id=1, source_target_pairs={{0,4},{4,0},{8,12},{12,8},{16,20},{20,16},{24,28},{28,24},{1,5},{5... | collective-permute-start | bytes 786440 | tf_op jit(solution)/shard_map/ppermute | solution.py:316
  70.2 5.0 %collective-permute-start.5 = (f16[512,128]{1,0:T(8,128)(2,1)S(1)}, f16[512,128]{1,0:T(8,128)(2,1)S(1)}, u32[]{:S(2)}, u32[]{:S(2)}) collective-permute-start(f16[512,128]{1,0:T(8,128)(2,1)S(1)} %slice_convert_fusion), channel_id=1, source_target_pairs={{0,8},{4,12},{8,0},{12,4},{16,24},{20,28},{24,16},{28,20},{1,9},{5... | collective-permute-start | bytes 393224 | tf_op jit(solution)/shard_map/ppermute | solution.py:316
  75.3 5.2 %collective-permute-start.6 = (f16[256,128]{1,0:T(8,128)(2,1)S(1)}, f16[256,128]{1,0:T(8,128)(2,1)S(1)}, u32[]{:S(2)}, u32[]{:S(2)}) collective-permute-start(f16[256,128]{1,0:T(8,128)(2,1)S(1)} %get-tuple-element.12), channel_id=1, source_target_pairs={{0,16},{4,20},{8,24},{12,28},{16,0},{20,4},{24,8},{28,12},{1,17},{... | collective-permute-start | bytes 196616 | tf_op jit(solution)/shard_map/ppermute | solution.py:316
  81.7 3.7 %collective-permute-start.7 = (f32[32,128]{1,0:T(8,128)S(1)}, f32[32,128]{1,0:T(8,128)S(1)}, u32[]{:S(2)}, u32[]{:S(2)}) collective-permute-start(f32[32,128]{1,0:T(8,128)S(1)} %get-tuple-element.9), channel_id=1, source_target_pairs={{0,4},{4,0},{8,12},{12,8},{16,20},{20,16},{24,28},{28,24},{1,5},{5... | collective-permute-start | bytes 49160 | tf_op jit(solution)/shard_map/ppermute | solution.py:316
  85.5 3.7 %collective-permute-start.8 = (f32[32,128]{1,0:T(8,128)S(1)}, f32[32,128]{1,0:T(8,128)S(1)}, u32[]{:S(2)}, u32[]{:S(2)}) collective-permute-start(f32[32,128]{1,0:T(8,128)S(1)} %add.30), channel_id=1, source_target_pairs={{0,8},{4,12},{8,0},{12,4},{16,24},{20,28},{24,16},{28,20},{1,9},{5... | collective-permute-start | bytes 49160 | tf_op jit(solution)/shard_map/ppermute | solution.py:316
  89.2 4.8 %collective-permute-start.9 = (f32[32,128]{1,0:T(8,128)S(1)}, f32[32,128]{1,0:T(8,128)S(1)}, u32[]{:S(2)}, u32[]{:S(2)}) collective-permute-start(f32[32,128]{1,0:T(8,128)S(1)} %add.31), channel_id=1, source_target_pairs={{0,16},{4,20},{8,24},{12,28},{16,0},{20,4},{24,8},{28,12},{1,17},{... | collective-permute-start | bytes 49160 | tf_op jit(solution)/shard_map/ppermute | solution.py:316
  94.0 1.2 %collective-permute-start.10 = (f32[16,128]{1,0:T(8,128)S(1)}, f32[16,128]{1,0:T(8,128)S(1)}, u32[]{:S(2)}, u32[]{:S(2)}) collective-permute-start(f32[16,128]{1,0:T(8,128)S(1)} %slice.41), channel_id=1, source_target_pairs={{0,1},{1,0},{2,3},{3,2},{4,5},{5,4},{6,7},{7,6},{8,9},{9,8},{10,11... | collective-permute-start | bytes 24584 | tf_op jit(solution)/shard_map/ppermute | solution.py:316
  95.1 3.7 %collective-permute-start.11 = (f32[16,128]{1,0:T(8,128)S(1)}, f32[16,128]{1,0:T(8,128)S(1)}, u32[]{:S(2)}, u32[]{:S(2)}) collective-permute-start(f32[16,128]{1,0:T(8,128)S(1)} %get-tuple-element.14.dots), channel_id=1, source_target_pairs={{0,2},{1,3},{2,0},{3,1},{4,6},{5,7},{6,4},{7,5},{8,10},{9,11},{10,... | collective-permute-start | bytes 24584 | tf_op jit(solution)/shard_map/ppermute | solution.py:316

commit v5 on v4

--- a/solution.py
+++ b/solution.py
@@ -10,6 +10,7 @@
 ridge = 0.2
 SUB = 8
 MAX_ACC = 3
+WIDE = 32
 VALUE_MAX = 0.3
 F32 = jnp.float32
 
@@ -139,8 +140,8 @@
     masks = sublane_masks()
 
     def group(g, carry):
-        for u in range(SUB):
-            e = g * SUB + u
+        for u in range(WIDE):
+            e = g * WIDE + u
             v = vals[e].astype(F32)
             total = None
             for t in range(0, active, SUB):
@@ -153,7 +154,7 @@
             rows[pl.ds(e, 1), :] = jnp.sum(total, axis=0, keepdims=True)
         return carry
 
-    run_chunks(srcs, dsts, sems, count // SUB, group)
+    run_chunks(srcs, dsts, sems, count // WIDE, group)
     lines = count // width
     for b in range(lines):
         flipped = rows[b * width : (b + 1) * width, :].T
@@ -161,10 +162,12 @@
     out[lines : lines + gram.shape[0], :] = gram[...]
 
 
-def scatter_body(ids_in, resid, vals_in, *refs, order, owned):
+def scatter_body(ids_in, resid_in, vals_in, *refs, order, owned):
     n_out = 2
-    outs, accs = refs[:n_out], refs[n_out:-3]
-    vals, ids, sems = refs[-3:]
+    outs, accs = refs[:n_out], refs[n_out:-5]
+    resid, resid_sem, vals, ids, sems = refs[-5:]
+    resid_copy = pltpu.make_async_copy(resid_in, resid, resid_sem)
+    resid_copy.start()
     srcs, dsts = (ids_in, vals_in), (ids, vals)
     count, active, width = vals.shape
     start_chunks(srcs, dsts, sems)
@@ -179,7 +182,8 @@
         return carry
 
     lax.fori_loop(0, blocks // SUB, clear, 0)
-    unroll = 8
+    resid_copy.wait()
+    unroll = WIDE
 
     def group(g, carry):
         turn = 0
@@ -214,7 +218,7 @@
             out[pl.ds(pl.multiple_of(base + j * SUB, SUB), SUB), :] = fold_tiles(tiles)
             return carry
 
-        lax.fori_loop(0, owned // SUB, fold, 0, unroll=2)
+        lax.fori_loop(0, owned // SUB, fold, 0, unroll=4)
 
 
 def dots_body(keep, recv, gram, w, hist, result, grad, dots):
@@ -278,19 +282,18 @@
     c_y = jnp.broadcast_to(mixed[count:], (count, width))
     gamma = coef[2 * count :, :]
     rate = steps[0]
-    masks = sublane_masks()
 
     def step(j, carry):
-        tile = jnp.zeros((SUB, width), F32)
+        tiles = []
         for u in range(SUB):
             at = pl.ds(pl.multiple_of((j * SUB + u) * width, width), width)
-            mix = jnp.sum(c_s * hist[0, :, at] + c_y * hist[1, :, at], axis=0, keepdims=True)
-            tile = jnp.where(masks[u], jnp.broadcast_to(mix, (SUB, width)), tile)
+            tiles.append(c_s * hist[0, :, at] + c_y * hist[1, :, at])
+        tile = fold_tiles(tiles)
         at = pl.ds(pl.multiple_of(j * SUB, SUB), SUB)
         out[at, :] = w[at, :] - rate * (gamma * grad[at, :] + tile)
         return carry
 
-    lax.fori_loop(0, rows // SUB, step, 0)
+    lax.fori_loop(0, rows // SUB, step, 0, unroll=2)
 
 
 def gather_stages(n):
@@ -331,6 +334,7 @@
     order = [0]
     for offsets in gather_stages(n_dp):
         whole = pieces[0] if len(pieces) == 1 else jnp.concatenate(pieces, axis=0)
+        whole, late_history = lax.optimization_barrier((whole, history))
         came = [xor_permute(whole, "dp", n_dp, k) for k in offsets]
         pieces = pieces + came
         order = order + [p ^ k for k in offsets for p in order]
@@ -350,7 +354,7 @@
         in_specs=[vmem_spec()],
         out_specs=vmem_spec(),
         compiler_params=params(2 * mib(history) + 2),
-    )(history)
+    )(late_history)
 
     streams = [
         pltpu.VMEM(values.shape, values.dtype),
@@ -367,7 +371,8 @@
         compiler_params=params(mib(values) + 2 * table_mib + 6),
     )(flat_ids, values, gram, *pieces)
 
-    packed = jnp.sum(lax.all_gather(packed, "mp", axis=0), axis=0)
+    for b in reduce_bits(n_mp):
+        packed = packed + xor_permute(packed, "mp", n_mp, b)
     resid = jax.nn.sigmoid(packed[:lines].reshape(-1)) - labels.astype(F32)
     gram_rows = packed[lines:]
 
@@ -384,9 +389,11 @@
     send, keep = pl.pallas_call(
         functools.partial(scatter_body, order=slots, owned=owned),
         out_shape=[jax.ShapeDtypeStruct((half, width), F32)] * 2,
-        in_specs=[any_spec(), smem_spec(), hbm_spec()],
+        in_specs=[any_spec(), any_spec(), hbm_spec()],
         out_specs=[vmem_spec(), vmem_spec()],
-        scratch_shapes=[pltpu.VMEM((blocks * SUB, width), F32)] * n_acc + streams,
+        scratch_shapes=[pltpu.VMEM((blocks * SUB, width), F32)] * n_acc
+        + [pltpu.SMEM((count,), F32), pltpu.SemaphoreType.DMA]
+        + streams,
         compiler_params=params(mib(values) + table_mib + n_acc * acc_mib + 3),
     )(flat_ids * SUB, resid, values)
 

time: 101 us -> 97.7 us (0.967)
  waiting for transfers between devices: 23.8 us -> 30.9 us
  blocking collectives: 5.35 us -> 0 us
  Pallas kernels: 44.6 us -> 41.6 us
  starting transfers between devices: 20.9 us -> 19.2 us
    ppermute x12 -> x14, waiting for transfers between devices: 23.8 us -> 30.9 us  [xor_permute(): return lax.ppermute(x, axis, [(i, i ^ k) for i in range(n)])]
    all_gather x1 -> x0, blocking collectives: 5.35 us -> none  [local(): packed = jnp.sum(lax.all_gather(packed, 'mp', axis=0), axis=0)]
    pallas_call x1, Pallas kernels: 21.5 us -> 19.8 us  [local(): pl.pallas_call(functools.partial(scatter_body, order=slots, owned=owned),...]
    ppermute x12 -> x14, starting transfers between devices: 20.9 us -> 19.2 us  [xor_permute(): return lax.ppermute(x, axis, [(i, i ^ k) for i in range(n)])]
    pallas_call x1, Pallas kernels: 17 us -> 15.8 us  [local(): pl.pallas_call(gather_body, out_shape=jax.ShapeDtypeStruct((lines + 2 * p...]
  transfers between devices with their start and end apart: 12 -> 14, of which waited for: 10 -> 11; matrix products, arithmetic and copies ran while one was open for 2% -> 2% of each run, Pallas kernels for 3% -> 3%
where the time goes in v5:
time: 97.7 us; the launch traced here: 97.5 us
  Pallas kernels  41.6 us (43%)
  waiting for transfers between devices  30.9 us (32%)
  starting transfers between devices  19.2 us (20%)
  other arithmetic  2.15 us (2%)
  local copies, waits for them, and re-layouts  2.13 us (2%)
  between operations  1.46 us (1%)
    ppermute x14, waiting for transfers between devices, xor_permute(): return lax.ppermute(x, axis, [(i, i ^ k) for i in range(n)])  30.9 us
    pallas_call x1, Pallas kernels, local(): pl.pallas_call(functools.partial(scatter_body, order=slots, owned=owned),...  19.8 us
    ppermute x14, starting transfers between devices, xor_permute(): return lax.ppermute(x, axis, [(i, i ^ k) for i in range(n)])  19.2 us
    pallas_call x1, Pallas kernels, local(): pl.pallas_call(gather_body, out_shape=jax.ShapeDtypeStruct((lines + 2 * p...  15.8 us
    pallas_call x1, Pallas kernels, local(): pl.pallas_call(gram_body, out_shape=jax.ShapeDtypeStruct((2 * pairs, widt...  2.64 us
  transfers between devices with their start and end apart: 14, of which 11 were waited for; matrix products, arithmetic and copies ran while one was open for 2% of the time, Pallas kernels for 3%

profile of v5, /device:TPU:0, one launch (start us, length us, event | category | flops | bytes accessed | tf_op | source)
XLA Modules:
  0.0 97.5 jit_solution(9689557154494588193)
XLA Ops:
  0.6 0.0 copy-start.3
  0.6 0.9 bitcast_convert_fusion.refs_0_
  1.6 4.1 %collective-permute-start = (bf16[256,128]{1,0:T(8,128)(2,1)S(1)}, bf16[256,128]{1,0:T(8,128)(2,1)S(1)}, u32[]{:S(2)}, u32[]{:S(2)}) collective-permute-start(bf16[256,128]{1,0:T(8,128)(2,1)S(1)} %bitcast_convert_fusion.refs_0_), channel_id=1, source_target_pairs={{0,16},{4,20},{8,24},{12,28},{16,0},{20,4},{24,8},{28,12},{1,17},{... | collective-permute-start | bytes 196616 | tf_op jit(solution)/shard_map/ppermute | solution.py:319
  5.6 3.6 %collective-permute-done.refs_1_ = bf16[256,128]{1,0:T(8,128)(2,1)S(1)} collective-permute-done((bf16[256,128]{1,0:T(8,128)(2,1)S(1)}, bf16[256,128]{1,0:T(8,128)(2,1)S(1)}, u32[]{:S(2)}, u32[]{:S(2)}) %collective-permute-start) | collective-permute-done | bytes 65568 | tf_op jit(solution)/shard_map/ppermute | solution.py:319
  9.3 1.6 %collective-permute-start.3 = (bf16[512,128]{1,0:T(8,128)(2,1)S(1)}, bf16[512,128]{1,0:T(8,128)(2,1)S(1)}, u32[]{:S(2)}, u32[]{:S(2)}) collective-permute-start(bf16[512,128]{1,0:T(8,128)(2,1)S(1)} %pad_maximum_fusion), channel_id=1, source_target_pairs={{0,12},{4,8},{8,4},{12,0},{16,28},{20,24},{24,20},{28,16},{1,13},{... | collective-permute-start | bytes 393224 | tf_op jit(solution)/shard_map/ppermute | solution.py:319
  10.8 1.7 %collective-permute-start.2 = (bf16[512,128]{1,0:T(8,128)(2,1)S(1)}, bf16[512,128]{1,0:T(8,128)(2,1)S(1)}, u32[]{:S(2)}, u32[]{:S(2)}) collective-permute-start(bf16[512,128]{1,0:T(8,128)(2,1)S(1)} %pad_maximum_fusion), channel_id=1, source_target_pairs={{0,8},{4,12},{8,0},{12,4},{16,24},{20,28},{24,16},{28,20},{1,9},{5... | collective-permute-start | bytes 393224 | tf_op jit(solution)/shard_map/ppermute | solution.py:319
  12.5 0.3 collective-permute-start.1
  12.8 1.0 %subtract_add_fusion = s32[1024,24]{0,1:T(8,128)S(1)} fusion(s32[1024,24]{0,1:T(8,128)} %param.7, s32[]{:T(128)S(6)} %axis_index.15), kind=kLoop, calls=%fused_computation.10 | loop fusion | flops 835584 | bytes 196612 | tf_op jit(solution)/shard_map/add | solution.py:349
  13.9 0.2 copy.8
  14.1 0.3 reshape.23.ids_in
  14.4 0.0 copy-start
  14.4 1.6 %copy-done = f32[2,8,32768]{2,1,0:T(8,128)S(1)} copy-done((f32[2,8,32768]{2,1,0:T(8,128)S(1)}, f32[2,8,32768]{2,1,0:T(8,128)}, u32[]{:S(2)}) %copy-start) | copy-done | bytes 2097176
  16.0 2.6 %shard_map.77.gram = f32[16,128]{1,0:T(8,128)S(1)} custom-call(f32[2,8,32768]{2,1,0:T(8,128)S(1)} %copy-done), custom_call_target="tpu_custom_call" | custom-call | tf_op jit(solution)/shard_map/pallas_call | solution.py:351
  18.6 0.0 collective-permute-done.3.refs_4_
  18.6 0.0 collective-permute-done.2.refs_3_
  18.6 0.0 collective-permute-done.1.refs_2_
  18.7 15.8 %shard_map.78 = f32[24,128]{1,0:T(8,128)S(1)} custom-call(s32[24576]{0:T(1024)S(1)} %reshape.23.ids_in, bf16[1024,24,128]{2,1,0:T(8,128)(2,1)} %vals_in.3, f32[16,128]{1,0:T(8,128)S(1)} %shard_map.77.gram, bf16[256,128]{1,0:T(8,128)(2,1)S(1)} %bitcast_convert_fusion.refs_0_, bf16[256,128]{1,0:T(8,128)(2,1)S(1)} %collective-permute-done.refs_1_, ...), custom_call_target="tpu_custom_call" | custom-call | tf_op jit(solution)/shard_map/pallas_call | solution.py:365
  34.5 0.0 copy-start.1
  34.5 0.0 copy-start.2
  34.5 0.1 collective-permute-start.4
  34.6 1.2 %collective-permute-done.4 = f32[24,128]{1,0:T(8,128)S(1)} collective-permute-done((f32[24,128]{1,0:T(8,128)S(1)}, f32[24,128]{1,0:T(8,128)S(1)}, u32[]{:S(2)}, u32[]{:S(2)}) %collective-permute-start.4) | collective-permute-done | bytes 12320 | tf_op jit(solution)/shard_map/ppermute | solution.py:319
  35.8 1.8 %collective-permute-start.5 = (f32[24,128]{1,0:T(8,128)S(1)}, f32[24,128]{1,0:T(8,128)S(1)}, u32[]{:S(2)}, u32[]{:S(2)}) collective-permute-start(f32[24,128]{1,0:T(8,128)S(1)} %add.33), channel_id=1, source_target_pairs={{0,2},{1,3},{2,0},{3,1},{4,6},{5,7},{6,4},{7,5},{8,10},{9,11},{10,... | collective-permute-start | bytes 36872 | tf_op jit(solution)/shard_map/ppermute | solution.py:319
  37.5 1.9 %collective-permute-done.5 = f32[24,128]{1,0:T(8,128)S(1)} collective-permute-done((f32[24,128]{1,0:T(8,128)S(1)}, f32[24,128]{1,0:T(8,128)S(1)}, u32[]{:S(2)}, u32[]{:S(2)}) %collective-permute-start.5) | collective-permute-done | bytes 12320 | tf_op jit(solution)/shard_map/ppermute | solution.py:319
  39.5 0.0 copy-done.3
  39.5 19.8 %shard_map.79 = (f32[1024,128]{1,0:T(8,128)S(1)}, f32[1024,128]{1,0:T(8,128)S(1)}) custom-call(s32[24576]{0:T(1024)S(1)} %broadcast_multiply_fusion.ids_in, f32[1024]{0:T(1024)S(1)} %fusion.6.resid_in, bf16[1024,24,128]{2,1,0:T(8,128)(2,1)} %vals_in.3), custom_call_target="tpu_custom_call" | custom-call | tf_op jit(solution)/shard_map/pallas_call | solution.py:389
  59.4 1.8 %collective-permute-start.6 = (f16[1024,128]{1,0:T(8,128)(2,1)S(1)}, f16[1024,128]{1,0:T(8,128)(2,1)S(1)}, u32[]{:S(2)}, u32[]{:S(2)}) collective-permute-start(f16[1024,128]{1,0:T(8,128)(2,1)S(1)} %convert_element_type.22), channel_id=1, source_target_pairs={{0,4},{4,0},{8,12},{12,8},{16,20},{20,16},{24,28},{28,24},{1,5},{5... | collective-permute-start | bytes 786440 | tf_op jit(solution)/shard_map/ppermute | solution.py:319
  61.1 5.5 %collective-permute-done.6 = f16[1024,128]{1,0:T(8,128)(2,1)S(1)} collective-permute-done((f16[1024,128]{1,0:T(8,128)(2,1)S(1)}, f16[1024,128]{1,0:T(8,128)(2,1)S(1)}, u32[]{:S(2)}, u32[]{:S(2)}) %collective-permute-start.6) | collective-permute-done | bytes 262176 | tf_op jit(solution)/shard_map/ppermute | solution.py:319
  66.7 0.1 convert_add_fusion
  66.8 0.6 collective-permute-start.7
  67.4 4.4 %collective-permute-done.7 = f16[512,128]{1,0:T(8,128)(2,1)S(1)} collective-permute-done((f16[512,128]{1,0:T(8,128)(2,1)S(1)}, f16[512,128]{1,0:T(8,128)(2,1)S(1)}, u32[]{:S(2)}, u32[]{:S(2)}) %collective-permute-start.7) | collective-permute-done | bytes 131104 | tf_op jit(solution)/shard_map/ppermute | solution.py:319
  71.8 2.1 %collective-permute-start.8 = (f16[256,128]{1,0:T(8,128)(2,1)S(1)}, f16[256,128]{1,0:T(8,128)(2,1)S(1)}, u32[]{:S(2)}, u32[]{:S(2)}) collective-permute-start(f16[256,128]{1,0:T(8,128)(2,1)S(1)} %get-tuple-element.18), channel_id=1, source_target_pairs={{0,16},{4,20},{8,24},{12,28},{16,0},{20,4},{24,8},{28,12},{1,17},{... | collective-permute-start | bytes 196616 | tf_op jit(solution)/shard_map/ppermute | solution.py:319
  74.0 3.8 %collective-permute-done.8 = f16[256,128]{1,0:T(8,128)(2,1)S(1)} collective-permute-done((f16[256,128]{1,0:T(8,128)(2,1)S(1)}, f16[256,128]{1,0:T(8,128)(2,1)S(1)}, u32[]{:S(2)}, u32[]{:S(2)}) %collective-permute-start.8) | collective-permute-done | bytes 65568 | tf_op jit(solution)/shard_map/ppermute | solution.py:319
  77.8 0.0 copy-done.1
  77.8 0.0 copy-done.2
  77.8 1.2 %shard_map.80 = (f32[256,128]{1,0:T(8,128)}, f32[256,128]{1,0:T(8,128)S(1)}, f32[32,128]{1,0:T(8,128)S(1)}) custom-call(f32[256,128]{1,0:T(8,128)S(1)} %get-tuple-element.19.keep, f32[256,128]{1,0:T(8,128)S(1)} %convert_element_type.25.recv, f32[16,128]{1,0:T(8,128)S(1)} %slice.39.gram, f32[256,128]{1,0:T(8,128)S(1)} %bitcast.8, f32[2,8,32768]{2,1,0:T(8,128)S(1)} %copy-done.1), custom_call_target="tpu_custom_call" | custom-call | tf_op jit(solution)/shard_map/pallas_call | solution.py:413
  79.0 1.7 %collective-permute-start.9 = (f32[32,128]{1,0:T(8,128)S(1)}, f32[32,128]{1,0:T(8,128)S(1)}, u32[]{:S(2)}, u32[]{:S(2)}) collective-permute-start(f32[32,128]{1,0:T(8,128)S(1)} %get-tuple-element.15), channel_id=1, source_target_pairs={{0,4},{4,0},{8,12},{12,8},{16,20},{20,16},{24,28},{28,24},{1,5},{5... | collective-permute-start | bytes 49160 | tf_op jit(solution)/shard_map/ppermute | solution.py:319
  80.7 2.1 %collective-permute-done.9 = f32[32,128]{1,0:T(8,128)S(1)} collective-permute-done((f32[32,128]{1,0:T(8,128)S(1)}, f32[32,128]{1,0:T(8,128)S(1)}, u32[]{:S(2)}, u32[]{:S(2)}) %collective-permute-start.9) | collective-permute-done | bytes 16416 | tf_op jit(solution)/shard_map/ppermute | solution.py:319
  82.7 0.4 collective-permute-start.10
  83.2 3.3 %collective-permute-done.10 = f32[32,128]{1,0:T(8,128)S(1)} collective-permute-done((f32[32,128]{1,0:T(8,128)S(1)}, f32[32,128]{1,0:T(8,128)S(1)}, u32[]{:S(2)}, u32[]{:S(2)}) %collective-permute-start.10) | collective-permute-done | bytes 16416 | tf_op jit(solution)/shard_map/ppermute | solution.py:319
  86.5 1.5 %collective-permute-start.11 = (f32[32,128]{1,0:T(8,128)S(1)}, f32[32,128]{1,0:T(8,128)S(1)}, u32[]{:S(2)}, u32[]{:S(2)}) collective-permute-start(f32[32,128]{1,0:T(8,128)S(1)} %add.39), channel_id=1, source_target_pairs={{0,16},{4,20},{8,24},{12,28},{16,0},{20,4},{24,8},{28,12},{1,17},{... | collective-permute-start | bytes 49160 | tf_op jit(solution)/shard_map/ppermute | solution.py:319
  88.0 3.3 %collective-permute-done.11 = f32[32,128]{1,0:T(8,128)S(1)} collective-permute-done((f32[32,128]{1,0:T(8,128)S(1)}, f32[32,128]{1,0:T(8,128)S(1)}, u32[]{:S(2)}, u32[]{:S(2)}) %collective-permute-start.11) | collective-permute-done | bytes 16416 | tf_op jit(solution)/shard_map/ppermute | solution.py:319
  91.3 0.0 collective-permute-start.12
  91.3 1.2 %collective-permute-done.12 = f32[16,128]{1,0:T(8,128)S(1)} collective-permute-done((f32[16,128]{1,0:T(8,128)S(1)}, f32[16,128]{1,0:T(8,128)S(1)}, u32[]{:S(2)}, u32[]{:S(2)}) %collective-permute-start.12) | collective-permute-done | bytes 8224 | tf_op jit(solution)/shard_map/ppermute | solution.py:319
  92.5 1.6 %collective-permute-start.13 = (f32[16,128]{1,0:T(8,128)S(1)}, f32[16,128]{1,0:T(8,128)S(1)}, u32[]{:S(2)}, u32[]{:S(2)}) collective-permute-start(f32[16,128]{1,0:T(8,128)S(1)} %get-tuple-element.20.dots), channel_id=1, source_target_pairs={{0,2},{1,3},{2,0},{3,1},{4,6},{5,7},{6,4},{7,5},{8,10},{9,11},{10,... | collective-permute-start | bytes 24584 | tf_op jit(solution)/shard_map/ppermute | solution.py:319
  94.7 0.8 shard_map.81.coef
  95.5 0.6 collective-permute-done.13.recv
  96.1 1.3 %shard_map.82 = f32[256,128]{1,0:T(8,128)} custom-call(f32[1]{0:T(128)S(6)} %copy.9.steps, f32[24,128]{1,0:T(8,128)S(1)} %shard_map.81.coef, f32[16,128]{1,0:T(8,128)S(1)} %get-tuple-element.20.dots, f32[16,128]{1,0:T(8,128)S(1)} %collective-permute-done.13.recv, f32[256,128]{1,0:T(8,128)S(1)} %get-tuple-element.16.grad, f32[256,128]{1,0:T(8,128)S(1)} %bitcast.9, ...), custom_call_target="tpu_custom_call" | custom-call | tf_op jit(solution)/shard_map/pallas_call | solution.py:442
  (16 shorter events, 0.2 us)
Async XLA Ops:
  0.6 38.8 %copy-start.3 = (s32[1024]{0:T(1024)S(1)}, s32[1024]{0:T(1024)}, u32[]{:S(2)}) copy-start(s32[1024]{0:T(1024)} %param.8) | copy-start | bytes 12292
  1.6 7.7 %collective-permute-start = (bf16[256,128]{1,0:T(8,128)(2,1)S(1)}, bf16[256,128]{1,0:T(8,128)(2,1)S(1)}, u32[]{:S(2)}, u32[]{:S(2)}) collective-permute-start(bf16[256,128]{1,0:T(8,128)(2,1)S(1)} %bitcast_convert_fusion.refs_0_), channel_id=1, source_target_pairs={{0,16},{4,20},{8,24},{12,28},{16,0},{20,4},{24,8},{28,12},{1,17},{... | collective-permute-start | bytes 196616 | tf_op jit(solution)/shard_map/ppermute | solution.py:319
  9.3 9.3 %collective-permute-start.3 = (bf16[512,128]{1,0:T(8,128)(2,1)S(1)}, bf16[512,128]{1,0:T(8,128)(2,1)S(1)}, u32[]{:S(2)}, u32[]{:S(2)}) collective-permute-start(bf16[512,128]{1,0:T(8,128)(2,1)S(1)} %pad_maximum_fusion), channel_id=1, source_target_pairs={{0,12},{4,8},{8,4},{12,0},{16,28},{20,24},{24,20},{28,16},{1,13},{... | collective-permute-start | bytes 393224 | tf_op jit(solution)/shard_map/ppermute | solution.py:319
  10.8 7.8 %collective-permute-start.2 = (bf16[512,128]{1,0:T(8,128)(2,1)S(1)}, bf16[512,128]{1,0:T(8,128)(2,1)S(1)}, u32[]{:S(2)}, u32[]{:S(2)}) collective-permute-start(bf16[512,128]{1,0:T(8,128)(2,1)S(1)} %pad_maximum_fusion), channel_id=1, source_target_pairs={{0,8},{4,12},{8,0},{12,4},{16,24},{20,28},{24,16},{28,20},{1,9},{5... | collective-permute-start | bytes 393224 | tf_op jit(solution)/shard_map/ppermute | solution.py:319
  12.5 6.1 %collective-permute-start.1 = (bf16[512,128]{1,0:T(8,128)(2,1)S(1)}, bf16[512,128]{1,0:T(8,128)(2,1)S(1)}, u32[]{:S(2)}, u32[]{:S(2)}) collective-permute-start(bf16[512,128]{1,0:T(8,128)(2,1)S(1)} %pad_maximum_fusion), channel_id=1, source_target_pairs={{0,4},{4,0},{8,12},{12,8},{16,20},{20,16},{24,28},{28,24},{1,5},{5... | collective-permute-start | bytes 393224 | tf_op jit(solution)/shard_map/ppermute | solution.py:319
  14.4 1.6 %copy-start = (f32[2,8,32768]{2,1,0:T(8,128)S(1)}, f32[2,8,32768]{2,1,0:T(8,128)}, u32[]{:S(2)}) copy-start(f32[2,8,32768]{2,1,0:T(8,128)} %hist.4) | copy-start | bytes 6291460
  34.5 43.3 %copy-start.1 = (f32[2,8,32768]{2,1,0:T(8,128)S(1)}, f32[2,8,32768]{2,1,0:T(8,128)}, u32[]{:S(2)}) copy-start(f32[2,8,32768]{2,1,0:T(8,128)} %hist.4) | copy-start | bytes 6291460
  34.5 43.3 %copy-start.2 = (f32[32768]{0:T(1024)S(1)}, f32[32768]{0:T(1024)}, u32[]{:S(2)}) copy-start(f32[32768]{0:T(1024)} %param.9) | copy-start | bytes 393220
  34.5 1.2 %collective-permute-start.4 = (f32[24,128]{1,0:T(8,128)S(1)}, f32[24,128]{1,0:T(8,128)S(1)}, u32[]{:S(2)}, u32[]{:S(2)}) collective-permute-start(f32[24,128]{1,0:T(8,128)S(1)} %shard_map.78), channel_id=1, source_target_pairs={{0,1},{1,0},{2,3},{3,2},{4,5},{5,4},{6,7},{7,6},{8,9},{9,8},{10,11... | collective-permute-start | bytes 36872 | tf_op jit(solution)/shard_map/ppermute | solution.py:319
  35.8 3.7 %collective-permute-start.5 = (f32[24,128]{1,0:T(8,128)S(1)}, f32[24,128]{1,0:T(8,128)S(1)}, u32[]{:S(2)}, u32[]{:S(2)}) collective-permute-start(f32[24,128]{1,0:T(8,128)S(1)} %add.33), channel_id=1, source_target_pairs={{0,2},{1,3},{2,0},{3,1},{4,6},{5,7},{6,4},{7,5},{8,10},{9,11},{10,... | collective-permute-start | bytes 36872 | tf_op jit(solution)/shard_map/ppermute | solution.py:319
  59.4 7.3 %collective-permute-start.6 = (f16[1024,128]{1,0:T(8,128)(2,1)S(1)}, f16[1024,128]{1,0:T(8,128)(2,1)S(1)}, u32[]{:S(2)}, u32[]{:S(2)}) collective-permute-start(f16[1024,128]{1,0:T(8,128)(2,1)S(1)} %convert_element_type.22), channel_id=1, source_target_pairs={{0,4},{4,0},{8,12},{12,8},{16,20},{20,16},{24,28},{28,24},{1,5},{5... | collective-permute-start | bytes 786440 | tf_op jit(solution)/shard_map/ppermute | solution.py:319
  66.8 5.0 %collective-permute-start.7 = (f16[512,128]{1,0:T(8,128)(2,1)S(1)}, f16[512,128]{1,0:T(8,128)(2,1)S(1)}, u32[]{:S(2)}, u32[]{:S(2)}) collective-permute-start(f16[512,128]{1,0:T(8,128)(2,1)S(1)} %slice_convert_fusion), channel_id=1, source_target_pairs={{0,8},{4,12},{8,0},{12,4},{16,24},{20,28},{24,16},{28,20},{1,9},{5... | collective-permute-start | bytes 393224 | tf_op jit(solution)/shard_map/ppermute | solution.py:319
  71.8 5.9 %collective-permute-start.8 = (f16[256,128]{1,0:T(8,128)(2,1)S(1)}, f16[256,128]{1,0:T(8,128)(2,1)S(1)}, u32[]{:S(2)}, u32[]{:S(2)}) collective-permute-start(f16[256,128]{1,0:T(8,128)(2,1)S(1)} %get-tuple-element.18), channel_id=1, source_target_pairs={{0,16},{4,20},{8,24},{12,28},{16,0},{20,4},{24,8},{28,12},{1,17},{... | collective-permute-start | bytes 196616 | tf_op jit(solution)/shard_map/ppermute | solution.py:319
  79.0 3.7 %collective-permute-start.9 = (f32[32,128]{1,0:T(8,128)S(1)}, f32[32,128]{1,0:T(8,128)S(1)}, u32[]{:S(2)}, u32[]{:S(2)}) collective-permute-start(f32[32,128]{1,0:T(8,128)S(1)} %get-tuple-element.15), channel_id=1, source_target_pairs={{0,4},{4,0},{8,12},{12,8},{16,20},{20,16},{24,28},{28,24},{1,5},{5... | collective-permute-start | bytes 49160 | tf_op jit(solution)/shard_map/ppermute | solution.py:319
  82.7 3.7 %collective-permute-start.10 = (f32[32,128]{1,0:T(8,128)S(1)}, f32[32,128]{1,0:T(8,128)S(1)}, u32[]{:S(2)}, u32[]{:S(2)}) collective-permute-start(f32[32,128]{1,0:T(8,128)S(1)} %add.38), channel_id=1, source_target_pairs={{0,8},{4,12},{8,0},{12,4},{16,24},{20,28},{24,16},{28,20},{1,9},{5... | collective-permute-start | bytes 49160 | tf_op jit(solution)/shard_map/ppermute | solution.py:319
  86.5 4.8 %collective-permute-start.11 = (f32[32,128]{1,0:T(8,128)S(1)}, f32[32,128]{1,0:T(8,128)S(1)}, u32[]{:S(2)}, u32[]{:S(2)}) collective-permute-start(f32[32,128]{1,0:T(8,128)S(1)} %add.39), channel_id=1, source_target_pairs={{0,16},{4,20},{8,24},{12,28},{16,0},{20,4},{24,8},{28,12},{1,17},{... | collective-permute-start | bytes 49160 | tf_op jit(solution)/shard_map/ppermute | solution.py:319
  91.3 1.2 %collective-permute-start.12 = (f32[16,128]{1,0:T(8,128)S(1)}, f32[16,128]{1,0:T(8,128)S(1)}, u32[]{:S(2)}, u32[]{:S(2)}) collective-permute-start(f32[16,128]{1,0:T(8,128)S(1)} %slice.41), channel_id=1, source_target_pairs={{0,1},{1,0},{2,3},{3,2},{4,5},{5,4},{6,7},{7,6},{8,9},{9,8},{10,11... | collective-permute-start | bytes 24584 | tf_op jit(solution)/shard_map/ppermute | solution.py:319
  92.5 3.7 %collective-permute-start.13 = (f32[16,128]{1,0:T(8,128)S(1)}, f32[16,128]{1,0:T(8,128)S(1)}, u32[]{:S(2)}, u32[]{:S(2)}) collective-permute-start(f32[16,128]{1,0:T(8,128)S(1)} %get-tuple-element.20.dots), channel_id=1, source_target_pairs={{0,2},{1,3},{2,0},{3,1},{4,6},{5,7},{6,4},{7,5},{8,10},{9,11},{10,... | collective-permute-start | bytes 24584 | tf_op jit(solution)/shard_map/ppermute | solution.py:319

commit v6 on v5

--- a/solution.py
+++ b/solution.py
@@ -162,8 +162,8 @@
     out[lines : lines + gram.shape[0], :] = gram[...]
 
 
-def scatter_body(ids_in, resid_in, vals_in, *refs, order, owned):
-    n_out = 2
+def scatter_body(ids_in, resid_in, vals_in, *refs, orders, owned):
+    n_out = len(orders)
     outs, accs = refs[:n_out], refs[n_out:-5]
     resid, resid_sem, vals, ids, sems = refs[-5:]
     resid_copy = pltpu.make_async_copy(resid_in, resid, resid_sem)
@@ -203,11 +203,9 @@
 
     run_chunks(srcs, dsts, sems, count // unroll, group)
 
-    half = len(order) // 2
-    for i, p in enumerate(order):
-        out = outs[0] if i < half else outs[1]
-
-        def fold(j, carry, p=p, out=out, base=(i % half) * owned):
+    for i, p, out in [(i, p, out) for order, out in zip(orders, outs) for i, p in enumerate(order)]:
+
+        def fold(j, carry, p=p, out=out, base=i * owned):
             tiles = []
             for i in range(SUB):
                 at = pl.ds(pl.multiple_of((p * owned + j * SUB + i) * SUB, SUB), SUB)
@@ -377,20 +375,21 @@
     gram_rows = packed[lines:]
 
     bits = reduce_bits(n_dp)
+    direct = [k for k in (1, 2, 3) if k < n_dp]
     wanted = [0]
-    for b in reversed(bits):
+    for b in reversed(bits[2:]):
         wanted = [p ^ b for p in wanted] + wanted
-    slots = [place[p] for p in wanted]
+    slots = [[place[p ^ k] for p in wanted] for k in direct + [0]]
 
     acc_mib = SUB * table_mib
     room = (60 * 1024) / 1024 - mib(values) - table_mib - 6
     n_acc = max(1, min(MAX_ACC, int(room // acc_mib)))
-    half = n_dp // 2 * owned
-    send, keep = pl.pallas_call(
-        functools.partial(scatter_body, order=slots, owned=owned),
-        out_shape=[jax.ShapeDtypeStruct((half, width), F32)] * 2,
+    part = len(wanted) * owned
+    *sends, keep = pl.pallas_call(
+        functools.partial(scatter_body, orders=slots, owned=owned),
+        out_shape=[jax.ShapeDtypeStruct((part, width), F32)] * len(slots),
         in_specs=[any_spec(), any_spec(), hbm_spec()],
-        out_specs=[vmem_spec(), vmem_spec()],
+        out_specs=[vmem_spec()] * len(slots),
         scratch_shapes=[pltpu.VMEM((blocks * SUB, width), F32)] * n_acc
         + [pltpu.SMEM((count,), F32), pltpu.SemaphoreType.DMA]
         + streams,
@@ -400,15 +399,19 @@
     scale, bound = 1.0, VALUE_MAX * count * active * max(1, n_dp // 2)
     while bound * scale > 60000:
         scale /= 2
-    for b in bits:
-        sent = send if scale == 1.0 else send * scale
-        came = xor_permute(sent.astype(jnp.float16), "dp", n_dp, b).astype(F32)
-        came = came if scale == 1.0 else came / scale
-        if b == bits[-1]:
-            break
-        total = keep + came
+
+    def partner(x, k):
+        sent = x if scale == 1.0 else x * scale
+        came = xor_permute(sent.astype(jnp.float16), "dp", n_dp, k).astype(F32)
+        return came if scale == 1.0 else came / scale
+
+    came = [partner(send, k) for send, k in zip(sends, direct)]
+    for b in bits[2:]:
+        total = functools.reduce(jnp.add, came, keep)
         cut = total.shape[0] // 2
-        send, keep = total[:cut], total[cut:]
+        came = [partner(total[:cut], b)]
+        keep = total[cut:]
+    came = functools.reduce(jnp.add, came)
 
     result, grad, dots = pl.pallas_call(
         dots_body,

time: 97.7 us -> 94 us (0.962)
  waiting for transfers between devices: 30.9 us -> 26.6 us
    ppermute x14 -> x15, waiting for transfers between devices: 30.9 us -> 26.6 us  [xor_permute(): return lax.ppermute(x, axis, [(i, i ^ k) for i in range(n)])]
    ppermute x14 -> x15, starting transfers between devices: 19.2 us -> 19.7 us  [xor_permute(): return lax.ppermute(x, axis, [(i, i ^ k) for i in range(n)])]
  transfers between devices with their start and end apart: 14 -> 15, of which waited for: 11 -> 12; matrix products, arithmetic and copies ran while one was open for 2% -> 2% of each run, Pallas kernels for 3% -> 4%
where the time goes in v6:
time: 94 us; the launch traced here: 93.8 us
  Pallas kernels  41.8 us (44%)
  waiting for transfers between devices  26.6 us (28%)
  starting transfers between devices  19.7 us (21%)
  local copies, waits for them, and re-layouts  2.13 us (2%)
  other arithmetic  2.13 us (2%)
  between operations  1.47 us (2%)
    ppermute x15, waiting for transfers between devices, xor_permute(): return lax.ppermute(x, axis, [(i, i ^ k) for i in range(n)])  26.6 us
    pallas_call x1, Pallas kernels, local(): pl.pallas_call(functools.partial(scatter_body, orders=slots, owned=owned)...  20 us
    ppermute x15, starting transfers between devices, xor_permute(): return lax.ppermute(x, axis, [(i, i ^ k) for i in range(n)])  19.7 us
    pallas_call x1, Pallas kernels, local(): pl.pallas_call(gather_body, out_shape=jax.ShapeDtypeStruct((lines + 2 * p...  15.8 us
    pallas_call x1, Pallas kernels, local(): pl.pallas_call(gram_body, out_shape=jax.ShapeDtypeStruct((2 * pairs, widt...  2.64 us
  transfers between devices with their start and end apart: 15, of which 12 were waited for; matrix products, arithmetic and copies ran while one was open for 2% of the time, Pallas kernels for 4%

profile of v6, /device:TPU:0, one launch (start us, length us, event | category | flops | bytes accessed | tf_op | source)
XLA Modules:
  0.0 93.8 jit_solution(12539595021471723776)
XLA Ops:
  0.6 0.0 copy-start.3
  0.6 0.9 bitcast_convert_fusion.refs_0_
  1.6 4.1 %collective-permute-start = (bf16[256,128]{1,0:T(8,128)(2,1)S(1)}, bf16[256,128]{1,0:T(8,128)(2,1)S(1)}, u32[]{:S(2)}, u32[]{:S(2)}) collective-permute-start(bf16[256,128]{1,0:T(8,128)(2,1)S(1)} %bitcast_convert_fusion.refs_0_), channel_id=1, source_target_pairs={{0,16},{4,20},{8,24},{12,28},{16,0},{20,4},{24,8},{28,12},{1,17},{... | collective-permute-start | bytes 196616 | tf_op jit(solution)/shard_map/ppermute | solution.py:317
  5.6 3.6 %collective-permute-done.refs_1_ = bf16[256,128]{1,0:T(8,128)(2,1)S(1)} collective-permute-done((bf16[256,128]{1,0:T(8,128)(2,1)S(1)}, bf16[256,128]{1,0:T(8,128)(2,1)S(1)}, u32[]{:S(2)}, u32[]{:S(2)}) %collective-permute-start) | collective-permute-done | bytes 65568 | tf_op jit(solution)/shard_map/ppermute | solution.py:317
  9.3 1.6 %collective-permute-start.3 = (bf16[512,128]{1,0:T(8,128)(2,1)S(1)}, bf16[512,128]{1,0:T(8,128)(2,1)S(1)}, u32[]{:S(2)}, u32[]{:S(2)}) collective-permute-start(bf16[512,128]{1,0:T(8,128)(2,1)S(1)} %pad_maximum_fusion), channel_id=1, source_target_pairs={{0,12},{4,8},{8,4},{12,0},{16,28},{20,24},{24,20},{28,16},{1,13},{... | collective-permute-start | bytes 393224 | tf_op jit(solution)/shard_map/ppermute | solution.py:317
  10.8 1.7 %collective-permute-start.2 = (bf16[512,128]{1,0:T(8,128)(2,1)S(1)}, bf16[512,128]{1,0:T(8,128)(2,1)S(1)}, u32[]{:S(2)}, u32[]{:S(2)}) collective-permute-start(bf16[512,128]{1,0:T(8,128)(2,1)S(1)} %pad_maximum_fusion), channel_id=1, source_target_pairs={{0,8},{4,12},{8,0},{12,4},{16,24},{20,28},{24,16},{28,20},{1,9},{5... | collective-permute-start | bytes 393224 | tf_op jit(solution)/shard_map/ppermute | solution.py:317
  12.5 0.3 collective-permute-start.1
  12.8 1.0 %subtract_add_fusion = s32[1024,24]{0,1:T(8,128)S(1)} fusion(s32[1024,24]{0,1:T(8,128)} %param.7, s32[]{:T(128)S(6)} %axis_index.15), kind=kLoop, calls=%fused_computation.8 | loop fusion | flops 835584 | bytes 196612 | tf_op jit(solution)/shard_map/add | solution.py:347
  13.9 0.2 copy.8
  14.1 0.3 reshape.23.ids_in
  14.4 0.0 copy-start
  14.4 1.6 %copy-done = f32[2,8,32768]{2,1,0:T(8,128)S(1)} copy-done((f32[2,8,32768]{2,1,0:T(8,128)S(1)}, f32[2,8,32768]{2,1,0:T(8,128)}, u32[]{:S(2)}) %copy-start) | copy-done | bytes 2097176
  16.0 2.6 %shard_map.77.gram = f32[16,128]{1,0:T(8,128)S(1)} custom-call(f32[2,8,32768]{2,1,0:T(8,128)S(1)} %copy-done), custom_call_target="tpu_custom_call" | custom-call | tf_op jit(solution)/shard_map/pallas_call | solution.py:349
  18.6 0.0 collective-permute-done.3.refs_4_
  18.6 0.0 collective-permute-done.2.refs_3_
  18.6 0.0 collective-permute-done.1.refs_2_
  18.7 15.8 %shard_map.78 = f32[24,128]{1,0:T(8,128)S(1)} custom-call(s32[24576]{0:T(1024)S(1)} %reshape.23.ids_in, bf16[1024,24,128]{2,1,0:T(8,128)(2,1)} %vals_in.3, f32[16,128]{1,0:T(8,128)S(1)} %shard_map.77.gram, bf16[256,128]{1,0:T(8,128)(2,1)S(1)} %bitcast_convert_fusion.refs_0_, bf16[256,128]{1,0:T(8,128)(2,1)S(1)} %collective-permute-done.refs_1_, ...), custom_call_target="tpu_custom_call" | custom-call | tf_op jit(solution)/shard_map/pallas_call | solution.py:363
  34.5 0.0 copy-start.1
  34.5 0.0 copy-start.2
  34.5 0.1 collective-permute-start.4
  34.6 1.2 %collective-permute-done.4 = f32[24,128]{1,0:T(8,128)S(1)} collective-permute-done((f32[24,128]{1,0:T(8,128)S(1)}, f32[24,128]{1,0:T(8,128)S(1)}, u32[]{:S(2)}, u32[]{:S(2)}) %collective-permute-start.4) | collective-permute-done | bytes 12320 | tf_op jit(solution)/shard_map/ppermute | solution.py:317
  35.8 1.8 %collective-permute-start.5 = (f32[24,128]{1,0:T(8,128)S(1)}, f32[24,128]{1,0:T(8,128)S(1)}, u32[]{:S(2)}, u32[]{:S(2)}) collective-permute-start(f32[24,128]{1,0:T(8,128)S(1)} %add.36), channel_id=1, source_target_pairs={{0,2},{1,3},{2,0},{3,1},{4,6},{5,7},{6,4},{7,5},{8,10},{9,11},{10,... | collective-permute-start | bytes 36872 | tf_op jit(solution)/shard_map/ppermute | solution.py:317
  37.5 1.9 %collective-permute-done.5 = f32[24,128]{1,0:T(8,128)S(1)} collective-permute-done((f32[24,128]{1,0:T(8,128)S(1)}, f32[24,128]{1,0:T(8,128)S(1)}, u32[]{:S(2)}, u32[]{:S(2)}) %collective-permute-start.5) | collective-permute-done | bytes 12320 | tf_op jit(solution)/shard_map/ppermute | solution.py:317
  39.5 0.0 copy-done.3
  39.5 20.0 %shard_map.79 = (f32[512,128]{1,0:T(8,128)S(1)}, f32[512,128]{1,0:T(8,128)S(1)}, f32[512,128]{1,0:T(8,128)S(1)}, f32[512,128]{1,0:T(8,128)S(1)}) custom-call(s32[24576]{0:T(1024)S(1)} %broadcast_multiply_fusion.ids_in, f32[1024]{0:T(1024)S(1)} %fusion.6.resid_in, bf16[1024,24,128]{2,1,0:T(8,128)(2,1)} %vals_in.3), custom_call_target="tpu_custom_call" | custom-call | tf_op jit(solution)/shard_map/pallas_call | solution.py:388
  59.6 1.6 %collective-permute-start.8 = (f16[512,128]{1,0:T(8,128)(2,1)S(1)}, f16[512,128]{1,0:T(8,128)(2,1)S(1)}, u32[]{:S(2)}, u32[]{:S(2)}) collective-permute-start(f16[512,128]{1,0:T(8,128)(2,1)S(1)} %convert_element_type.34), channel_id=1, source_target_pairs={{0,12},{4,8},{8,4},{12,0},{16,28},{20,24},{24,20},{28,16},{1,13},{... | collective-permute-start | bytes 393224 | tf_op jit(solution)/shard_map/ppermute | solution.py:317
  61.2 1.7 %collective-permute-start.7 = (f16[512,128]{1,0:T(8,128)(2,1)S(1)}, f16[512,128]{1,0:T(8,128)(2,1)S(1)}, u32[]{:S(2)}, u32[]{:S(2)}) collective-permute-start(f16[512,128]{1,0:T(8,128)(2,1)S(1)} %convert_element_type.32), channel_id=1, source_target_pairs={{0,8},{4,12},{8,0},{12,4},{16,24},{20,28},{24,16},{28,20},{1,9},{5... | collective-permute-start | bytes 393224 | tf_op jit(solution)/shard_map/ppermute | solution.py:317
  62.8 0.3 collective-permute-start.6
  63.2 3.3 %collective-permute-done.8 = f16[512,128]{1,0:T(8,128)(2,1)S(1)} collective-permute-done((f16[512,128]{1,0:T(8,128)(2,1)S(1)}, f16[512,128]{1,0:T(8,128)(2,1)S(1)}, u32[]{:S(2)}, u32[]{:S(2)}) %collective-permute-start.8) | collective-permute-done | bytes 131104 | tf_op jit(solution)/shard_map/ppermute | solution.py:317
  66.5 1.5 %collective-permute-done.7 = f16[512,128]{1,0:T(8,128)(2,1)S(1)} collective-permute-done((f16[512,128]{1,0:T(8,128)(2,1)S(1)}, f16[512,128]{1,0:T(8,128)(2,1)S(1)}, u32[]{:S(2)}, u32[]{:S(2)}) %collective-permute-start.7) | collective-permute-done | bytes 131104 | tf_op jit(solution)/shard_map/ppermute | solution.py:317
  68.0 0.1 collective-permute-done.6
  68.1 0.1 convert_add_fusion
  68.2 2.1 %collective-permute-start.9 = (f16[256,128]{1,0:T(8,128)(2,1)S(1)}, f16[256,128]{1,0:T(8,128)(2,1)S(1)}, u32[]{:S(2)}, u32[]{:S(2)}) collective-permute-start(f16[256,128]{1,0:T(8,128)(2,1)S(1)} %get-tuple-element.22), channel_id=1, source_target_pairs={{0,16},{4,20},{8,24},{12,28},{16,0},{20,4},{24,8},{28,12},{1,17},{... | collective-permute-start | bytes 196616 | tf_op jit(solution)/shard_map/ppermute | solution.py:317
  70.3 3.9 %collective-permute-done.9 = f16[256,128]{1,0:T(8,128)(2,1)S(1)} collective-permute-done((f16[256,128]{1,0:T(8,128)(2,1)S(1)}, f16[256,128]{1,0:T(8,128)(2,1)S(1)}, u32[]{:S(2)}, u32[]{:S(2)}) %collective-permute-start.9) | collective-permute-done | bytes 65568 | tf_op jit(solution)/shard_map/ppermute | solution.py:317
  74.1 0.0 copy-done.1
  74.2 1.2 %shard_map.80 = (f32[256,128]{1,0:T(8,128)}, f32[256,128]{1,0:T(8,128)S(1)}, f32[32,128]{1,0:T(8,128)S(1)}) custom-call(f32[256,128]{1,0:T(8,128)S(1)} %get-tuple-element.23.keep, f32[256,128]{1,0:T(8,128)S(1)} %convert_element_type.36.recv, f32[16,128]{1,0:T(8,128)S(1)} %slice.28.gram, f32[256,128]{1,0:T(8,128)S(1)} %bitcast.8, f32[2,8,32768]{2,1,0:T(8,128)S(1)} %copy-done.1), custom_call_target="tpu_custom_call" | custom-call | tf_op jit(solution)/shard_map/pallas_call | solution.py:416
  75.3 1.4 %collective-permute-start.10 = (f32[32,128]{1,0:T(8,128)S(1)}, f32[32,128]{1,0:T(8,128)S(1)}, u32[]{:S(2)}, u32[]{:S(2)}) collective-permute-start(f32[32,128]{1,0:T(8,128)S(1)} %get-tuple-element.19), channel_id=1, source_target_pairs={{0,4},{4,0},{8,12},{12,8},{16,20},{20,16},{24,28},{28,24},{1,5},{5... | collective-permute-start | bytes 49160 | tf_op jit(solution)/shard_map/ppermute | solution.py:317
  76.8 2.3 %collective-permute-done.10 = f32[32,128]{1,0:T(8,128)S(1)} collective-permute-done((f32[32,128]{1,0:T(8,128)S(1)}, f32[32,128]{1,0:T(8,128)S(1)}, u32[]{:S(2)}, u32[]{:S(2)}) %collective-permute-start.10) | collective-permute-done | bytes 16416 | tf_op jit(solution)/shard_map/ppermute | solution.py:317
  79.1 0.2 collective-permute-start.11
  79.3 3.5 %collective-permute-done.11 = f32[32,128]{1,0:T(8,128)S(1)} collective-permute-done((f32[32,128]{1,0:T(8,128)S(1)}, f32[32,128]{1,0:T(8,128)S(1)}, u32[]{:S(2)}, u32[]{:S(2)}) %collective-permute-start.11) | collective-permute-done | bytes 16416 | tf_op jit(solution)/shard_map/ppermute | solution.py:317
  82.8 1.4 %collective-permute-start.12 = (f32[32,128]{1,0:T(8,128)S(1)}, f32[32,128]{1,0:T(8,128)S(1)}, u32[]{:S(2)}, u32[]{:S(2)}) collective-permute-start(f32[32,128]{1,0:T(8,128)S(1)} %add.43), channel_id=1, source_target_pairs={{0,16},{4,20},{8,24},{12,28},{16,0},{20,4},{24,8},{28,12},{1,17},{... | collective-permute-start | bytes 49160 | tf_op jit(solution)/shard_map/ppermute | solution.py:317
  84.3 3.4 %collective-permute-done.12 = f32[32,128]{1,0:T(8,128)S(1)} collective-permute-done((f32[32,128]{1,0:T(8,128)S(1)}, f32[32,128]{1,0:T(8,128)S(1)}, u32[]{:S(2)}, u32[]{:S(2)}) %collective-permute-start.12) | collective-permute-done | bytes 16416 | tf_op jit(solution)/shard_map/ppermute | solution.py:317
  87.6 0.0 collective-permute-start.13
  87.6 1.2 %collective-permute-done.13 = f32[16,128]{1,0:T(8,128)S(1)} collective-permute-done((f32[16,128]{1,0:T(8,128)S(1)}, f32[16,128]{1,0:T(8,128)S(1)}, u32[]{:S(2)}, u32[]{:S(2)}) %collective-permute-start.13) | collective-permute-done | bytes 8224 | tf_op jit(solution)/shard_map/ppermute | solution.py:317
  88.8 1.5 %collective-permute-start.14 = (f32[16,128]{1,0:T(8,128)S(1)}, f32[16,128]{1,0:T(8,128)S(1)}, u32[]{:S(2)}, u32[]{:S(2)}) collective-permute-start(f32[16,128]{1,0:T(8,128)S(1)} %get-tuple-element.24.dots), channel_id=1, source_target_pairs={{0,2},{1,3},{2,0},{3,1},{4,6},{5,7},{6,4},{7,5},{8,10},{9,11},{10,... | collective-permute-start | bytes 24584 | tf_op jit(solution)/shard_map/ppermute | solution.py:317
  91.0 0.8 shard_map.81.coef
  91.8 0.7 collective-permute-done.14.recv
  92.5 1.3 %shard_map.82 = f32[256,128]{1,0:T(8,128)} custom-call(f32[1]{0:T(128)S(6)} %copy.9.steps, f32[24,128]{1,0:T(8,128)S(1)} %shard_map.81.coef, f32[16,128]{1,0:T(8,128)S(1)} %get-tuple-element.24.dots, f32[16,128]{1,0:T(8,128)S(1)} %collective-permute-done.14.recv, f32[256,128]{1,0:T(8,128)S(1)} %get-tuple-element.20.grad, f32[256,128]{1,0:T(8,128)S(1)} %bitcast.9, ...), custom_call_target="tpu_custom_call" | custom-call | tf_op jit(solution)/shard_map/pallas_call | solution.py:445
  (17 shorter events, 0.2 us)
Async XLA Ops:
  0.6 38.8 %copy-start.3 = (s32[1024]{0:T(1024)S(1)}, s32[1024]{0:T(1024)}, u32[]{:S(2)}) copy-start(s32[1024]{0:T(1024)} %param.8) | copy-start | bytes 12292
  1.6 7.7 %collective-permute-start = (bf16[256,128]{1,0:T(8,128)(2,1)S(1)}, bf16[256,128]{1,0:T(8,128)(2,1)S(1)}, u32[]{:S(2)}, u32[]{:S(2)}) collective-permute-start(bf16[256,128]{1,0:T(8,128)(2,1)S(1)} %bitcast_convert_fusion.refs_0_), channel_id=1, source_target_pairs={{0,16},{4,20},{8,24},{12,28},{16,0},{20,4},{24,8},{28,12},{1,17},{... | collective-permute-start | bytes 196616 | tf_op jit(solution)/shard_map/ppermute | solution.py:317
  9.3 9.3 %collective-permute-start.3 = (bf16[512,128]{1,0:T(8,128)(2,1)S(1)}, bf16[512,128]{1,0:T(8,128)(2,1)S(1)}, u32[]{:S(2)}, u32[]{:S(2)}) collective-permute-start(bf16[512,128]{1,0:T(8,128)(2,1)S(1)} %pad_maximum_fusion), channel_id=1, source_target_pairs={{0,12},{4,8},{8,4},{12,0},{16,28},{20,24},{24,20},{28,16},{1,13},{... | collective-permute-start | bytes 393224 | tf_op jit(solution)/shard_map/ppermute | solution.py:317
  10.8 7.8 %collective-permute-start.2 = (bf16[512,128]{1,0:T(8,128)(2,1)S(1)}, bf16[512,128]{1,0:T(8,128)(2,1)S(1)}, u32[]{:S(2)}, u32[]{:S(2)}) collective-permute-start(bf16[512,128]{1,0:T(8,128)(2,1)S(1)} %pad_maximum_fusion), channel_id=1, source_target_pairs={{0,8},{4,12},{8,0},{12,4},{16,24},{20,28},{24,16},{28,20},{1,9},{5... | collective-permute-start | bytes 393224 | tf_op jit(solution)/shard_map/ppermute | solution.py:317
  12.5 6.1 %collective-permute-start.1 = (bf16[512,128]{1,0:T(8,128)(2,1)S(1)}, bf16[512,128]{1,0:T(8,128)(2,1)S(1)}, u32[]{:S(2)}, u32[]{:S(2)}) collective-permute-start(bf16[512,128]{1,0:T(8,128)(2,1)S(1)} %pad_maximum_fusion), channel_id=1, source_target_pairs={{0,4},{4,0},{8,12},{12,8},{16,20},{20,16},{24,28},{28,24},{1,5},{5... | collective-permute-start | bytes 393224 | tf_op jit(solution)/shard_map/ppermute | solution.py:317
  14.4 1.6 %copy-start = (f32[2,8,32768]{2,1,0:T(8,128)S(1)}, f32[2,8,32768]{2,1,0:T(8,128)}, u32[]{:S(2)}) copy-start(f32[2,8,32768]{2,1,0:T(8,128)} %hist.4) | copy-start | bytes 6291460
  34.5 39.6 %copy-start.1 = (f32[2,8,32768]{2,1,0:T(8,128)S(1)}, f32[2,8,32768]{2,1,0:T(8,128)}, u32[]{:S(2)}) copy-start(f32[2,8,32768]{2,1,0:T(8,128)} %hist.4) | copy-start | bytes 6291460
  34.5 39.6 %copy-start.2 = (f32[32768]{0:T(1024)S(1)}, f32[32768]{0:T(1024)}, u32[]{:S(2)}) copy-start(f32[32768]{0:T(1024)} %param.9) | copy-start | bytes 393220
  34.5 1.2 %collective-permute-start.4 = (f32[24,128]{1,0:T(8,128)S(1)}, f32[24,128]{1,0:T(8,128)S(1)}, u32[]{:S(2)}, u32[]{:S(2)}) collective-permute-start(f32[24,128]{1,0:T(8,128)S(1)} %shard_map.78), channel_id=1, source_target_pairs={{0,1},{1,0},{2,3},{3,2},{4,5},{5,4},{6,7},{7,6},{8,9},{9,8},{10,11... | collective-permute-start | bytes 36872 | tf_op jit(solution)/shard_map/ppermute | solution.py:317
  35.8 3.7 %collective-permute-start.5 = (f32[24,128]{1,0:T(8,128)S(1)}, f32[24,128]{1,0:T(8,128)S(1)}, u32[]{:S(2)}, u32[]{:S(2)}) collective-permute-start(f32[24,128]{1,0:T(8,128)S(1)} %add.36), channel_id=1, source_target_pairs={{0,2},{1,3},{2,0},{3,1},{4,6},{5,7},{6,4},{7,5},{8,10},{9,11},{10,... | collective-permute-start | bytes 36872 | tf_op jit(solution)/shard_map/ppermute | solution.py:317
  59.6 6.9 %collective-permute-start.8 = (f16[512,128]{1,0:T(8,128)(2,1)S(1)}, f16[512,128]{1,0:T(8,128)(2,1)S(1)}, u32[]{:S(2)}, u32[]{:S(2)}) collective-permute-start(f16[512,128]{1,0:T(8,128)(2,1)S(1)} %convert_element_type.34), channel_id=1, source_target_pairs={{0,12},{4,8},{8,4},{12,0},{16,28},{20,24},{24,20},{28,16},{1,13},{... | collective-permute-start | bytes 393224 | tf_op jit(solution)/shard_map/ppermute | solution.py:317
  61.2 6.9 %collective-permute-start.7 = (f16[512,128]{1,0:T(8,128)(2,1)S(1)}, f16[512,128]{1,0:T(8,128)(2,1)S(1)}, u32[]{:S(2)}, u32[]{:S(2)}) collective-permute-start(f16[512,128]{1,0:T(8,128)(2,1)S(1)} %convert_element_type.32), channel_id=1, source_target_pairs={{0,8},{4,12},{8,0},{12,4},{16,24},{20,28},{24,16},{28,20},{1,9},{5... | collective-permute-start | bytes 393224 | tf_op jit(solution)/shard_map/ppermute | solution.py:317
  62.8 5.3 %collective-permute-start.6 = (f16[512,128]{1,0:T(8,128)(2,1)S(1)}, f16[512,128]{1,0:T(8,128)(2,1)S(1)}, u32[]{:S(2)}, u32[]{:S(2)}) collective-permute-start(f16[512,128]{1,0:T(8,128)(2,1)S(1)} %convert_element_type.30), channel_id=1, source_target_pairs={{0,4},{4,0},{8,12},{12,8},{16,20},{20,16},{24,28},{28,24},{1,5},{5... | collective-permute-start | bytes 393224 | tf_op jit(solution)/shard_map/ppermute | solution.py:317
  68.2 5.9 %collective-permute-start.9 = (f16[256,128]{1,0:T(8,128)(2,1)S(1)}, f16[256,128]{1,0:T(8,128)(2,1)S(1)}, u32[]{:S(2)}, u32[]{:S(2)}) collective-permute-start(f16[256,128]{1,0:T(8,128)(2,1)S(1)} %get-tuple-element.22), channel_id=1, source_target_pairs={{0,16},{4,20},{8,24},{12,28},{16,0},{20,4},{24,8},{28,12},{1,17},{... | collective-permute-start | bytes 196616 | tf_op jit(solution)/shard_map/ppermute | solution.py:317
  75.3 3.7 %collective-permute-start.10 = (f32[32,128]{1,0:T(8,128)S(1)}, f32[32,128]{1,0:T(8,128)S(1)}, u32[]{:S(2)}, u32[]{:S(2)}) collective-permute-start(f32[32,128]{1,0:T(8,128)S(1)} %get-tuple-element.19), channel_id=1, source_target_pairs={{0,4},{4,0},{8,12},{12,8},{16,20},{20,16},{24,28},{28,24},{1,5},{5... | collective-permute-start | bytes 49160 | tf_op jit(solution)/shard_map/ppermute | solution.py:317
  79.1 3.7 %collective-permute-start.11 = (f32[32,128]{1,0:T(8,128)S(1)}, f32[32,128]{1,0:T(8,128)S(1)}, u32[]{:S(2)}, u32[]{:S(2)}) collective-permute-start(f32[32,128]{1,0:T(8,128)S(1)} %add.42), channel_id=1, source_target_pairs={{0,8},{4,12},{8,0},{12,4},{16,24},{20,28},{24,16},{28,20},{1,9},{5... | collective-permute-start | bytes 49160 | tf_op jit(solution)/shard_map/ppermute | solution.py:317
  82.8 4.8 %collective-permute-start.12 = (f32[32,128]{1,0:T(8,128)S(1)}, f32[32,128]{1,0:T(8,128)S(1)}, u32[]{:S(2)}, u32[]{:S(2)}) collective-permute-start(f32[32,128]{1,0:T(8,128)S(1)} %add.43), channel_id=1, source_target_pairs={{0,16},{4,20},{8,24},{12,28},{16,0},{20,4},{24,8},{28,12},{1,17},{... | collective-permute-start | bytes 49160 | tf_op jit(solution)/shard_map/ppermute | solution.py:317
  87.6 1.2 %collective-permute-start.13 = (f32[16,128]{1,0:T(8,128)S(1)}, f32[16,128]{1,0:T(8,128)S(1)}, u32[]{:S(2)}, u32[]{:S(2)}) collective-permute-start(f32[16,128]{1,0:T(8,128)S(1)} %slice.30), channel_id=1, source_target_pairs={{0,1},{1,0},{2,3},{3,2},{4,5},{5,4},{6,7},{7,6},{8,9},{9,8},{10,11... | collective-permute-start | bytes 24584 | tf_op jit(solution)/shard_map/ppermute | solution.py:317
  88.8 3.7 %collective-permute-start.14 = (f32[16,128]{1,0:T(8,128)S(1)}, f32[16,128]{1,0:T(8,128)S(1)}, u32[]{:S(2)}, u32[]{:S(2)}) collective-permute-start(f32[16,128]{1,0:T(8,128)S(1)} %get-tuple-element.24.dots), channel_id=1, source_target_pairs={{0,2},{1,3},{2,0},{3,1},{4,6},{5,7},{6,4},{7,5},{8,10},{9,11},{10,... | collective-permute-start | bytes 24584 | tf_op jit(solution)/shard_map/ppermute | solution.py:317
